TPU v7x, 128 devices: a whole 4x4x4 slice. The times are simulated.
128 devices in a mesh: grp: 8 (over z, core), loc: 16 (over x, y).
Axes of the slice: x: 4, y: 4, z: 4, core: 2. Of those that a mesh axis runs over, the one named last changes fastest.
Arguments:
- tokens: bfloat16 [16384, 2048], P(('grp', 'loc')), may hold values from -6 to 6
- expert_ids: int32 [16384, 6], P(('grp', 'loc')), may hold values from 0 to 63, as said below
- gate_weights: bfloat16 [16384, 6], P(('grp', 'loc')), may hold values from 0.099609375 to 1
- w_gate: bfloat16 [128, 2048, 704], P(('grp', 'loc')), may hold values from -0.125 to 0.125
- w_up: bfloat16 [128, 2048, 704], P(('grp', 'loc')), may hold values from -0.125 to 0.125
- w_down: bfloat16 [128, 704, 2048], P(('grp', 'loc')), may hold values from -0.15625 to 0.15625
Outputs:
- moe_out: bfloat16 [16384, 2048], P(('grp', 'loc'))
Inputs may be any that keep to these rules, and one draw needn't show every extreme that they name: `expert_ids`: each row names 6 different experts in increasing order; they lie in exactly 4 of the 8 groups, expert e belonging to group e // 8.
All inputs are finite; a program needn't handle non-finite values.
Results may differ from a plain program's by a relative error of at most 0.008.
Values may be sent and summed in bfloat16 or wider, within the bound.
No kernel may reach another device: no remote copies, remote signals or barrier semaphores. Data moves between devices by JAX's collectives and lax.ppermute only.
A program may use at most 128 MiB of HBM per device.

v0:
```python
import jax
import jax.numpy as jnp
from jax import lax
from jax.sharding import PartitionSpec as P


def silu_ffn(row_block, w_gate, w_up, w_down):
    row_shape = row_block.shape
    flat_rows = row_block.reshape(-1, row_shape[-1])
    gate_proj = jnp.dot(flat_rows, w_gate[0], preferred_element_type=jnp.float32)
    up_proj = jnp.dot(flat_rows, w_up[0], preferred_element_type=jnp.float32)
    hidden = (jax.nn.silu(gate_proj) * up_proj).astype(jnp.bfloat16)
    return (
        jnp.dot(hidden, w_down[0], preferred_element_type=jnp.float32)
        .astype(jnp.bfloat16)
        .reshape(row_shape)
    )


def with_zero_row(table):
    return jnp.concatenate([table, jnp.zeros((1, table.shape[1]), table.dtype)], axis=0)


def per_device(tokens, expert_ids, gate_weights, w_gate, w_up, w_down):
    groups = lax.axis_size("grp")
    loc_count = lax.axis_size("loc")
    experts = groups * loc_count // 2
    per_group = loc_count // 2
    tok_count, top_count = expert_ids.shape
    model_width = tokens.shape[1]
    capacity = 3 * tok_count * top_count // (2 * experts)
    flat_ids = expert_ids.reshape(-1)
    onehot = (flat_ids[:, None] == jnp.arange(experts, dtype=jnp.int32)[None, :]).astype(jnp.int32)
    slot_of = jnp.sum((jnp.cumsum(onehot, axis=0) - onehot) * onehot, axis=1).reshape(
        tok_count, top_count
    )
    is_kept = slot_of < capacity
    home_group = expert_ids // per_group
    token_index = jnp.arange(tok_count, dtype=jnp.int32)
    group_range = jnp.arange(groups, dtype=jnp.int32)
    padded = with_zero_row(tokens)
    place_at = jnp.where(is_kept, expert_ids * capacity + slot_of, experts * capacity)
    source_of = (
        jnp.full((experts * capacity + 1,), tok_count, jnp.int32)
        .at[place_at.reshape(-1)]
        .set(jnp.repeat(token_index, top_count))[:-1]
    )
    outgoing = padded[source_of].reshape(experts, 1, capacity, model_width)
    outgoing = jnp.broadcast_to(outgoing, (experts, 2, capacity, model_width)).reshape(
        2 * experts, capacity, model_width
    )
    returned = lax.all_to_all(
        silu_ffn(
            lax.all_to_all(outgoing, ("grp", "loc"), split_axis=0, concat_axis=0, tiled=True),
            w_gate,
            w_up,
            w_down,
        ),
        ("grp", "loc"),
        split_axis=0,
        concat_axis=0,
        tiled=True,
    )
    halves = returned.reshape(experts, 2, capacity, model_width)
    first_half = with_zero_row(halves[:, 0].reshape(-1, model_width))[place_at]
    second_half = with_zero_row(halves[:, 1].reshape(-1, model_width))[place_at]
    weights = jnp.where(is_kept, gate_weights.astype(jnp.float32), jnp.float32(0.0))
    combined = weights[:, :, None] * (
        first_half.astype(jnp.float32) + second_half.astype(jnp.float32)
    )
    group_mask = (home_group[:, :, None] == group_range[None, None, :]).astype(jnp.float32)
    group_sum = jnp.einsum("tkg,tkd->tgd", group_mask, combined)
    group_part = lax.optimization_barrier(group_sum.astype(jnp.bfloat16))
    return jnp.sum(group_part.astype(jnp.float32), axis=1).astype(jnp.bfloat16)


def solution(mesh):
    in_specs = (
        P(("grp", "loc"), None),
        P(("grp", "loc"), None),
        P(("grp", "loc"), None),
        P(("grp", "loc"), None, None),
        P(("grp", "loc"), None, None),
        P(("grp", "loc"), None, None),
    )
    out_specs = P(("grp", "loc"), None)
    return jax.shard_map(
        per_device, mesh=mesh, in_specs=in_specs, out_specs=out_specs, check_vma=False
    )
```

profile of v0, /device:TPU:37, one launch (start us, length us, event | category | flops | bytes accessed | tf_op | source)
XLA Modules:
  0.0 507.6 jit_solution(15876827924128513851)
XLA Ops:
  0.0 0.0 copy-start
  0.0 0.8 broadcast_multiply_fusion
  0.8 0.8 copy.11
  1.7 0.1 eq.45
  1.8 0.1 eq.41
  2.0 0.1 copy.20
  2.1 0.1 reshape.106
  2.2 1.8 reduce-window.6
  4.0 0.3 slice_reduce_fusion
  4.3 0.1 fusion.15
  4.5 0.1 reshape.71
  4.6 0.0 copy-start.2
  4.6 0.7 compare_select_fusion
  5.3 0.1 reshape.72
  5.4 3.4 scatter_custom_fusion
  8.9 0.0 copy-done.2
  8.9 1.1 concatenate.9
  10.0 6.1 %gather_fusion = bf16[1152,2048]{1,0:T(8,128)(2,1)} fusion(bf16[129,2048]{1,0:T(8,128)(2,1)S(1)} %concatenate.9, s32[2048]{0:T(1024)S(1)} %pad_clamp_fusion), kind=kCustom, calls=%fused_computation | custom fusion | bytes 9441792 | tf_op jit(solution)/shard_map/gather | solution.py:48
  16.0 7.6 %broadcast_in_dim.38 = bf16[64,18,2048]{2,1,0:T(8,128)(2,1)} reshape(bf16[1152,2048]{1,0:T(8,128)(2,1)} %gather_fusion) | data formatting | bytes 9437184 | tf_op jit(solution)/shard_map/broadcast_in_dim | solution.py:49
  23.6 5.2 %broadcast_in_dim.39 = bf16[64,2,18,2048]{3,2,1,0:T(8,128)(2,1)S(1)} broadcast(bf16[64,18,2048]{2,1,0:T(8,128)(2,1)} %broadcast_in_dim.38), dimensions={0,2,3} | broadcast | bytes 14155776 | tf_op jit(solution)/shard_map/broadcast_in_dim | solution.py:49
  28.8 149.4 %all_to_all.10 = bf16[128,18,2048]{2,1,0:T(8,128)(2,1)} all-to-all(bf16[128,18,2048]{2,1,0:T(8,128)(2,1)S(1)} %bitcast.43), channel_id=1, replica_groups=mesh['grp'=8,'loc'=16] {'grp','loc'}, dimensions={0} | all-to-all | bytes 18874368 | tf_op jit(solution)/shard_map/all_to_all | solution.py:54
  178.3 14.1 %reshape.75 = bf16[2304,2048]{1,0:T(8,128)(2,1)} reshape(bf16[128,18,2048]{2,1,0:T(8,128)(2,1)} %all_to_all.10) | data formatting | bytes 18874368 | tf_op jit(solution)/shard_map/reshape | solution.py:9
  192.3 13.0 %fusion.10 = f32[2304,704]{0,1:T(8,128)} fusion(bf16[2304,2048]{1,0:T(8,128)(2,1)} %reshape.75, bf16[1,2048,704]{1,2,0:T(8,128)(2,1)} %param.9), kind=kOutput, calls=%fused_computation.16 | convolution fusion | flops 6643777536 | bytes 18808832 | tf_op jit(solution)/shard_map/dot_general | solution.py:10
  205.3 0.0 copy-done
  205.3 24.7 %convolution_convert_fusion = bf16[2304,2048]{1,0:T(8,128)(2,1)} fusion(f32[2304,704]{0,1:T(8,128)} %fusion.10, bf16[2304,2048]{1,0:T(8,128)(2,1)} %reshape.75, bf16[1,704,2048]{2,1,0:T(8,128)(2,1)S(1)} %copy-done, bf16[1,2048,704]{1,2,0:T(8,128)(2,1)} %param.10), kind=kOutput, calls=%fused_computation.4 | convolution fusion | flops 13302005760 | bytes 31129600 | tf_op jit(solution)/shard_map/dot_general | solution.py:14
  230.0 13.8 %reshape.76 = bf16[128,18,2048]{2,1,0:T(8,128)(2,1)} reshape(bf16[2304,2048]{1,0:T(8,128)(2,1)} %convolution_convert_fusion) | data formatting | bytes 18874368 | tf_op jit(solution)/shard_map/reshape | solution.py:16
  243.8 0.0 copy-start.5
  243.8 0.0 copy-start.4
  243.8 0.0 copy-start.3
  243.8 8.6 %all-to-all-start.1 = ((bf16[128,18,2048]{2,1,0:T(8,128)(2,1)}), bf16[128,18,2048]{2,1,0:T(8,128)(2,1)}, u32[]{:S(2)}, u32[]{:S(2)}) async-start(bf16[128,18,2048]{2,1,0:T(8,128)(2,1)} %reshape.76), calls=%async_computation.1 | async-start | bytes 25165824 | tf_op jit(solution)/shard_map/all_to_all | solution.py:52
  252.5 0.0 copy-done.5
  252.5 0.1 copy.18
  252.6 0.0 copy-done.4
  252.6 0.1 reshape.88
  252.8 0.0 copy-done.3
  252.8 170.6 %all-to-all-done.1 = bf16[128,18,2048]{2,1,0:T(8,128)(2,1)} async-done(((bf16[128,18,2048]{2,1,0:T(8,128)(2,1)}), bf16[128,18,2048]{2,1,0:T(8,128)(2,1)}, u32[]{:S(2)}, u32[]{:S(2)}) %all-to-all-start.1) | async-done | bytes 9437216 | tf_op jit(solution)/shard_map/all_to_all | solution.py:52
  423.5 10.7 %slice_bitcast_fusion.1 = (bf16[64,1,18,2048]{3,2,0,1:T(8,128)(2,1)}, bf16[64,1,18,2048]{3,2,0,1:T(8,128)(2,1)}) fusion(bf16[64,2,18,2048]{3,2,1,0:T(8,128)(2,1)} %bitcast.5), kind=kLoop, calls=%fused_computation.9 | loop fusion | bytes 18874368
  434.1 7.7 %reshape_squeeze.6 = bf16[1152,2048]{1,0:T(8,128)(2,1)} reshape(bf16[64,1,18,2048]{3,2,0,1:T(8,128)(2,1)} %get-tuple-element.7) | data formatting | bytes 9437184 | tf_op jit(solution)/shard_map/reshape;squeeze | solution.py:65
  441.9 5.2 %concatenate.10 = bf16[1153,2048]{1,0:T(8,128)(2,1)} pad(bf16[1152,2048]{1,0:T(8,128)(2,1)} %reshape_squeeze.6, bf16[]{:T(256)} %constant.37.clone.1), padding=0_1x0_0 | pad | bytes 9441282 | tf_op jit(solution)/shard_map/concatenate | solution.py:21
  447.1 7.7 %reshape_squeeze.7 = bf16[1152,2048]{1,0:T(8,128)(2,1)} reshape(bf16[64,1,18,2048]{3,2,0,1:T(8,128)(2,1)} %get-tuple-element.8) | data formatting | bytes 9437184 | tf_op jit(solution)/shard_map/reshape;squeeze | solution.py:66
  454.8 5.2 %concatenate.11 = bf16[1153,2048]{1,0:T(8,128)(2,1)} pad(bf16[1152,2048]{1,0:T(8,128)(2,1)} %reshape_squeeze.7, bf16[]{:T(256)} %constant.37.clone.1), padding=0_1x0_0 | pad | bytes 9441282 | tf_op jit(solution)/shard_map/concatenate | solution.py:21
  460.0 10.1 %gather_fusion.1 = bf16[768,2048]{1,0:T(8,128)(2,1)} fusion(bf16[1153,2048]{1,0:T(8,128)(2,1)} %concatenate.10, s32[1024]{0:T(1024)S(1)} %pad_clamp_fusion.1), kind=kCustom, calls=%fused_computation.1 | custom fusion | bytes 6294528 | tf_op jit(solution)/shard_map/gather | solution.py:65
  470.1 10.1 %gather_fusion.2 = bf16[768,2048]{1,0:T(8,128)(2,1)} fusion(bf16[1153,2048]{1,0:T(8,128)(2,1)} %concatenate.11, s32[1024]{0:T(1024)S(1)} %pad_clamp_fusion.1), kind=kCustom, calls=%fused_computation.2 | custom fusion | bytes 6294528 | tf_op jit(solution)/shard_map/gather | solution.py:66
  480.1 6.9 %convert_add_fusion = f32[768,2048]{1,0:T(8,128)} fusion(bf16[768,2048]{1,0:T(8,128)(2,1)} %gather_fusion.2, bf16[768,2048]{1,0:T(8,128)(2,1)} %gather_fusion.1), kind=kLoop, calls=%fused_computation.10 | loop fusion | flops 4718592 | bytes 12582912 | tf_op jit(solution)/shard_map/add | solution.py:69
  487.0 0.0 copy-start.1
  487.0 8.0 %reshape.117 = f32[128,6,2048]{2,1,0:T(8,128)} reshape(f32[768,2048]{1,0:T(8,128)} %convert_add_fusion) | data formatting | bytes 12582912 | tf_op jit(solution)/shard_map/add | solution.py:69
  495.0 6.7 %fusion.3 = bf16[128,8,2048]{2,1,0:T(8,128)(2,1)} fusion(f32[128,6,2048]{2,1,0:T(8,128)} %reshape.117, f32[128,6]{1,0:T(8,128)S(1)} %broadcast_select_fusion, s32[128,6]{1,0:T(8,128)S(1)} %add_select_fusion), kind=kOutput, calls=%fused_computation.12 | convolution fusion | flops 28841984 | bytes 10491904 | tf_op jit(solution)/shard_map/tkg,tkd->tgd/dot_general | solution.py:72
  501.7 5.9 %reduce_sum.22 = bf16[128,2048]{1,0:T(8,128)(2,1)} reduce(bf16[128,8,2048]{2,1,0:T(8,128)(2,1)} %fusion.3, bf16[]{:T(256)} %constant.37.clone.1), dimensions={1}, to_apply=%region_4.5 | reduce | flops 1835008 | bytes 4718594 | tf_op jit(solution)/shard_map/reduce_sum | solution.py:74
  507.6 0.0 copy-done.1
  (9 shorter events, 0.1 us)
Async XLA Ops:
  0.0 205.3 %copy-start = (bf16[1,704,2048]{2,1,0:T(8,128)(2,1)S(1)}, bf16[1,704,2048]{2,1,0:T(8,128)(2,1)}, u32[]{:S(2)}) copy-start(bf16[1,704,2048]{2,1,0:T(8,128)(2,1)} %param.11) | copy-start | bytes 8650756
  4.6 4.2 copy-start.2
  243.8 8.6 %copy-start.5 = (bf16[128,6]{0,1:T(8,128)(2,1)S(1)}, bf16[128,6]{0,1:T(8,128)(2,1)}, u32[]{:S(2)}) copy-start(bf16[128,6]{0,1:T(8,128)(2,1)} %param.8) | copy-start | bytes 4612
  243.8 8.8 %copy-start.4 = (s32[128,6]{1,0:T(8,128)S(1)}, s32[128,6]{1,0:T(8,128)}, u32[]{:S(2)}) copy-start(s32[128,6]{1,0:T(8,128)} %get-tuple-element.5) | copy-start | bytes 9220
  243.8 9.0 %copy-start.3 = (s32[128,6]{1,0:T(8,128)S(1)}, s32[128,6]{1,0:T(8,128)}, u32[]{:S(2)}) copy-start(s32[128,6]{1,0:T(8,128)} %copy-done.2) | copy-start | bytes 9220
  243.8 179.6 %all-to-all-start.1 = ((bf16[128,18,2048]{2,1,0:T(8,128)(2,1)}), bf16[128,18,2048]{2,1,0:T(8,128)(2,1)}, u32[]{:S(2)}, u32[]{:S(2)}) async-start(bf16[128,18,2048]{2,1,0:T(8,128)(2,1)} %reshape.76), calls=%async_computation.1 | async-start | bytes 25165824 | tf_op jit(solution)/shard_map/all_to_all | solution.py:52
  487.0 20.6 %copy-start.1 = (bf16[1,704,2048]{2,1,0:T(8,128)(2,1)S(1)}, bf16[1,704,2048]{2,1,0:T(8,128)(2,1)}, u32[]{:S(2)}) copy-start(bf16[1,704,2048]{2,1,0:T(8,128)(2,1)} %param.11) | copy-start | bytes 8650756
where the time goes:
time: 509 us; the launch traced here: 508 us
  waiting for transfers between devices  171 us (34%)
  blocking collectives  149 us (29%)
  local copies, waits for them, and re-layouts  118 us (23%)
  matrix products  44.4 us (9%)
  other arithmetic  16.3 us (3%)
  starting transfers between devices  8.63 us (2%)
    all_to_all x1, waiting for transfers between devices, per_device(): lax.all_to_all(silu_ffn(lax.all_to_all(outgoing, ('grp', 'loc'), split_ax...  171 us
    all_to_all x1, blocking collectives, per_device(): lax.all_to_all(outgoing, ('grp', 'loc'), split_axis=0, concat_axis=0, til...  149 us
    dot_general x1, matrix products, silu_ffn(): jnp.dot(hidden, w_down[0], preferred_element_type=jnp.float32)  24.7 us
    reshape x1, local copies, waits for them, and re-layouts, silu_ffn(): flat_rows = row_block.reshape(-1, row_shape[-1])  14.1 us
    reshape x1, local copies, waits for them, and re-layouts, silu_ffn(): return jnp.dot(hidden, w_down[0], preferred_element_type=jnp.float32).ast...  13.8 us
    dot_general x1, matrix products, silu_ffn(): jnp.dot(flat_rows, w_gate[0], preferred_element_type=jnp.float32)  13 us
    broadcast_in_dim x2, local copies, waits for them, and re-layouts, per_device(): jnp.broadcast_to(outgoing, (experts, 2, capacity, model_width))  12.8 us
    unnamed x14, local copies, waits for them, and re-layouts  11.5 us
  transfers between devices with their start and end apart: 1, of which 1 were waited for; matrix products, arithmetic and copies ran while one was open for 0% of the time, Pallas kernels for 0%

commit v1 on v0

v1 whole, which is shorter than its diff:
```python
import functools

import jax
import jax.numpy as jnp
from jax import lax
from jax.experimental import pallas as pl
from jax.experimental.pallas import tpu as pltpu
from jax.sharding import PartitionSpec as P

AXES = ("grp", "loc")
CAP = 18
MAIN = 16
PIECES = 8
TILE = MAIN * PIECES


def split_matrix():
    row = lax.broadcasted_iota(jnp.int32, (TILE, TILE), 0)
    col = lax.broadcasted_iota(jnp.int32, (TILE, TILE), 1)
    source = (row % MAIN) // 2 * MAIN + (row % 2) * PIECES + row // MAIN
    return (source == col).astype(jnp.bfloat16)


def exact_dot(a, b, dims=((1,), (0,))):
    return lax.dot_general(a, b, (dims, ((), ())), preferred_element_type=jnp.float32)


def pieces_to_rows(tile, matrix):
    stacked = exact_dot(matrix, tile).astype(jnp.bfloat16)
    return jnp.concatenate(
        [stacked[MAIN * q : MAIN * (q + 1)] for q in range(PIECES)], axis=1
    )


def rows_to_pieces(rows, matrix):
    width = rows.shape[1] // PIECES
    stacked = jnp.concatenate(
        [rows[:, width * q : width * (q + 1)] for q in range(PIECES)], axis=0
    )
    return exact_dot(matrix, stacked, ((0,), (0,))).astype(jnp.bfloat16)


def slots_of(ids_t, experts, gates_t=None):
    top, count = ids_t.shape
    expert = lax.broadcasted_iota(jnp.int32, (experts, count), 0)
    used = jnp.zeros((experts, count), jnp.float32)
    weight = jnp.zeros((experts, count), jnp.float32)
    for k in range(top):
        hit = expert == ids_t[k : k + 1, :]
        used = jnp.where(hit, 1.0, used)
        if gates_t is not None:
            weight = jnp.where(hit, gates_t[k : k + 1, :], weight)
    earlier = lax.broadcasted_iota(jnp.int32, (count, count), 0)
    later = lax.broadcasted_iota(jnp.int32, (count, count), 1)
    before = exact_dot(used.astype(jnp.bfloat16), (earlier < later).astype(jnp.bfloat16))
    return jnp.where(used > 0.0, before, -1.0), weight


def dispatch_kernel(ids_ref, tokens_ref, out_ref, slot_ref):
    block, _, _, width = out_ref.shape
    count, model = tokens_ref.shape
    step = pl.program_id(0)

    @pl.when(step == 0)
    def _():
        slot_ref[...] = slots_of(ids_ref[...], slot_ref.shape[0])[0]

    slot = slot_ref[pl.ds(pl.multiple_of(step * block, block), block), :]
    main_id = lax.broadcasted_iota(jnp.int32, (block, MAIN, count), 1).astype(jnp.float32)
    pick = (slot[:, None, :] == main_id).astype(jnp.float32).reshape(block * MAIN, count)
    rows = exact_dot(pick.astype(jnp.bfloat16), tokens_ref[...]).astype(jnp.bfloat16)
    rows = rows.reshape(block, MAIN, model)
    row = lax.broadcasted_iota(jnp.int32, (2 * block, count), 0)
    slot_twice = jnp.broadcast_to(slot[:, None, :], (block, 2, count)).reshape(2 * block, count)
    pick_last = (slot_twice == (MAIN + row % 2).astype(jnp.float32)).astype(jnp.bfloat16)
    last = exact_dot(pick_last, tokens_ref[...]).astype(jnp.bfloat16)
    pieces = rows_to_pieces(last, split_matrix()).reshape(block, MAIN, width - model)
    for half in range(2):
        out_ref[:, half, :, :model] = rows
        out_ref[:, half, :, model:] = pieces


def dispatch(ids_t, tokens, experts):
    count, model = tokens.shape
    width = model * CAP // MAIN
    block = 8
    return pl.pallas_call(
        dispatch_kernel,
        grid=(experts // block,),
        in_specs=[
            pl.BlockSpec(ids_t.shape, lambda i: (0, 0)),
            pl.BlockSpec(tokens.shape, lambda i: (0, 0)),
        ],
        out_specs=pl.BlockSpec((block, 2, MAIN, width), lambda i: (i, 0, 0, 0)),
        out_shape=jax.ShapeDtypeStruct((experts, 2, MAIN, width), jnp.bfloat16),
        scratch_shapes=[pltpu.VMEM((experts, count), jnp.float32)],
        cost_estimate=pl.CostEstimate(
            flops=4 * experts * CAP * count * model, bytes_accessed=4 * experts * MAIN * width,
            transcendentals=0,
        ),
        name="dispatch_rows",
    )(ids_t, tokens)


def ffn_kernel(x_ref, gate_ref, up_ref, down_ref, out_ref, rows_ref):
    block, _, width = x_ref.shape
    model = gate_ref.shape[1]
    main = block * MAIN
    matrix = split_matrix()
    rows_ref[:main, :] = x_ref[:, :, :model].reshape(main, model)
    pieces = x_ref[:, :, model:].reshape(main, width - model)
    for tile in range(main // TILE):
        rows_ref[main + MAIN * tile : main + MAIN * (tile + 1), :] = pieces_to_rows(
            pieces[TILE * tile : TILE * (tile + 1)], matrix
        )
    rows = rows_ref[...]
    gate = exact_dot(rows, gate_ref[0])
    up = exact_dot(rows, up_ref[0])
    hidden = (gate / (1.0 + jnp.exp(-gate)) * up).astype(jnp.bfloat16)
    half_out = exact_dot(hidden, down_ref[0]).astype(jnp.bfloat16)
    out_ref[:, :, :model] = half_out[:main].reshape(block, MAIN, model)
    for tile in range(main // TILE):
        piece = rows_to_pieces(half_out[main + MAIN * tile : main + MAIN * (tile + 1)], matrix)
        chunks = TILE // MAIN
        out_ref[chunks * tile : chunks * (tile + 1), :, model:] = piece.reshape(
            chunks, MAIN, width - model
        )


def half_ffn(chunks, w_gate, w_up, w_down):
    sources, _, width = chunks.shape
    model, hidden = w_gate.shape[1:]
    block = 32
    whole = lambda i: (0, 0, 0)
    return pl.pallas_call(
        ffn_kernel,
        grid=(sources // block,),
        in_specs=[
            pl.BlockSpec((block, MAIN, width), lambda i: (i, 0, 0)),
            pl.BlockSpec(w_gate.shape, whole, pipeline_mode=pl.Buffered(1)),
            pl.BlockSpec(w_up.shape, whole, pipeline_mode=pl.Buffered(1)),
            pl.BlockSpec(w_down.shape, whole, pipeline_mode=pl.Buffered(1)),
        ],
        out_specs=pl.BlockSpec((block, MAIN, width), lambda i: (i, 0, 0)),
        out_shape=jax.ShapeDtypeStruct(chunks.shape, jnp.bfloat16),
        scratch_shapes=[pltpu.VMEM((block * CAP, model), jnp.bfloat16)],
        cost_estimate=pl.CostEstimate(
            flops=6 * sources * CAP * model * hidden,
            bytes_accessed=4 * sources * CAP * model + 6 * model * hidden,
            transcendentals=sources * CAP * hidden,
        ),
        compiler_params=pltpu.CompilerParams(vmem_limit_bytes=56 * 1024 * 1024),
        name="half_ffn",
    )(chunks, w_gate, w_up, w_down)


def combine_kernel(ids_ref, gates_ref, rows_ref, out_ref, slot_ref, weight_ref, acc_ref):
    block, _, _, width = rows_ref.shape
    count, model = out_ref.shape
    step = pl.program_id(0)

    @pl.when(step == 0)
    def _():
        slot, weight = slots_of(ids_ref[...], slot_ref.shape[0], gates_ref[...])
        slot_ref[...] = slot
        weight_ref[...] = weight
        acc_ref[...] = jnp.zeros_like(acc_ref)

    here = pl.ds(pl.multiple_of(step * block, block), block)
    slot = slot_ref[here, :]
    weight = weight_ref[here, :]

    def spread(first, slots):
        shape = (block, 2 * slots, count)
        slot_id = first + lax.broadcasted_iota(jnp.int32, shape, 1) % slots
        hit = slot[:, None, :] == slot_id.astype(jnp.float32)
        scaled = jnp.where(hit, jnp.broadcast_to(weight[:, None, :], shape), 0.0)
        return scaled.reshape(block * 2 * slots, count).astype(jnp.bfloat16)

    rows = rows_ref[:, :, :, :model].reshape(block * 2 * MAIN, model)
    total = exact_dot(spread(0, MAIN), rows, ((0,), (0,)))
    matrix = split_matrix()
    pieces = rows_ref[:, :, :, model:].reshape(block * 2 * MAIN, width - model)
    last = jnp.concatenate(
        [
            pieces_to_rows(pieces[TILE * tile : TILE * (tile + 1)], matrix)
            for tile in range(block * 2 * MAIN // TILE)
        ],
        axis=0,
    )
    total += exact_dot(spread(MAIN, CAP - MAIN), last, ((0,), (0,)))
    acc_ref[...] += total

    @pl.when(step == pl.num_programs(0) - 1)
    def _():
        out_ref[...] = acc_ref[...].astype(jnp.bfloat16)


def combine(ids_t, gates_t, returned):
    experts, _, _, width = returned.shape
    count = ids_t.shape[1]
    model = width * MAIN // CAP
    block = 8
    return pl.pallas_call(
        combine_kernel,
        grid=(experts // block,),
        in_specs=[
            pl.BlockSpec(ids_t.shape, lambda i: (0, 0)),
            pl.BlockSpec(gates_t.shape, lambda i: (0, 0)),
            pl.BlockSpec((block, 2, MAIN, width), lambda i: (i, 0, 0, 0)),
        ],
        out_specs=pl.BlockSpec((count, model), lambda i: (0, 0)),
        out_shape=jax.ShapeDtypeStruct((count, model), jnp.bfloat16),
        scratch_shapes=[
            pltpu.VMEM((experts, count), jnp.float32),
            pltpu.VMEM((experts, count), jnp.float32),
            pltpu.VMEM((count, model), jnp.float32),
        ],
        cost_estimate=pl.CostEstimate(
            flops=4 * experts * CAP * count * model, bytes_accessed=4 * experts * CAP * model,
            transcendentals=0,
        ),
        name="combine_rows",
    )(ids_t, gates_t, returned)


def per_device(tokens, expert_ids, gate_weights, w_gate, w_up, w_down):
    devices = lax.axis_size("grp") * lax.axis_size("loc")
    experts = devices // 2
    ids_t = expert_ids.T
    gates_t = gate_weights.astype(jnp.float32).T
    exchange = functools.partial(
        lax.all_to_all, axis_name=AXES, split_axis=0, concat_axis=0, tiled=True
    )
    outgoing = dispatch(ids_t, tokens, experts)
    arrived = exchange(outgoing.reshape((devices,) + outgoing.shape[2:]))
    returned = exchange(half_ffn(arrived, w_gate, w_up, w_down))
    return combine(ids_t, gates_t, returned.reshape(outgoing.shape))


def solution(mesh):
    rows = P(AXES, None)
    weights = P(AXES, None, None)
    return jax.shard_map(
        per_device,
        mesh=mesh,
        in_specs=(rows, rows, rows, weights, weights, weights),
        out_specs=rows,
        check_vma=False,
    )
```

time: 509 us -> 302 us (0.59)
  blocking collectives: 149 us -> 0 us
  local copies, waits for them, and re-layouts: 118 us -> 7.47 us
  waiting for transfers between devices: 171 us -> 222 us
  Pallas kernels: 0 us -> 46.7 us
  matrix products: 44.4 us -> 0 us
  other arithmetic: 16.3 us -> 0.59 us
  starting transfers between devices: 8.63 us -> 23.2 us
    all_to_all x1 -> x0, blocking collectives: 149 us -> none  [per_device(): lax.all_to_all(outgoing, ('grp', 'loc'), split_axis=0, concat_axis=0, til...]
    all_to_all x1 -> x2, waiting for transfers between devices: 171 us -> 222 us  [the longest x1 114 us: per_device(): returned = exchange(half_ffn(arrived, w_gate, w_up, w_down))]
    pallas_call x0 -> x3, Pallas kernels: none -> 46.7 us  [the longest x1 29.6 us: half_ffn(): pl.pallas_call(ffn_kernel, grid=(sources // block,), in_specs=[pl.BlockSp...]
    dot_general x3 -> x0, matrix products: 44.4 us -> none  [the longest x1 24.7 us: silu_ffn(): jnp.dot(hidden, w_down[0], preferred_element_type=jnp.float32)]
    reshape x5 -> x0, local copies, waits for them, and re-layouts: 28.3 us -> none  [the longest x1 14.1 us: silu_ffn(): flat_rows = row_block.reshape(-1, row_shape[-1])]
    gather x3 -> x0, local copies, waits for them, and re-layouts: 26.2 us -> none  [the longest x1 10.1 us: per_device(): first_half = with_zero_row(halves[:, 0].reshape(-1, model_width))[place_at]]
    another operation x2 -> x0, local copies, waits for them, and re-layouts: 15.4 us -> none  [the longest x1 7.73 us: per_device(): first_half = with_zero_row(halves[:, 0].reshape(-1, model_width))[place_at]]
    all_to_all x1 -> x2, starting transfers between devices: 8.63 us -> 23.2 us  [the longest x1 12.4 us: per_device(): returned = exchange(half_ffn(arrived, w_gate, w_up, w_down))]
  transfers between devices with their start and end apart: 1 -> 2, of which waited for: 1 -> 2; matrix products, arithmetic and copies ran while one was open for 0% -> 3% of each run, Pallas kernels for 0% -> 0%
where the time goes in v1:
time: 302 us; the launch traced here: 300 us
  waiting for transfers between devices  222 us (74%)
  Pallas kernels  46.7 us (15%)
  starting transfers between devices  23.2 us (8%)
  local copies, waits for them, and re-layouts  7.47 us (2%)
    all_to_all x1, waiting for transfers between devices, per_device(): returned = exchange(half_ffn(arrived, w_gate, w_up, w_down))  114 us
    all_to_all x1, waiting for transfers between devices, per_device(): arrived = exchange(outgoing.reshape((devices,) + outgoing.shape[2:]))  108 us
    pallas_call x1, Pallas kernels, half_ffn(): pl.pallas_call(ffn_kernel, grid=(sources // block,), in_specs=[pl.BlockSp...  29.6 us
    all_to_all x1, starting transfers between devices, per_device(): returned = exchange(half_ffn(arrived, w_gate, w_up, w_down))  12.4 us
    all_to_all x1, starting transfers between devices, per_device(): arrived = exchange(outgoing.reshape((devices,) + outgoing.shape[2:]))  10.9 us
    pallas_call x1, Pallas kernels, combine(): pl.pallas_call(combine_kernel, grid=(experts // block,), in_specs=[pl.Blo...  9.16 us
    pallas_call x1, Pallas kernels, dispatch(): pl.pallas_call(dispatch_kernel, grid=(experts // block,), in_specs=[pl.Bl...  7.96 us
    unnamed x6, local copies, waits for them, and re-layouts  7.47 us
  transfers between devices with their start and end apart: 2, of which 2 were waited for; matrix products, arithmetic and copies ran while one was open for 3% of the time, Pallas kernels for 0%

profile of v1, /device:TPU:37, one launch (start us, length us, event | category | flops | bytes accessed | tf_op | source)
XLA Modules:
  0.0 300.0 jit_solution(956869556212719237)
XLA Ops:
  0.0 8.0 %dispatch_rows.1 = bf16[64,2,16,2304]{3,2,1,0:T(8,128)(2,1)} custom-call(s32[6,128]{1,0:T(8,128)} %bitcast.6, bf16[128,2048]{1,0:T(8,128)(2,1)} %tokens_ref.1), custom_call_target="tpu_custom_call" | custom-call | flops 1207959552 | bytes 9437184 | tf_op jit(solution)/shard_map/dispatch_rows/pallas_call | solution.py:87
  8.0 0.0 copy-start
  8.0 10.9 %all-to-all-start = ((bf16[128,16,2304]{2,1,0:T(8,128)(2,1)}), bf16[128,16,2304]{2,1,0:T(8,128)(2,1)}, u32[]{:S(2)}, u32[]{:S(2)}) async-start(bf16[128,16,2304]{2,1,0:T(8,128)(2,1)} %bitcast.5), calls=%async_computation | async-start | bytes 18874368 | tf_op jit(solution)/shard_map/all_to_all | solution.py:236
  18.9 0.0 copy-done
  18.9 2.8 copy.7.gate_ref
  21.7 4.7 %copy.8.up_ref = bf16[1,2048,704]{2,1,0:T(8,128)(2,1)} copy(bf16[1,2048,704]{1,2,0:T(8,128)(2,1)} %param.10) | data formatting | bytes 5767168 | tf_op args[4]
  26.3 107.5 %all-to-all-done.x_ref = bf16[128,16,2304]{2,1,0:T(8,128)(2,1)} async-done(((bf16[128,16,2304]{2,1,0:T(8,128)(2,1)}), bf16[128,16,2304]{2,1,0:T(8,128)(2,1)}, u32[]{:S(2)}, u32[]{:S(2)}) %all-to-all-start) | async-done | bytes 9437216 | tf_op jit(solution)/shard_map/all_to_all | solution.py:236
  133.9 29.6 %half_ffn.1 = bf16[128,16,2304]{2,1,0:T(8,128)(2,1)} custom-call(bf16[128,16,2304]{2,1,0:T(8,128)(2,1)} %all-to-all-done.x_ref, bf16[1,2048,704]{2,1,0:T(8,128)(2,1)} %copy.7.gate_ref, bf16[1,2048,704]{2,1,0:T(8,128)(2,1)} %copy.8.up_ref, bf16[1,704,2048]{2,1,0:T(8,128)(2,1)} %down_ref.1), custom_call_target="tpu_custom_call" | custom-call | flops 19931332608 | bytes 27525120 | tf_op jit(solution)/shard_map/half_ffn/pallas_call | solution.py:135
  163.4 0.0 copy-start.1
  163.4 12.4 %all-to-all-start.1 = ((bf16[128,16,2304]{2,1,0:T(8,128)(2,1)}), bf16[128,16,2304]{2,1,0:T(8,128)(2,1)}, u32[]{:S(2)}, u32[]{:S(2)}) async-start(bf16[128,16,2304]{2,1,0:T(8,128)(2,1)} %half_ffn.1), calls=%async_computation.1 | async-start | bytes 18874368 | tf_op jit(solution)/shard_map/all_to_all | solution.py:237
  175.8 0.0 copy-done.1
  175.8 0.6 convert_bitcast_fusion.gates_ref
  176.4 114.4 %all-to-all-done.1 = bf16[128,16,2304]{2,1,0:T(8,128)(2,1)} async-done(((bf16[128,16,2304]{2,1,0:T(8,128)(2,1)}), bf16[128,16,2304]{2,1,0:T(8,128)(2,1)}, u32[]{:S(2)}, u32[]{:S(2)}) %all-to-all-start.1) | async-done | bytes 9437216 | tf_op jit(solution)/shard_map/all_to_all | solution.py:237
  290.8 9.2 %combine_rows.1 = bf16[128,2048]{1,0:T(8,128)(2,1)} custom-call(s32[6,128]{1,0:T(8,128)} %bitcast.7, f32[6,128]{1,0:T(8,128)} %convert_bitcast_fusion.gates_ref, bf16[64,2,16,2304]{3,2,1,0:T(8,128)(2,1)} %bitcast.3.rows_ref), custom_call_target="tpu_custom_call" | custom-call | flops 1207959552 | bytes 9437184 | tf_op jit(solution)/shard_map/combine_rows/pallas_call | solution.py:204
Async XLA Ops:
  8.0 10.9 %copy-start = (bf16[1,2048,704]{1,2,0:T(8,128)(2,1)S(1)}, bf16[1,2048,704]{1,2,0:T(8,128)(2,1)}, u32[]{:S(2)}) copy-start(bf16[1,2048,704]{1,2,0:T(8,128)(2,1)} %param.9) | copy-start | bytes 8650756
  8.0 125.9 %all-to-all-start = ((bf16[128,16,2304]{2,1,0:T(8,128)(2,1)}), bf16[128,16,2304]{2,1,0:T(8,128)(2,1)}, u32[]{:S(2)}, u32[]{:S(2)}) async-start(bf16[128,16,2304]{2,1,0:T(8,128)(2,1)} %bitcast.5), calls=%async_computation | async-start | bytes 18874368 | tf_op jit(solution)/shard_map/all_to_all | solution.py:236
  163.4 12.4 %copy-start.1 = (bf16[128,6]{0,1:T(8,128)(2,1)S(1)}, bf16[128,6]{0,1:T(8,128)(2,1)}, u32[]{:S(2)}) copy-start(bf16[128,6]{0,1:T(8,128)(2,1)} %param.8) | copy-start | bytes 4612
  163.4 127.4 %all-to-all-start.1 = ((bf16[128,16,2304]{2,1,0:T(8,128)(2,1)}), bf16[128,16,2304]{2,1,0:T(8,128)(2,1)}, u32[]{:S(2)}, u32[]{:S(2)}) async-start(bf16[128,16,2304]{2,1,0:T(8,128)(2,1)} %half_ffn.1), calls=%async_computation.1 | async-start | bytes 18874368 | tf_op jit(solution)/shard_map/all_to_all | solution.py:237

commit v2 on v1

v2 whole, which is shorter than its diff:
```python
import functools

import jax
import jax.numpy as jnp
from jax import lax
from jax.experimental import pallas as pl
from jax.experimental.pallas import tpu as pltpu
from jax.sharding import Mesh, PartitionSpec as P

AXES = ("grp", "x", "y")
PLANE = ("grp", "x")
CAP = 18
MAIN = 16
PIECES = 8
TILE = MAIN * PIECES
RING = 4


def split_matrix():
    row = lax.broadcasted_iota(jnp.int32, (TILE, TILE), 0)
    col = lax.broadcasted_iota(jnp.int32, (TILE, TILE), 1)
    source = (row % MAIN) // 2 * MAIN + (row % 2) * PIECES + row // MAIN
    return (source == col).astype(jnp.bfloat16)


def exact_dot(a, b, dims=((1,), (0,))):
    return lax.dot_general(a, b, (dims, ((), ())), preferred_element_type=jnp.float32)


def pieces_to_rows(pieces, matrix):
    tiles = []
    for tile in range(pieces.shape[0] // TILE):
        stacked = exact_dot(matrix, pieces[TILE * tile : TILE * (tile + 1)])
        stacked = stacked.astype(jnp.bfloat16)
        tiles.append(
            jnp.concatenate([stacked[MAIN * q : MAIN * (q + 1)] for q in range(PIECES)], axis=1)
        )
    return jnp.concatenate(tiles, axis=0)


def rows_to_pieces(rows, matrix):
    width = rows.shape[1] // PIECES
    tiles = []
    for tile in range(rows.shape[0] // MAIN):
        part = rows[MAIN * tile : MAIN * (tile + 1)]
        stacked = jnp.concatenate(
            [part[:, width * q : width * (q + 1)] for q in range(PIECES)], axis=0
        )
        tiles.append(exact_dot(matrix, stacked, ((0,), (0,))).astype(jnp.bfloat16))
    return jnp.concatenate(tiles, axis=0)


def slots_of(ids_t, expert, gates_t=None):
    count = ids_t.shape[1]
    used = jnp.zeros(expert.shape, jnp.float32)
    weight = jnp.zeros(expert.shape, jnp.float32)
    for k in range(ids_t.shape[0]):
        hit = expert == ids_t[k : k + 1, :]
        used = jnp.where(hit, 1.0, used)
        if gates_t is not None:
            weight = jnp.where(hit, gates_t[k : k + 1, :], weight)
    earlier = lax.broadcasted_iota(jnp.int32, (count, count), 0)
    later = lax.broadcasted_iota(jnp.int32, (count, count), 1)
    before = exact_dot(used.astype(jnp.bfloat16), (earlier < later).astype(jnp.bfloat16))
    return jnp.where(used > 0.0, before, -1.0), weight


def near_first(rows, count, pair):
    row = lax.broadcasted_iota(jnp.int32, (rows, count), 0)
    other = row % 2
    return row - other + jnp.where(other == 0, pair, 1 - pair)


def own_pair(rows, count, pair):
    return 2 * lax.broadcasted_iota(jnp.int32, (rows, count), 0) + pair


def pick_rows(slot, tokens):
    block, count = slot.shape
    model = tokens.shape[1]
    main_id = lax.broadcasted_iota(jnp.int32, (block, MAIN, count), 1).astype(jnp.float32)
    pick = (slot[:, None, :] == main_id).astype(jnp.float32).reshape(block * MAIN, count)
    rows = exact_dot(pick.astype(jnp.bfloat16), tokens).astype(jnp.bfloat16)
    row = lax.broadcasted_iota(jnp.int32, (2 * block, count), 0)
    slot_twice = jnp.broadcast_to(slot[:, None, :], (block, 2, count)).reshape(2 * block, count)
    pick_last = (slot_twice == (MAIN + row % 2).astype(jnp.float32)).astype(jnp.bfloat16)
    last = exact_dot(pick_last, tokens).astype(jnp.bfloat16)
    pieces = rows_to_pieces(last, split_matrix())
    return rows.reshape(block, MAIN, model), pieces.reshape(block, MAIN, model // PIECES)


def combine_rows(slot, weight, main, pieces):
    block, count = slot.shape

    def spread(first, slots):
        shape = (block, slots, count)
        slot_id = first + lax.broadcasted_iota(jnp.int32, shape, 1)
        hit = slot[:, None, :] == slot_id.astype(jnp.float32)
        scaled = jnp.where(hit, jnp.broadcast_to(weight[:, None, :], shape), 0.0)
        return scaled.reshape(block * slots, count).astype(jnp.bfloat16)

    total = exact_dot(spread(0, MAIN), main, ((0,), (0,)))
    last = pieces_to_rows(pieces, split_matrix())
    return total + exact_dot(spread(MAIN, CAP - MAIN), last, ((0,), (0,)))


def late_dispatch_kernel(pair_ref, ids_ref, tokens_ref, out_ref, slot_ref):
    block, _, _ = out_ref.shape
    model = tokens_ref.shape[1]
    step = pl.program_id(0)

    @pl.when(step == 0)
    def _():
        expert = near_first(*slot_ref.shape, pair_ref[0])
        slot_ref[...] = slots_of(ids_ref[...], expert)[0]

    slot = slot_ref[pl.ds(pl.multiple_of(step * block, block), block), :]
    rows, pieces = pick_rows(slot, tokens_ref[...])
    out_ref[:, :, :model] = rows
    out_ref[:, :, model:] = pieces


def late_dispatch(pair, ids_t, tokens, experts):
    count, model = tokens.shape
    half = model // 2
    width = half * CAP // MAIN
    block = 16
    return pl.pallas_call(
        late_dispatch_kernel,
        grid=(experts // block,),
        in_specs=[
            pl.BlockSpec(memory_space=pltpu.SMEM),
            pl.BlockSpec(ids_t.shape, lambda i: (0, 0)),
            pl.BlockSpec((count, half), lambda i: (0, 0)),
        ],
        out_specs=pl.BlockSpec((block, MAIN, width), lambda i: (i, 0, 0)),
        out_shape=jax.ShapeDtypeStruct((experts, MAIN, width), jnp.bfloat16),
        scratch_shapes=[pltpu.VMEM((experts, count), jnp.float32)],
        cost_estimate=pl.CostEstimate(
            flops=2 * experts * CAP * count * half,
            bytes_accessed=2 * experts * MAIN * width,
            transcendentals=0,
        ),
        name="late_dispatch",
    )(pair, ids_t, tokens)


def early_dispatch_kernel(pair_ref, ids_ref, tokens_ref, out_ref):
    chunks = out_ref.shape[0]
    _, count, model = tokens_ref.shape
    expert = own_pair(chunks, count, pair_ref[0])
    slot = slots_of(ids_ref[0], expert)[0]
    rows, pieces = pick_rows(slot, tokens_ref[0])
    out_ref[:, 0, :, :model] = rows
    out_ref[:, 0, :, model:] = pieces


def early_dispatch(pair, ids_t, tokens, chunks):
    ring, count, half = tokens.shape
    width = half * CAP // MAIN
    return pl.pallas_call(
        early_dispatch_kernel,
        grid=(ring,),
        in_specs=[
            pl.BlockSpec(memory_space=pltpu.SMEM),
            pl.BlockSpec((1,) + ids_t.shape[1:], lambda i: (i, 0, 0)),
            pl.BlockSpec((1, count, half), lambda i: (i, 0, 0)),
        ],
        out_specs=pl.BlockSpec((chunks, 1, MAIN, width), lambda i: (0, i, 0, 0)),
        out_shape=jax.ShapeDtypeStruct((chunks, ring, MAIN, width), jnp.bfloat16),
        cost_estimate=pl.CostEstimate(
            flops=2 * ring * chunks * CAP * count * half,
            bytes_accessed=2 * ring * chunks * MAIN * width,
            transcendentals=0,
        ),
        name="early_dispatch",
    )(pair, ids_t, tokens)


def ffn_kernel(*refs):
    late_in, (early_in, gate_ref, up_ref, down_ref) = refs[:RING], refs[RING : RING + 4]
    late_out, early_out, rows_ref = refs[RING + 4 : 2 * RING + 4], refs[-2], refs[-1]
    chunks, _, width = late_in[0].shape
    half = width * MAIN // CAP
    main = chunks * MAIN
    step = pl.program_id(0)
    matrix = split_matrix()

    def unpack(block, at):
        rows_ref[:main, at : at + half] = block[:, :, :half].reshape(main, half)
        rows_ref[main:, at : at + half] = pieces_to_rows(
            block[:, :, half:].reshape(main, width - half), matrix
        )

    def pack(value, ref, *index):
        ref[(slice(None), *index, slice(None), slice(0, half))] = value[:main].reshape(
            chunks, MAIN, half
        )
        ref[(slice(None), *index, slice(None), slice(half, None))] = rows_to_pieces(
            value[main:], matrix
        ).reshape(chunks, MAIN, width - half)

    for j in range(RING):

        @pl.when(step == j)
        def _(j=j):
            unpack(late_in[j][...], 0)

    unpack(early_in[:, 0], half)
    rows = rows_ref[...]
    gate = exact_dot(rows, gate_ref[0])
    up = exact_dot(rows, up_ref[0])
    hidden = (gate / (1.0 + jnp.exp(-gate)) * up).astype(jnp.bfloat16)
    half_out = exact_dot(hidden, down_ref[0]).astype(jnp.bfloat16)
    for j in range(RING):

        @pl.when(step == j)
        def _(j=j):
            pack(half_out[:, :half], late_out[j])

    pack(half_out[:, half:], early_out, 0)


def half_ffn(late, early, w_gate, w_up, w_down):
    chunks, _, width = late[0].shape
    model, hidden = w_gate.shape[1:]
    rows = RING * chunks * CAP
    once = pl.Buffered(1)
    late_spec = pl.BlockSpec(late[0].shape, lambda i: (0, 0, 0), pipeline_mode=once)
    early_spec = pl.BlockSpec((chunks, 1, MAIN, width), lambda i: (0, i, 0, 0))
    weights = [
        pl.BlockSpec(w.shape, lambda i: (0, 0, 0), pipeline_mode=once)
        for w in (w_gate, w_up, w_down)
    ]
    late_shape = jax.ShapeDtypeStruct(late[0].shape, jnp.bfloat16)
    *late_out, early_out = pl.pallas_call(
        ffn_kernel,
        grid=(RING,),
        in_specs=[late_spec] * RING + [early_spec] + weights,
        out_specs=[late_spec] * RING + [early_spec],
        out_shape=[late_shape] * RING + [jax.ShapeDtypeStruct(early.shape, jnp.bfloat16)],
        scratch_shapes=[pltpu.VMEM((chunks * CAP, model), jnp.bfloat16)],
        cost_estimate=pl.CostEstimate(
            flops=6 * rows * model * hidden,
            bytes_accessed=4 * rows * model + 6 * model * hidden,
            transcendentals=rows * hidden,
        ),
        compiler_params=pltpu.CompilerParams(vmem_limit_bytes=56 * 1024 * 1024),
        name="half_ffn",
    )(*late, early, w_gate, w_up, w_down)
    return late_out, early_out


def sum_halves_kernel(a_ref, b_ref, c_ref, d_ref, out_ref):
    for r, (first, second) in enumerate(((a_ref, b_ref), (c_ref, d_ref))):
        both = first[...].astype(jnp.float32) + second[...].astype(jnp.float32)
        out_ref[:, r] = both.astype(jnp.bfloat16)


def sum_halves(arrays):
    chunks, _, width = arrays[0].shape
    block = 8
    return pl.pallas_call(
        sum_halves_kernel,
        grid=(chunks // block,),
        in_specs=[pl.BlockSpec((block, MAIN, width), lambda i: (i, 0, 0))] * RING,
        out_specs=pl.BlockSpec((block, 2, MAIN, width), lambda i: (i, 0, 0, 0)),
        out_shape=jax.ShapeDtypeStruct((chunks, 2, MAIN, width), jnp.bfloat16),
        cost_estimate=pl.CostEstimate(
            flops=4 * chunks * MAIN * width, bytes_accessed=12 * chunks * MAIN * width,
            transcendentals=0,
        ),
        name="sum_halves",
    )(*arrays)


def early_combine_kernel(pair_ref, ids_ref, gates_ref, rows_ref, out_ref):
    chunks = rows_ref.shape[0]
    _, count, half = out_ref.shape
    expert = own_pair(chunks, count, pair_ref[0])
    slot, weight = slots_of(ids_ref[0], expert, gates_ref[0])
    main = rows_ref[:, 0, :, :half].reshape(chunks * MAIN, half)
    pieces = rows_ref[:, 0, :, half:].reshape(chunks * MAIN, half // PIECES)
    out_ref[0] = combine_rows(slot, weight, main, pieces).astype(jnp.bfloat16)


def early_combine(pair, ids_t, gates_t, rows):
    chunks, ring, _, width = rows.shape
    count = ids_t.shape[2]
    half = width * MAIN // CAP
    return pl.pallas_call(
        early_combine_kernel,
        grid=(ring,),
        in_specs=[
            pl.BlockSpec(memory_space=pltpu.SMEM),
            pl.BlockSpec((1,) + ids_t.shape[1:], lambda i: (i, 0, 0)),
            pl.BlockSpec((1,) + gates_t.shape[1:], lambda i: (i, 0, 0)),
            pl.BlockSpec((chunks, 1, MAIN, width), lambda i: (0, i, 0, 0)),
        ],
        out_specs=pl.BlockSpec((1, count, half), lambda i: (i, 0, 0)),
        out_shape=jax.ShapeDtypeStruct((ring, count, half), jnp.bfloat16),
        cost_estimate=pl.CostEstimate(
            flops=2 * ring * chunks * CAP * count * half,
            bytes_accessed=2 * ring * chunks * MAIN * width,
            transcendentals=0,
        ),
        name="early_combine",
    )(pair, ids_t, gates_t, rows)


def final_kernel(pair_ref, ids_ref, gates_ref, rows_ref, *refs):
    parts, (out_ref, slot_ref, weight_ref, acc_ref) = refs[:RING], refs[RING:]
    block = rows_ref.shape[0]
    half = acc_ref.shape[1]
    step = pl.program_id(0)

    @pl.when(step == 0)
    def _():
        expert = near_first(*slot_ref.shape, pair_ref[0])
        slot, weight = slots_of(ids_ref[...], expert, gates_ref[...])
        slot_ref[...] = slot
        weight_ref[...] = weight
        acc_ref[...] = jnp.zeros_like(acc_ref)

    here = pl.ds(pl.multiple_of(step * block, block), block)
    main = rows_ref[:, :, :half].reshape(block * MAIN, half)
    pieces = rows_ref[:, :, half:].reshape(block * MAIN, half // PIECES)
    acc_ref[...] += combine_rows(slot_ref[here, :], weight_ref[here, :], main, pieces)

    @pl.when(step == pl.num_programs(0) - 1)
    def _():
        out_ref[:, :half] = acc_ref[...].astype(jnp.bfloat16)
        total = parts[0][...].astype(jnp.float32)
        for part in parts[1:]:
            total += part[...].astype(jnp.float32)
        out_ref[:, half:] = total.astype(jnp.bfloat16)


def final_combine(pair, ids_t, gates_t, rows, parts):
    experts, _, width = rows.shape
    count, half = parts[0].shape
    block = 16
    whole = lambda i: (0, 0)
    return pl.pallas_call(
        final_kernel,
        grid=(experts // block,),
        in_specs=[
            pl.BlockSpec(memory_space=pltpu.SMEM),
            pl.BlockSpec(ids_t.shape, whole),
            pl.BlockSpec(gates_t.shape, whole),
            pl.BlockSpec((block, MAIN, width), lambda i: (i, 0, 0)),
        ]
        + [pl.BlockSpec((count, half), whole)] * RING,
        out_specs=pl.BlockSpec((count, 2 * half), whole),
        out_shape=jax.ShapeDtypeStruct((count, 2 * half), jnp.bfloat16),
        scratch_shapes=[
            pltpu.VMEM((experts, count), jnp.float32),
            pltpu.VMEM((experts, count), jnp.float32),
            pltpu.VMEM((count, half), jnp.float32),
        ],
        cost_estimate=pl.CostEstimate(
            flops=2 * experts * CAP * count * half,
            bytes_accessed=2 * experts * MAIN * width,
            transcendentals=0,
        ),
        name="final_combine",
    )(pair, ids_t, gates_t, rows, *parts)


def across(array, j):
    return lax.ppermute(array, "y", [(y, y ^ j) for y in range(RING)])


def gather_ring(array):
    return jnp.stack([array] + [across(array, j) for j in range(1, RING)])


def plane_exchange(array):
    return lax.all_to_all(array, PLANE, split_axis=0, concat_axis=0, tiled=True)


def per_device(tokens, expert_ids, gate_weights, w_gate, w_up, w_down):
    chunks = lax.axis_size("grp") * lax.axis_size("x")
    experts = 2 * chunks
    top = expert_ids.shape[1]
    half = tokens.shape[1] // 2
    pair = (lax.axis_index("y") // 2).astype(jnp.int32).reshape(1)
    ids_t = expert_ids.T
    gates_t = gate_weights.T

    late = late_dispatch(pair, ids_t, tokens, experts)
    width = late.shape[2]
    late = plane_exchange(late.reshape(chunks, 2 * MAIN, width))
    late = late.reshape(chunks, 2, MAIN, width)
    near, far = late[:, 0], late[:, 1]

    routing = gather_ring(jnp.concatenate([ids_t.astype(jnp.bfloat16), gates_t], axis=0))
    ids_ring = routing[:, :top].astype(jnp.int32)
    gates_ring = routing[:, top:].astype(jnp.float32)
    early = early_dispatch(pair, ids_ring, gather_ring(tokens[:, half:]), chunks)
    early = plane_exchange(early.reshape(chunks, RING * MAIN, width))
    early = early.reshape(chunks, RING, MAIN, width)

    late_in = (near, across(near, 1), across(far, 2), across(far, 3))
    late_out, early_out = half_ffn(late_in, early, w_gate, w_up, w_down)

    early_out = plane_exchange(early_out.reshape(chunks, RING * MAIN, width))
    late_back = [late_out[0]] + [across(late_out[j], j) for j in range(1, RING)]
    late_back = plane_exchange(sum_halves(late_back).reshape(chunks, 2 * MAIN, width))
    partial = early_combine(
        pair, ids_ring, gates_ring, early_out.reshape(chunks, RING, MAIN, width)
    )
    parts = [partial[0]] + [across(partial[j], j) for j in range(1, RING)]
    return final_combine(
        pair, ids_t, gates_t.astype(jnp.float32), late_back.reshape(experts, MAIN, width), parts
    )


def solution(mesh):
    ring = Mesh(mesh.devices.reshape(mesh.devices.shape[0], -1, RING), AXES)
    rows = P(AXES, None)
    weights = P(AXES, None, None)
    return jax.shard_map(
        per_device,
        mesh=ring,
        in_specs=(rows, rows, rows, weights, weights, weights),
        out_specs=rows,
        check_vma=False,
    )
```

time: 302 us -> 255 us (0.84)
  waiting for transfers between devices: 222 us -> 123 us
  starting transfers between devices: 23.2 us -> 52.8 us
  Pallas kernels: 46.7 us -> 58.4 us
  local copies, waits for them, and re-layouts: 7.47 us -> 15.6 us
    all_to_all x2 -> x4, waiting for transfers between devices: 222 us -> 16.4 us  [plane_exchange(): return lax.all_to_all(array, PLANE, split_axis=0, concat_axis=0, tiled=True)]
    ppermute x0 -> x15, waiting for transfers between devices: none -> 106 us  [across(): return lax.ppermute(array, 'y', [(y, y ^ j) for y in range(RING)])]
    ppermute x0 -> x15, starting transfers between devices: none -> 18.7 us  [across(): return lax.ppermute(array, 'y', [(y, y ^ j) for y in range(RING)])]
    pallas_call x3 -> x6, Pallas kernels: 46.7 us -> 58.4 us  [the longest x1 34 us: half_ffn(): pl.pallas_call(ffn_kernel, grid=(RING,), in_specs=[late_spec] * RING + [e...]
    all_to_all x2 -> x4, starting transfers between devices: 23.2 us -> 34 us  [plane_exchange(): return lax.all_to_all(array, PLANE, split_axis=0, concat_axis=0, tiled=True)]
    unnamed x6 -> x28, local copies, waits for them, and re-layouts: 7.47 us -> 12.3 us
    squeeze x0 -> x2, local copies, waits for them, and re-layouts: none -> 3.28 us  [the longest x1 2.09 us: per_device(): parts = [partial[0]] + [across(partial[j], j) for j in range(1, RING)]]
  transfers between devices with their start and end apart: 2 -> 19, of which waited for: 2 -> 9; matrix products, arithmetic and copies ran while one was open for 3% -> 6% of each run, Pallas kernels for 0% -> 6%
where the time goes in v2:
time: 255 us; the launch traced here: 252 us
  waiting for transfers between devices  123 us (48%)
  Pallas kernels  58.4 us (23%)
  starting transfers between devices  52.8 us (21%)
  local copies, waits for them, and re-layouts  15.6 us (6%)
    ppermute x15, waiting for transfers between devices, across(): return lax.ppermute(array, 'y', [(y, y ^ j) for y in range(RING)])  106 us
    all_to_all x4, starting transfers between devices, plane_exchange(): return lax.all_to_all(array, PLANE, split_axis=0, concat_axis=0, tiled=True)  34 us
    pallas_call x1, Pallas kernels, half_ffn(): pl.pallas_call(ffn_kernel, grid=(RING,), in_specs=[late_spec] * RING + [e...  34 us
    ppermute x15, starting transfers between devices, across(): return lax.ppermute(array, 'y', [(y, y ^ j) for y in range(RING)])  18.7 us
    all_to_all x4, waiting for transfers between devices, plane_exchange(): return lax.all_to_all(array, PLANE, split_axis=0, concat_axis=0, tiled=True)  16.4 us
    unnamed x28, local copies, waits for them, and re-layouts  12.3 us
    pallas_call x1, Pallas kernels, early_dispatch(): pl.pallas_call(early_dispatch_kernel, grid=(ring,), in_specs=[pl.BlockSpe...  5.66 us
    pallas_call x1, Pallas kernels, early_combine(): pl.pallas_call(early_combine_kernel, grid=(ring,), in_specs=[pl.BlockSpec...  5.21 us
  transfers between devices with their start and end apart: 19, of which 9 were waited for; matrix products, arithmetic and copies ran while one was open for 6% of the time, Pallas kernels for 6%

profile of v2, /device:TPU:37, one launch (start us, length us, event | category | flops | bytes accessed | tf_op | source)
XLA Modules:
  0.0 252.0 jit_solution(2059824962763778871)
XLA Ops:
  0.0 4.1 %late_dispatch.1 = bf16[64,16,1152]{2,1,0:T(8,128)(2,1)} custom-call(s32[1]{0:T(128)} %bitcast.pair_ref, s32[6,128]{1,0:T(8,128)} %bitcast.48, bf16[128,2048]{1,0:T(8,128)(2,1)} %tokens_ref.1), custom_call_target="tpu_custom_call" | custom-call | flops 301989888 | bytes 2359296 | tf_op jit(solution)/shard_map/late_dispatch/pallas_call | solution.py:128
  4.1 8.4 %all-to-all-start = ((bf16[32,32,1152]{2,1,0:T(8,128)(2,1)}), bf16[32,32,1152]{2,1,0:T(8,128)(2,1)S(1)}, u32[]{:S(2)}, u32[]{:S(2)}) async-start(bf16[32,32,1152]{2,1,0:T(8,128)(2,1)} %bitcast.42), calls=%async_computation | async-start | bytes 4718592 | tf_op jit(solution)/shard_map/all_to_all | solution.py:379
  12.6 0.0 copy-done.9
  12.6 0.0 copy-done.10
  12.6 2.8 %collective-permute-start.5 = (bf16[12,128]{1,0:T(8,128)(2,1)S(1)}, bf16[12,128]{1,0:T(8,128)(2,1)S(1)}, u32[]{:S(2)}, u32[]{:S(2)}) collective-permute-start(bf16[12,128]{1,0:T(8,128)(2,1)S(1)} %get-tuple-element.26), channel_id=1, source_target_pairs={{0,3},{1,2},{2,1},{3,0},{4,7},{5,6},{6,5},{7,4},{8,11},{9,10},{10,... | collective-permute-start | bytes 9224 | tf_op jit(solution)/shard_map/ppermute | solution.py:371
  15.4 0.0 collective-permute-start.3
  15.4 1.3 collective-permute-start.4
  16.7 0.0 copy-done.4
  16.7 0.3 collective-permute-start.6
  17.0 3.6 %collective-permute-start.7 = (bf16[128,1024]{1,0:T(8,128)(2,1)S(1)}, bf16[128,1024]{1,0:T(8,128)(2,1)S(1)}, u32[]{:S(2)}, u32[]{:S(2)}) collective-permute-start(bf16[128,1024]{1,0:T(8,128)(2,1)S(1)} %get-tuple-element.22), channel_id=1, source_target_pairs={{0,2},{1,3},{2,0},{3,1},{4,6},{5,7},{6,4},{7,5},{8,10},{9,11},{10,... | collective-permute-start | bytes 786440 | tf_op jit(solution)/shard_map/ppermute | solution.py:371
  20.6 0.0 collective-permute-done.5
  20.6 0.1 collective-permute-start.8
  20.7 0.0 collective-permute-done.3
  20.7 0.0 collective-permute-done.4
  20.7 0.6 slice_convert_fusion
  21.3 2.3 collective-permute-done.6
  23.6 7.8 %collective-permute-done.7 = bf16[128,1024]{1,0:T(8,128)(2,1)S(1)} collective-permute-done((bf16[128,1024]{1,0:T(8,128)(2,1)S(1)}, bf16[128,1024]{1,0:T(8,128)(2,1)S(1)}, u32[]{:S(2)}, u32[]{:S(2)}) %collective-permute-start.7) | collective-permute-done | bytes 262176 | tf_op jit(solution)/shard_map/ppermute | solution.py:371
  31.4 2.6 %collective-permute-done.8 = bf16[128,1024]{1,0:T(8,128)(2,1)S(1)} collective-permute-done((bf16[128,1024]{1,0:T(8,128)(2,1)S(1)}, bf16[128,1024]{1,0:T(8,128)(2,1)S(1)}, u32[]{:S(2)}, u32[]{:S(2)}) %collective-permute-start.8) | collective-permute-done | bytes 262176 | tf_op jit(solution)/shard_map/ppermute | solution.py:371
  34.0 1.2 pad_maximum_fusion.tokens_ref
  35.2 5.7 %early_dispatch.1 = bf16[32,4,16,1152]{3,2,1,0:T(8,128)(2,1)} custom-call(s32[1]{0:T(128)} %bitcast.pair_ref, s32[4,6,128]{2,1,0:T(8,128)} %get-tuple-element.24.ids_ref, bf16[4,128,1024]{2,1,0:T(8,128)(2,1)} %pad_maximum_fusion.tokens_ref), custom_call_target="tpu_custom_call" | custom-call | flops 603979776 | bytes 4718592 | tf_op jit(solution)/shard_map/early_dispatch/pallas_call | solution.py:161
  40.9 0.0 all-to-all-done
  40.9 9.2 %all-to-all-start.1 = ((bf16[32,64,1152]{2,1,0:T(8,128)(2,1)}), bf16[32,64,1152]{2,1,0:T(8,128)(2,1)}, u32[]{:S(2)}, u32[]{:S(2)}) async-start(bf16[32,64,1152]{2,1,0:T(8,128)(2,1)} %bitcast.39), calls=%async_computation.1 | async-start | bytes 9437184 | tf_op jit(solution)/shard_map/all_to_all | solution.py:379
  50.1 1.2 slice_bitcast_fusion
  51.3 0.0 collective-permute-start
  51.3 1.5 collective-permute-start.1
  52.8 2.3 collective-permute-start.2
  55.1 4.6 %copy.11.refs_5_ = bf16[1,2048,704]{2,1,0:T(8,128)(2,1)} copy(bf16[1,2048,704]{1,2,0:T(8,128)(2,1)} %param.9) | data formatting | bytes 5767168 | tf_op args[3]
  59.8 0.0 copy-done.5
  59.8 4.6 %copy.12.refs_6_ = bf16[1,2048,704]{2,1,0:T(8,128)(2,1)} copy(bf16[1,2048,704]{1,2,0:T(8,128)(2,1)} %param.10) | data formatting | bytes 5767168 | tf_op args[4]
  64.4 14.1 %collective-permute-done.refs_1_ = bf16[32,16,1152]{2,1,0:T(8,128)(2,1)S(1)} collective-permute-done((bf16[32,16,1152]{2,1,0:T(8,128)(2,1)S(1)}, bf16[32,16,1152]{2,1,0:T(8,128)(2,1)S(1)}, u32[]{:S(2)}, u32[]{:S(2)}) %collective-permute-start) | collective-permute-done | bytes 1179680 | tf_op jit(solution)/shard_map/ppermute | solution.py:371
  78.5 25.3 %collective-permute-done.1.refs_2_ = bf16[32,16,1152]{2,1,0:T(8,128)(2,1)S(1)} collective-permute-done((bf16[32,16,1152]{2,1,0:T(8,128)(2,1)}, bf16[32,16,1152]{2,1,0:T(8,128)(2,1)S(1)}, u32[]{:S(2)}, u32[]{:S(2)}) %collective-permute-start.1) | collective-permute-done | bytes 1179680 | tf_op jit(solution)/shard_map/ppermute | solution.py:371
  103.8 2.4 collective-permute-done.2.refs_3_
  106.2 0.0 all-to-all-done.1
  106.2 0.0 copy-done.11
  106.2 0.0 copy-done.12
  106.2 34.0 %half_ffn.1 = (bf16[32,16,1152]{2,1,0:T(8,128)(2,1)}, bf16[32,16,1152]{2,1,0:T(8,128)(2,1)}, bf16[32,16,1152]{2,1,0:T(8,128)(2,1)}, bf16[32,16,1152]{2,1,0:T(8,128)(2,1)}, bf16[32,4,16,1152]{3,2,1,0:T(8,128)(2,1)}) custom-call(bf16[32,16,1152]{2,1,0:T(8,128)(2,1)} %copy-done.5, bf16[32,16,1152]{2,1,0:T(8,128)(2,1)} %copy-done.11, ...), custom_call_target="tpu_custom_call" | custom-call | flops 19931332608 | bytes 27525120 | tf_op jit(solution)/shard_map/half_ffn/pallas_call | solution.py:236
  140.2 8.9 %all-to-all-start.3 = ((bf16[32,64,1152]{2,1,0:T(8,128)(2,1)}), bf16[32,64,1152]{2,1,0:T(8,128)(2,1)}, u32[]{:S(2)}, u32[]{:S(2)}) async-start(bf16[32,64,1152]{2,1,0:T(8,128)(2,1)} %bitcast.44), calls=%async_computation.3 | async-start | bytes 9437184 | tf_op jit(solution)/shard_map/all_to_all | solution.py:379
  149.0 0.3 collective-permute-start.10
  149.3 2.2 collective-permute-start.11
  151.5 0.5 collective-permute-start.9
  152.0 26.0 %collective-permute-done.10.c_ref = bf16[32,16,1152]{2,1,0:T(8,128)(2,1)S(1)} collective-permute-done((bf16[32,16,1152]{2,1,0:T(8,128)(2,1)}, bf16[32,16,1152]{2,1,0:T(8,128)(2,1)S(1)}, u32[]{:S(2)}, u32[]{:S(2)}) %collective-permute-start.10) | collective-permute-done | bytes 1179680 | tf_op jit(solution)/shard_map/ppermute | solution.py:371
  178.0 25.8 %collective-permute-done.11.d_ref = bf16[32,16,1152]{2,1,0:T(8,128)(2,1)S(1)} collective-permute-done((bf16[32,16,1152]{2,1,0:T(8,128)(2,1)}, bf16[32,16,1152]{2,1,0:T(8,128)(2,1)S(1)}, u32[]{:S(2)}, u32[]{:S(2)}) %collective-permute-start.11) | collective-permute-done | bytes 1179680 | tf_op jit(solution)/shard_map/ppermute | solution.py:371
  203.9 0.0 collective-permute-done.9.b_ref
  203.9 1.0 copy-done.2
  204.9 0.4 copy-done.3
  205.3 4.5 %sum_halves.1 = bf16[32,2,16,1152]{3,2,1,0:T(8,128)(2,1)} custom-call(bf16[32,16,1152]{2,1,0:T(8,128)(2,1)} %get-tuple-element.10.a_ref, bf16[32,16,1152]{2,1,0:T(8,128)(2,1)} %copy-done.3, bf16[32,16,1152]{2,1,0:T(8,128)(2,1)} %copy-done.1, bf16[32,16,1152]{2,1,0:T(8,128)(2,1)} %copy-done.2), custom_call_target="tpu_custom_call" | custom-call | flops 2359296 | bytes 7077888 | tf_op jit(solution)/shard_map/sum_halves/pallas_call | solution.py:263
  209.7 0.0 all-to-all-done.3
  209.7 7.6 %all-to-all-start.2 = ((bf16[32,32,1152]{2,1,0:T(8,128)(2,1)}), bf16[32,32,1152]{2,1,0:T(8,128)(2,1)S(1)}, u32[]{:S(2)}, u32[]{:S(2)}) async-start(bf16[32,32,1152]{2,1,0:T(8,128)(2,1)} %bitcast.40), calls=%async_computation.2 | async-start | bytes 4718592 | tf_op jit(solution)/shard_map/all_to_all | solution.py:379
  217.3 5.2 %early_combine.1 = bf16[4,128,1024]{2,1,0:T(8,128)(2,1)} custom-call(s32[1]{0:T(128)} %bitcast.pair_ref, s32[4,6,128]{2,1,0:T(8,128)} %get-tuple-element.24.ids_ref, f32[4,6,128]{2,1,0:T(8,128)} %get-tuple-element.23.gates_ref, bf16[32,4,16,1152]{3,2,1,0:T(8,128)(2,1)} %bitcast.20.rows_ref), custom_call_target="tpu_custom_call" | custom-call | flops 603979776 | bytes 4718592 | tf_op jit(solution)/shard_map/early_combine/pallas_call | solution.py:291
  222.5 2.1 slice_bitcast_fusion.2
  224.6 0.0 collective-permute-start.12
  224.6 3.4 %collective-permute-start.13 = (bf16[128,1024]{1,0:T(8,128)(2,1)}, bf16[128,1024]{1,0:T(8,128)(2,1)S(1)}, u32[]{:S(2)}, u32[]{:S(2)}) collective-permute-start(bf16[128,1024]{1,0:T(8,128)(2,1)} %get-tuple-element.18), channel_id=1, source_target_pairs={{0,2},{1,3},{2,0},{3,1},{4,6},{5,7},{6,4},{7,5},{8,10},{9,11},{10,... | collective-permute-start | bytes 786440 | tf_op jit(solution)/shard_map/ppermute | solution.py:371
  228.0 0.5 collective-permute-start.14
  228.5 0.6 bitcast_convert_fusion.gates_ref
  229.1 16.4 %all-to-all-done.2 = bf16[32,32,1152]{2,1,0:T(8,128)(2,1)S(1)} async-done(((bf16[32,32,1152]{2,1,0:T(8,128)(2,1)}), bf16[32,32,1152]{2,1,0:T(8,128)(2,1)S(1)}, u32[]{:S(2)}, u32[]{:S(2)}) %all-to-all-start.2) | async-done | bytes 2359328 | tf_op jit(solution)/shard_map/all_to_all | solution.py:379
  245.5 0.0 collective-permute-done.12.refs_1_
  245.5 0.0 collective-permute-done.13.refs_2_
  245.5 0.0 collective-permute-done.14.refs_3_
  245.5 0.0 copy-start.8
  245.5 1.4 copy-done
  246.9 0.1 copy-done.6
  247.0 0.1 copy-done.7
  247.1 0.1 copy-done.8
  247.1 4.9 %final_combine.1 = bf16[128,2048]{1,0:T(8,128)(2,1)} custom-call(s32[1]{0:T(128)} %bitcast.pair_ref, s32[6,128]{1,0:T(8,128)} %bitcast.49, f32[6,128]{1,0:T(8,128)} %bitcast_convert_fusion.gates_ref, bf16[64,16,1152]{2,1,0:T(8,128)(2,1)} %bitcast.43, bf16[128,1024]{1,0:T(8,128)(2,1)} %get-tuple-element.20.refs_0_, bf16[128,1024]{1,0:T(8,128)(2,1)} %copy-done.6, ...), custom_call_target="tpu_custom_call" | custom-call | flops 301989888 | bytes 2359296 | tf_op jit(solution)/shard_map/final_combine/pallas_call | solution.py:344
  (17 shorter events, 0.1 us)
Async XLA Ops:
  4.1 8.4 %copy-start.9 = (s32[128,6]{0,1:T(8,128)S(1)}, s32[128,6]{0,1:T(8,128)}, u32[]{:S(2)}) copy-start(s32[128,6]{0,1:T(8,128)} %param.7) | copy-start | bytes 9220
  4.1 8.4 %copy-start.10 = (bf16[128,6]{0,1:T(8,128)(2,1)S(1)}, bf16[128,6]{0,1:T(8,128)(2,1)}, u32[]{:S(2)}) copy-start(bf16[128,6]{0,1:T(8,128)(2,1)} %param.8) | copy-start | bytes 4612
  4.1 12.6 %copy-start.4 = (bf16[128,2048]{1,0:T(8,128)(2,1)S(1)}, bf16[128,2048]{1,0:T(8,128)(2,1)}, u32[]{:S(2)}) copy-start(bf16[128,2048]{1,0:T(8,128)(2,1)} %tokens_ref.1) | copy-start | bytes 1572868
  4.1 36.7 %all-to-all-start = ((bf16[32,32,1152]{2,1,0:T(8,128)(2,1)}), bf16[32,32,1152]{2,1,0:T(8,128)(2,1)S(1)}, u32[]{:S(2)}, u32[]{:S(2)}) async-start(bf16[32,32,1152]{2,1,0:T(8,128)(2,1)} %bitcast.42), calls=%async_computation | async-start | bytes 4718592 | tf_op jit(solution)/shard_map/all_to_all | solution.py:379
  12.6 8.0 %collective-permute-start.5 = (bf16[12,128]{1,0:T(8,128)(2,1)S(1)}, bf16[12,128]{1,0:T(8,128)(2,1)S(1)}, u32[]{:S(2)}, u32[]{:S(2)}) collective-permute-start(bf16[12,128]{1,0:T(8,128)(2,1)S(1)} %get-tuple-element.26), channel_id=1, source_target_pairs={{0,3},{1,2},{2,1},{3,0},{4,7},{5,6},{6,5},{7,4},{8,11},{9,10},{10,... | collective-permute-start | bytes 9224 | tf_op jit(solution)/shard_map/ppermute | solution.py:371
  15.4 5.3 %collective-permute-start.3 = (bf16[12,128]{1,0:T(8,128)(2,1)S(1)}, bf16[12,128]{1,0:T(8,128)(2,1)S(1)}, u32[]{:S(2)}, u32[]{:S(2)}) collective-permute-start(bf16[12,128]{1,0:T(8,128)(2,1)S(1)} %get-tuple-element.26), channel_id=1, source_target_pairs={{0,1},{1,0},{2,3},{3,2},{4,5},{5,4},{6,7},{7,6},{8,9},{9,8},{10,11... | collective-permute-start | bytes 9224 | tf_op jit(solution)/shard_map/ppermute | solution.py:371
  15.4 5.3 %collective-permute-start.4 = (bf16[12,128]{1,0:T(8,128)(2,1)S(1)}, bf16[12,128]{1,0:T(8,128)(2,1)S(1)}, u32[]{:S(2)}, u32[]{:S(2)}) collective-permute-start(bf16[12,128]{1,0:T(8,128)(2,1)S(1)} %get-tuple-element.26), channel_id=1, source_target_pairs={{0,2},{1,3},{2,0},{3,1},{4,6},{5,7},{6,4},{7,5},{8,10},{9,11},{10,... | collective-permute-start | bytes 9224 | tf_op jit(solution)/shard_map/ppermute | solution.py:371
  16.7 6.9 %collective-permute-start.6 = (bf16[128,1024]{1,0:T(8,128)(2,1)S(1)}, bf16[128,1024]{1,0:T(8,128)(2,1)S(1)}, u32[]{:S(2)}, u32[]{:S(2)}) collective-permute-start(bf16[128,1024]{1,0:T(8,128)(2,1)S(1)} %get-tuple-element.22), channel_id=1, source_target_pairs={{0,1},{1,0},{2,3},{3,2},{4,5},{5,4},{6,7},{7,6},{8,9},{9,8},{10,11... | collective-permute-start | bytes 786440 | tf_op jit(solution)/shard_map/ppermute | solution.py:371
  17.0 14.4 %collective-permute-start.7 = (bf16[128,1024]{1,0:T(8,128)(2,1)S(1)}, bf16[128,1024]{1,0:T(8,128)(2,1)S(1)}, u32[]{:S(2)}, u32[]{:S(2)}) collective-permute-start(bf16[128,1024]{1,0:T(8,128)(2,1)S(1)} %get-tuple-element.22), channel_id=1, source_target_pairs={{0,2},{1,3},{2,0},{3,1},{4,6},{5,7},{6,4},{7,5},{8,10},{9,11},{10,... | collective-permute-start | bytes 786440 | tf_op jit(solution)/shard_map/ppermute | solution.py:371
  20.6 13.4 %collective-permute-start.8 = (bf16[128,1024]{1,0:T(8,128)(2,1)S(1)}, bf16[128,1024]{1,0:T(8,128)(2,1)S(1)}, u32[]{:S(2)}, u32[]{:S(2)}) collective-permute-start(bf16[128,1024]{1,0:T(8,128)(2,1)S(1)} %get-tuple-element.22), channel_id=1, source_target_pairs={{0,3},{1,2},{2,1},{3,0},{4,7},{5,6},{6,5},{7,4},{8,11},{9,10},{10,... | collective-permute-start | bytes 786440 | tf_op jit(solution)/shard_map/ppermute | solution.py:371
  40.9 65.3 %all-to-all-start.1 = ((bf16[32,64,1152]{2,1,0:T(8,128)(2,1)}), bf16[32,64,1152]{2,1,0:T(8,128)(2,1)}, u32[]{:S(2)}, u32[]{:S(2)}) async-start(bf16[32,64,1152]{2,1,0:T(8,128)(2,1)} %bitcast.39), calls=%async_computation.1 | async-start | bytes 9437184 | tf_op jit(solution)/shard_map/all_to_all | solution.py:379
  51.3 8.5 %copy-start.5 = (bf16[32,16,1152]{2,1,0:T(8,128)(2,1)}, bf16[32,16,1152]{2,1,0:T(8,128)(2,1)S(1)}, u32[]{:S(2)}) copy-start(bf16[32,16,1152]{2,1,0:T(8,128)(2,1)S(1)} %get-tuple-element.16.refs_0_) | copy-start | bytes 3538948
  51.3 27.2 %collective-permute-start = (bf16[32,16,1152]{2,1,0:T(8,128)(2,1)S(1)}, bf16[32,16,1152]{2,1,0:T(8,128)(2,1)S(1)}, u32[]{:S(2)}, u32[]{:S(2)}) collective-permute-start(bf16[32,16,1152]{2,1,0:T(8,128)(2,1)S(1)} %get-tuple-element.16.refs_0_), channel_id=1, source_target_pairs={{0,1},{1,0},{2,3},{3,2},{4,5},{5,4},{6,7},{7,6},{8,9},{9,8},{10,11... | collective-permute-start | bytes 3538952 | tf_op jit(solution)/shard_map/ppermute | solution.py:371
  51.3 52.5 %collective-permute-start.1 = (bf16[32,16,1152]{2,1,0:T(8,128)(2,1)}, bf16[32,16,1152]{2,1,0:T(8,128)(2,1)S(1)}, u32[]{:S(2)}, u32[]{:S(2)}) collective-permute-start(bf16[32,16,1152]{2,1,0:T(8,128)(2,1)} %get-tuple-element.15), channel_id=1, source_target_pairs={{0,2},{1,3},{2,0},{3,1},{4,6},{5,7},{6,4},{7,5},{8,10},{9,11},{10,... | collective-permute-start | bytes 3538952 | tf_op jit(solution)/shard_map/ppermute | solution.py:371
  52.8 53.4 %collective-permute-start.2 = (bf16[32,16,1152]{2,1,0:T(8,128)(2,1)}, bf16[32,16,1152]{2,1,0:T(8,128)(2,1)}, u32[]{:S(2)}, u32[]{:S(2)}) collective-permute-start(bf16[32,16,1152]{2,1,0:T(8,128)(2,1)} %get-tuple-element.15), channel_id=1, source_target_pairs={{0,3},{1,2},{2,1},{3,0},{4,7},{5,6},{6,5},{7,4},{8,11},{9,10},{10,... | collective-permute-start | bytes 3538952 | tf_op jit(solution)/shard_map/ppermute | solution.py:371
  78.5 27.7 %copy-start.11 = (bf16[32,16,1152]{2,1,0:T(8,128)(2,1)}, bf16[32,16,1152]{2,1,0:T(8,128)(2,1)S(1)}, u32[]{:S(2)}) copy-start(bf16[32,16,1152]{2,1,0:T(8,128)(2,1)S(1)} %collective-permute-done.refs_1_) | copy-start | bytes 3538948
  103.8 2.4 copy-start.12
  140.2 69.5 %all-to-all-start.3 = ((bf16[32,64,1152]{2,1,0:T(8,128)(2,1)}), bf16[32,64,1152]{2,1,0:T(8,128)(2,1)}, u32[]{:S(2)}, u32[]{:S(2)}) async-start(bf16[32,64,1152]{2,1,0:T(8,128)(2,1)} %bitcast.44), calls=%async_computation.3 | async-start | bytes 9437184 | tf_op jit(solution)/shard_map/all_to_all | solution.py:379
  149.0 29.0 %collective-permute-start.10 = (bf16[32,16,1152]{2,1,0:T(8,128)(2,1)}, bf16[32,16,1152]{2,1,0:T(8,128)(2,1)S(1)}, u32[]{:S(2)}, u32[]{:S(2)}) collective-permute-start(bf16[32,16,1152]{2,1,0:T(8,128)(2,1)} %get-tuple-element.12), channel_id=1, source_target_pairs={{0,2},{1,3},{2,0},{3,1},{4,6},{5,7},{6,4},{7,5},{8,10},{9,11},{10,... | collective-permute-start | bytes 3538952 | tf_op jit(solution)/shard_map/ppermute | solution.py:371
  149.3 54.5 %collective-permute-start.11 = (bf16[32,16,1152]{2,1,0:T(8,128)(2,1)}, bf16[32,16,1152]{2,1,0:T(8,128)(2,1)S(1)}, u32[]{:S(2)}, u32[]{:S(2)}) collective-permute-start(bf16[32,16,1152]{2,1,0:T(8,128)(2,1)} %get-tuple-element.13), channel_id=1, source_target_pairs={{0,3},{1,2},{2,1},{3,0},{4,7},{5,6},{6,5},{7,4},{8,11},{9,10},{10,... | collective-permute-start | bytes 3538952 | tf_op jit(solution)/shard_map/ppermute | solution.py:371
  151.5 52.3 %collective-permute-start.9 = (bf16[32,16,1152]{2,1,0:T(8,128)(2,1)}, bf16[32,16,1152]{2,1,0:T(8,128)(2,1)S(1)}, u32[]{:S(2)}, u32[]{:S(2)}) collective-permute-start(bf16[32,16,1152]{2,1,0:T(8,128)(2,1)} %get-tuple-element.11), channel_id=1, source_target_pairs={{0,1},{1,0},{2,3},{3,2},{4,5},{5,4},{6,7},{7,6},{8,9},{9,8},{10,11... | collective-permute-start | bytes 3538952 | tf_op jit(solution)/shard_map/ppermute | solution.py:371
  178.0 25.9 %copy-start.1 = (bf16[32,16,1152]{2,1,0:T(8,128)(2,1)}, bf16[32,16,1152]{2,1,0:T(8,128)(2,1)S(1)}, u32[]{:S(2)}) copy-start(bf16[32,16,1152]{2,1,0:T(8,128)(2,1)S(1)} %collective-permute-done.10.c_ref) | copy-start | bytes 3538948
  203.9 1.0 copy-start.2
  203.9 1.4 copy-start.3
  209.7 35.8 %all-to-all-start.2 = ((bf16[32,32,1152]{2,1,0:T(8,128)(2,1)}), bf16[32,32,1152]{2,1,0:T(8,128)(2,1)S(1)}, u32[]{:S(2)}, u32[]{:S(2)}) async-start(bf16[32,32,1152]{2,1,0:T(8,128)(2,1)} %bitcast.40), calls=%async_computation.2 | async-start | bytes 4718592 | tf_op jit(solution)/shard_map/all_to_all | solution.py:379
  224.6 20.9 %collective-permute-start.12 = (bf16[128,1024]{1,0:T(8,128)(2,1)}, bf16[128,1024]{1,0:T(8,128)(2,1)S(1)}, u32[]{:S(2)}, u32[]{:S(2)}) collective-permute-start(bf16[128,1024]{1,0:T(8,128)(2,1)} %get-tuple-element.19), channel_id=1, source_target_pairs={{0,1},{1,0},{2,3},{3,2},{4,5},{5,4},{6,7},{7,6},{8,9},{9,8},{10,11... | collective-permute-start | bytes 786440 | tf_op jit(solution)/shard_map/ppermute | solution.py:371
  224.6 20.9 %collective-permute-start.13 = (bf16[128,1024]{1,0:T(8,128)(2,1)}, bf16[128,1024]{1,0:T(8,128)(2,1)S(1)}, u32[]{:S(2)}, u32[]{:S(2)}) collective-permute-start(bf16[128,1024]{1,0:T(8,128)(2,1)} %get-tuple-element.18), channel_id=1, source_target_pairs={{0,2},{1,3},{2,0},{3,1},{4,6},{5,7},{6,4},{7,5},{8,10},{9,11},{10,... | collective-permute-start | bytes 786440 | tf_op jit(solution)/shard_map/ppermute | solution.py:371
  228.0 17.5 %collective-permute-start.14 = (bf16[128,1024]{1,0:T(8,128)(2,1)S(1)}, bf16[128,1024]{1,0:T(8,128)(2,1)S(1)}, u32[]{:S(2)}, u32[]{:S(2)}) collective-permute-start(bf16[128,1024]{1,0:T(8,128)(2,1)S(1)} %get-tuple-element.17), channel_id=1, source_target_pairs={{0,3},{1,2},{2,1},{3,0},{4,7},{5,6},{6,5},{7,4},{8,11},{9,10},{10,... | collective-permute-start | bytes 786440 | tf_op jit(solution)/shard_map/ppermute | solution.py:371
  245.5 1.4 copy-start
  245.5 1.5 copy-start.6
  245.5 1.6 copy-start.7
  245.5 1.6 copy-start.8

commit v3 on v2

--- a/solution.py
+++ b/solution.py
@@ -1,5 +1,3 @@
-import functools
-
 import jax
 import jax.numpy as jnp
 from jax import lax
@@ -14,6 +12,7 @@
 PIECES = 8
 TILE = MAIN * PIECES
 RING = 4
+ORDER = (2, 1, 3, 0)
 
 
 def split_matrix():
@@ -141,6 +140,7 @@
             bytes_accessed=2 * experts * MAIN * width,
             transcendentals=0,
         ),
+        compiler_params=pltpu.CompilerParams(vmem_limit_bytes=12 * 1024 * 1024),
         name="late_dispatch",
     )(pair, ids_t, tokens)
 
@@ -173,103 +173,124 @@
             bytes_accessed=2 * ring * chunks * MAIN * width,
             transcendentals=0,
         ),
+        compiler_params=pltpu.CompilerParams(vmem_limit_bytes=12 * 1024 * 1024),
         name="early_dispatch",
     )(pair, ids_t, tokens)
 
 
-def ffn_kernel(*refs):
-    late_in, (early_in, gate_ref, up_ref, down_ref) = refs[:RING], refs[RING : RING + 4]
-    late_out, early_out, rows_ref = refs[RING + 4 : 2 * RING + 4], refs[-2], refs[-1]
-    chunks, _, width = late_in[0].shape
-    half = width * MAIN // CAP
+def unpack_chunks(block, rows_ref, matrix):
+    chunks, _, width = block.shape
+    half = rows_ref.shape[1]
     main = chunks * MAIN
-    step = pl.program_id(0)
+    rows_ref[:main, :] = block[:, :, :half].reshape(main, half)
+    rows_ref[main:, :] = pieces_to_rows(block[:, :, half:].reshape(main, width - half), matrix)
+
+
+def pack_chunks(value, matrix):
+    half = value.shape[1]
+    chunks = value.shape[0] // CAP
+    main = chunks * MAIN
+    pieces = rows_to_pieces(value[main:], matrix).reshape(chunks, MAIN, half // PIECES)
+    return value[:main].reshape(chunks, MAIN, half), pieces
+
+
+def first_ffn_kernel(late_ref, gate_ref, up_ref, gate_out, up_out, rows_ref):
+    half = rows_ref.shape[1]
+    unpack_chunks(late_ref[...], rows_ref, split_matrix())
+    rows = rows_ref[...]
+    gate_out[...] = exact_dot(rows, gate_ref[0, :half, :])
+    up_out[...] = exact_dot(rows, up_ref[0, :half, :])
+
+
+def first_ffn(late, w_gate, w_up):
+    chunks, _, _ = late.shape
+    model, hidden = w_gate.shape[1:]
+    rows = chunks * CAP
+    half = model // 2
+    on_chip = pl.BlockSpec(memory_space=pltpu.VMEM)
+    out = jax.ShapeDtypeStruct((rows, hidden), jnp.float32)
+    return pl.pallas_call(
+        first_ffn_kernel,
+        in_specs=[on_chip] * 3,
+        out_specs=[on_chip] * 2,
+        out_shape=[out, out],
+        scratch_shapes=[pltpu.VMEM((rows, half), jnp.bfloat16)],
+        cost_estimate=pl.CostEstimate(
+            flops=4 * rows * half * hidden, bytes_accessed=8 * rows * hidden, transcendentals=0
+        ),
+        compiler_params=pltpu.CompilerParams(vmem_limit_bytes=12 * 1024 * 1024),
+        name="first_ffn",
+    )(late, w_gate, w_up)
+
+
+def second_ffn_kernel(early_ref, gate_in, up_in, gate_ref, up_ref, down_ref, *refs):
+    late_out, early_out, rows_ref = refs[-3:]
+    half = rows_ref.shape[1]
     matrix = split_matrix()
-
-    def unpack(block, at):
-        rows_ref[:main, at : at + half] = block[:, :, :half].reshape(main, half)
-        rows_ref[main:, at : at + half] = pieces_to_rows(
-            block[:, :, half:].reshape(main, width - half), matrix
-        )
-
-    def pack(value, ref, *index):
-        ref[(slice(None), *index, slice(None), slice(0, half))] = value[:main].reshape(
-            chunks, MAIN, half
-        )
-        ref[(slice(None), *index, slice(None), slice(half, None))] = rows_to_pieces(
-            value[main:], matrix
-        ).reshape(chunks, MAIN, width - half)
-
-    for j in range(RING):
-
-        @pl.when(step == j)
-        def _(j=j):
-            unpack(late_in[j][...], 0)
-
-    unpack(early_in[:, 0], half)
+    unpack_chunks(early_ref[:, 0], rows_ref, matrix)
     rows = rows_ref[...]
-    gate = exact_dot(rows, gate_ref[0])
-    up = exact_dot(rows, up_ref[0])
+    gate = gate_in[...] + exact_dot(rows, gate_ref[0, half:, :])
+    up = up_in[...] + exact_dot(rows, up_ref[0, half:, :])
     hidden = (gate / (1.0 + jnp.exp(-gate)) * up).astype(jnp.bfloat16)
-    half_out = exact_dot(hidden, down_ref[0]).astype(jnp.bfloat16)
-    for j in range(RING):
-
-        @pl.when(step == j)
-        def _(j=j):
-            pack(half_out[:, :half], late_out[j])
-
-    pack(half_out[:, half:], early_out, 0)
-
-
-def half_ffn(late, early, w_gate, w_up, w_down):
-    chunks, _, width = late[0].shape
+    value = exact_dot(hidden, down_ref[0, :, :half]).astype(jnp.bfloat16)
+    main, pieces = pack_chunks(value, matrix)
+    late_out[:, :, :half] = main
+    late_out[:, :, half:] = pieces
+    value = exact_dot(hidden, down_ref[0, :, half:]).astype(jnp.bfloat16)
+    main, pieces = pack_chunks(value, matrix)
+    early_out[:, 0, :, :half] = main
+    early_out[:, 0, :, half:] = pieces
+
+
+def second_ffn(j, early, gate, up, w_gate, w_up, w_down, early_out):
+    chunks, _, _, width = early.shape
     model, hidden = w_gate.shape[1:]
-    rows = RING * chunks * CAP
-    once = pl.Buffered(1)
-    late_spec = pl.BlockSpec(late[0].shape, lambda i: (0, 0, 0), pipeline_mode=once)
-    early_spec = pl.BlockSpec((chunks, 1, MAIN, width), lambda i: (0, i, 0, 0))
-    weights = [
-        pl.BlockSpec(w.shape, lambda i: (0, 0, 0), pipeline_mode=once)
-        for w in (w_gate, w_up, w_down)
-    ]
-    late_shape = jax.ShapeDtypeStruct(late[0].shape, jnp.bfloat16)
-    *late_out, early_out = pl.pallas_call(
-        ffn_kernel,
-        grid=(RING,),
-        in_specs=[late_spec] * RING + [early_spec] + weights,
-        out_specs=[late_spec] * RING + [early_spec],
-        out_shape=[late_shape] * RING + [jax.ShapeDtypeStruct(early.shape, jnp.bfloat16)],
-        scratch_shapes=[pltpu.VMEM((chunks * CAP, model), jnp.bfloat16)],
-        cost_estimate=pl.CostEstimate(
-            flops=6 * rows * model * hidden,
-            bytes_accessed=4 * rows * model + 6 * model * hidden,
+    rows = chunks * CAP
+    half = model // 2
+    on_chip = pl.BlockSpec(memory_space=pltpu.VMEM)
+    block = pl.BlockSpec((chunks, 1, MAIN, width), lambda i: (0, j, 0, 0))
+    held = [] if early_out is None else [early_out]
+    return pl.pallas_call(
+        second_ffn_kernel,
+        grid=(1,),
+        in_specs=[block] + [on_chip] * 5 + [pl.BlockSpec(memory_space=pl.ANY)] * len(held),
+        out_specs=[on_chip, block],
+        out_shape=[
+            jax.ShapeDtypeStruct((chunks, MAIN, width), jnp.bfloat16),
+            pltpu.HBM(early.shape, jnp.bfloat16),
+        ],
+        input_output_aliases={6: 1} if held else {},
+        scratch_shapes=[pltpu.VMEM((rows, half), jnp.bfloat16)],
+        cost_estimate=pl.CostEstimate(
+            flops=2 * rows * model * hidden + 4 * rows * half * hidden,
+            bytes_accessed=4 * rows * half + 8 * rows * hidden,
             transcendentals=rows * hidden,
         ),
-        compiler_params=pltpu.CompilerParams(vmem_limit_bytes=56 * 1024 * 1024),
-        name="half_ffn",
-    )(*late, early, w_gate, w_up, w_down)
-    return late_out, early_out
+        compiler_params=pltpu.CompilerParams(vmem_limit_bytes=20 * 1024 * 1024),
+        name="second_ffn",
+    )(early, gate, up, w_gate, w_up, w_down, *held)
 
 
 def sum_halves_kernel(a_ref, b_ref, c_ref, d_ref, out_ref):
     for r, (first, second) in enumerate(((a_ref, b_ref), (c_ref, d_ref))):
-        both = first[...].astype(jnp.float32) + second[...].astype(jnp.float32)
-        out_ref[:, r] = both.astype(jnp.bfloat16)
+        for i in range(0, first.shape[0], 8):
+            both = first[i : i + 8].astype(jnp.float32) + second[i : i + 8].astype(jnp.float32)
+            out_ref[i : i + 8, r] = both.astype(jnp.bfloat16)
 
 
 def sum_halves(arrays):
     chunks, _, width = arrays[0].shape
-    block = 8
+    on_chip = pl.BlockSpec(memory_space=pltpu.VMEM)
     return pl.pallas_call(
         sum_halves_kernel,
-        grid=(chunks // block,),
-        in_specs=[pl.BlockSpec((block, MAIN, width), lambda i: (i, 0, 0))] * RING,
-        out_specs=pl.BlockSpec((block, 2, MAIN, width), lambda i: (i, 0, 0, 0)),
+        in_specs=[on_chip] * RING,
+        out_specs=on_chip,
         out_shape=jax.ShapeDtypeStruct((chunks, 2, MAIN, width), jnp.bfloat16),
         cost_estimate=pl.CostEstimate(
             flops=4 * chunks * MAIN * width, bytes_accessed=12 * chunks * MAIN * width,
             transcendentals=0,
         ),
+        compiler_params=pltpu.CompilerParams(vmem_limit_bytes=12 * 1024 * 1024),
         name="sum_halves",
     )(*arrays)
 
@@ -304,65 +325,52 @@
             bytes_accessed=2 * ring * chunks * MAIN * width,
             transcendentals=0,
         ),
+        compiler_params=pltpu.CompilerParams(vmem_limit_bytes=12 * 1024 * 1024),
         name="early_combine",
     )(pair, ids_t, gates_t, rows)
 
 
 def final_kernel(pair_ref, ids_ref, gates_ref, rows_ref, *refs):
-    parts, (out_ref, slot_ref, weight_ref, acc_ref) = refs[:RING], refs[RING:]
-    block = rows_ref.shape[0]
-    half = acc_ref.shape[1]
-    step = pl.program_id(0)
-
-    @pl.when(step == 0)
-    def _():
-        expert = near_first(*slot_ref.shape, pair_ref[0])
-        slot, weight = slots_of(ids_ref[...], expert, gates_ref[...])
-        slot_ref[...] = slot
-        weight_ref[...] = weight
-        acc_ref[...] = jnp.zeros_like(acc_ref)
-
-    here = pl.ds(pl.multiple_of(step * block, block), block)
-    main = rows_ref[:, :, :half].reshape(block * MAIN, half)
-    pieces = rows_ref[:, :, half:].reshape(block * MAIN, half // PIECES)
-    acc_ref[...] += combine_rows(slot_ref[here, :], weight_ref[here, :], main, pieces)
-
-    @pl.when(step == pl.num_programs(0) - 1)
-    def _():
-        out_ref[:, :half] = acc_ref[...].astype(jnp.bfloat16)
-        total = parts[0][...].astype(jnp.float32)
-        for part in parts[1:]:
-            total += part[...].astype(jnp.float32)
-        out_ref[:, half:] = total.astype(jnp.bfloat16)
+    parts, (out_ref, slot_ref, weight_ref) = refs[:RING], refs[RING:]
+    experts = rows_ref.shape[0]
+    half = parts[0].shape[1]
+    block = 16
+    expert = near_first(*slot_ref.shape, pair_ref[0])
+    slot, weight = slots_of(ids_ref[...], expert, gates_ref[...])
+    slot_ref[...] = slot
+    weight_ref[...] = weight
+    total = jnp.zeros((slot.shape[1], half), jnp.float32)
+    for first in range(0, experts, block):
+        here = slice(first, first + block)
+        main = rows_ref[here, :, :half].reshape(block * MAIN, half)
+        pieces = rows_ref[here, :, half:].reshape(block * MAIN, half // PIECES)
+        total += combine_rows(slot_ref[here, :], weight_ref[here, :], main, pieces)
+    out_ref[:, :half] = total.astype(jnp.bfloat16)
+    total = parts[0][...].astype(jnp.float32)
+    for part in parts[1:]:
+        total += part[...].astype(jnp.float32)
+    out_ref[:, half:] = total.astype(jnp.bfloat16)
 
 
 def final_combine(pair, ids_t, gates_t, rows, parts):
     experts, _, width = rows.shape
     count, half = parts[0].shape
-    block = 16
-    whole = lambda i: (0, 0)
+    on_chip = pl.BlockSpec(memory_space=pltpu.VMEM)
     return pl.pallas_call(
         final_kernel,
-        grid=(experts // block,),
-        in_specs=[
-            pl.BlockSpec(memory_space=pltpu.SMEM),
-            pl.BlockSpec(ids_t.shape, whole),
-            pl.BlockSpec(gates_t.shape, whole),
-            pl.BlockSpec((block, MAIN, width), lambda i: (i, 0, 0)),
-        ]
-        + [pl.BlockSpec((count, half), whole)] * RING,
-        out_specs=pl.BlockSpec((count, 2 * half), whole),
+        in_specs=[pl.BlockSpec(memory_space=pltpu.SMEM)] + [on_chip] * (3 + RING),
+        out_specs=on_chip,
         out_shape=jax.ShapeDtypeStruct((count, 2 * half), jnp.bfloat16),
         scratch_shapes=[
             pltpu.VMEM((experts, count), jnp.float32),
             pltpu.VMEM((experts, count), jnp.float32),
-            pltpu.VMEM((count, half), jnp.float32),
         ],
         cost_estimate=pl.CostEstimate(
             flops=2 * experts * CAP * count * half,
             bytes_accessed=2 * experts * MAIN * width,
             transcendentals=0,
         ),
+        compiler_params=pltpu.CompilerParams(vmem_limit_bytes=16 * 1024 * 1024),
         name="final_combine",
     )(pair, ids_t, gates_t, rows, *parts)
 
@@ -402,10 +410,13 @@
     early = early.reshape(chunks, RING, MAIN, width)
 
     late_in = (near, across(near, 1), across(far, 2), across(far, 3))
-    late_out, early_out = half_ffn(late_in, early, w_gate, w_up, w_down)
+    first = {j: first_ffn(late_in[j], w_gate, w_up) for j in (0, 1, 3, 2)}
+    early_out, late_back = None, [None] * RING
+    for j in ORDER:
+        late_out, early_out = second_ffn(j, early, *first[j], w_gate, w_up, w_down, early_out)
+        late_back[j] = across(late_out, j) if j else late_out
 
     early_out = plane_exchange(early_out.reshape(chunks, RING * MAIN, width))
-    late_back = [late_out[0]] + [across(late_out[j], j) for j in range(1, RING)]
     late_back = plane_exchange(sum_halves(late_back).reshape(chunks, 2 * MAIN, width))
     partial = early_combine(
         pair, ids_ring, gates_ring, early_out.reshape(chunks, RING, MAIN, width)
@@ -420,6 +431,7 @@
     ring = Mesh(mesh.devices.reshape(mesh.devices.shape[0], -1, RING), AXES)
     rows = P(AXES, None)
     weights = P(AXES, None, None)
+
     return jax.shard_map(
         per_device,
         mesh=ring,

time: 255 us -> 262 us (1.027)
  local copies, waits for them, and re-layouts: 15.6 us -> 35.8 us
  waiting for transfers between devices: 123 us -> 114 us
    unnamed x28 -> x64, local copies, waits for them, and re-layouts: 12.3 us -> 33.2 us
    ppermute x15, waiting for transfers between devices: 106 us -> 91.2 us  [across(): return lax.ppermute(array, 'y', [(y, y ^ j) for y in range(RING)])]
    all_to_all x4, waiting for transfers between devices: 16.4 us -> 22.8 us  [plane_exchange(): return lax.all_to_all(array, PLANE, split_axis=0, concat_axis=0, tiled=True)]
    pallas_call x3 -> x10, Pallas kernels: 43.3 us -> 45.8 us  [the longest x4 28.3 us: second_ffn(): pl.pallas_call(second_ffn_kernel, grid=(1,), in_specs=[block] + [on_chip]...]
  transfers between devices with their start and end apart: 19 -> 19, of which waited for: 9 -> 9; matrix products, arithmetic and copies ran while one was open for 6% -> 4% of each run, Pallas kernels for 6% -> 9%
where the time goes in v3:
time: 262 us; the launch traced here: 259 us
  waiting for transfers between devices  114 us (44%)
  Pallas kernels  56.7 us (22%)
  starting transfers between devices  51.8 us (20%)
  local copies, waits for them, and re-layouts  35.8 us (14%)
    ppermute x15, waiting for transfers between devices, across(): return lax.ppermute(array, 'y', [(y, y ^ j) for y in range(RING)])  91.2 us
    unnamed x64, local copies, waits for them, and re-layouts  33.2 us
    all_to_all x4, starting transfers between devices, plane_exchange(): return lax.all_to_all(array, PLANE, split_axis=0, concat_axis=0, tiled=True)  32.3 us
    pallas_call x4, Pallas kernels, second_ffn(): pl.pallas_call(second_ffn_kernel, grid=(1,), in_specs=[block] + [on_chip]...  28.3 us
    all_to_all x4, waiting for transfers between devices, plane_exchange(): return lax.all_to_all(array, PLANE, split_axis=0, concat_axis=0, tiled=True)  22.8 us
    ppermute x15, starting transfers between devices, across(): return lax.ppermute(array, 'y', [(y, y ^ j) for y in range(RING)])  19.5 us
    pallas_call x4, Pallas kernels, first_ffn(): pl.pallas_call(first_ffn_kernel, in_specs=[on_chip] * 3, out_specs=[on_ch...  13.3 us
  transfers between devices with their start and end apart: 19, of which 9 were waited for; matrix products, arithmetic and copies ran while one was open for 4% of the time, Pallas kernels for 9%

profile of v3, /device:TPU:37, one launch (start us, length us, event | category | flops | bytes accessed | tf_op | source)
XLA Modules:
  0.0 258.5 jit_solution(13977860606931878757)
XLA Ops:
  0.0 1.0 copy-done.22
  1.0 0.7 copy-done.24
  1.7 3.2 %late_dispatch.1 = bf16[64,16,1152]{2,1,0:T(8,128)(2,1)} custom-call(s32[1]{0:T(128)} %bitcast.pair_ref, s32[6,128]{1,0:T(8,128)S(1)} %bitcast.41, bf16[128,2048]{1,0:T(8,128)(2,1)S(1)} %copy-done.22), custom_call_target="tpu_custom_call" | custom-call | flops 301989888 | bytes 2359296 | tf_op jit(solution)/shard_map/late_dispatch/pallas_call | solution.py:127
  4.9 8.4 %all-to-all-start.1 = ((bf16[32,32,1152]{2,1,0:T(8,128)(2,1)}), bf16[32,32,1152]{2,1,0:T(8,128)(2,1)S(1)}, u32[]{:S(2)}, u32[]{:S(2)}) async-start(bf16[32,32,1152]{2,1,0:T(8,128)(2,1)} %bitcast.13), calls=%async_computation.1 | async-start | bytes 4718592 | tf_op jit(solution)/shard_map/all_to_all | solution.py:387
  13.3 1.4 collective-permute-start
  14.7 2.6 %collective-permute-start.1 = (bf16[12,128]{1,0:T(8,128)(2,1)S(1)}, bf16[12,128]{1,0:T(8,128)(2,1)S(1)}, u32[]{:S(2)}, u32[]{:S(2)}) collective-permute-start(bf16[12,128]{1,0:T(8,128)(2,1)S(1)} %get-tuple-element.48), channel_id=1, source_target_pairs={{0,2},{1,3},{2,0},{3,1},{4,6},{5,7},{6,4},{7,5},{8,10},{9,11},{10,... | collective-permute-start | bytes 9224 | tf_op jit(solution)/shard_map/ppermute | solution.py:379
  17.4 2.8 %collective-permute-start.5 = (bf16[128,1024]{1,0:T(8,128)(2,1)S(1)}, bf16[128,1024]{1,0:T(8,128)(2,1)S(1)}, u32[]{:S(2)}, u32[]{:S(2)}) collective-permute-start(bf16[128,1024]{1,0:T(8,128)(2,1)S(1)} %get-tuple-element.44), channel_id=1, source_target_pairs={{0,3},{1,2},{2,1},{3,0},{4,7},{5,6},{6,5},{7,4},{8,11},{9,10},{10,... | collective-permute-start | bytes 786440 | tf_op jit(solution)/shard_map/ppermute | solution.py:379
  20.1 0.0 collective-permute-start.3
  20.1 1.3 collective-permute-start.4
  21.4 0.0 collective-permute-done.1
  21.5 4.0 %collective-permute-done.5 = bf16[128,1024]{1,0:T(8,128)(2,1)S(1)} collective-permute-done((bf16[128,1024]{1,0:T(8,128)(2,1)S(1)}, bf16[128,1024]{1,0:T(8,128)(2,1)S(1)}, u32[]{:S(2)}, u32[]{:S(2)}) %collective-permute-start.5) | collective-permute-done | bytes 262176 | tf_op jit(solution)/shard_map/ppermute | solution.py:379
  25.5 1.0 collective-permute-done.3
  26.5 5.6 %collective-permute-done.4 = bf16[128,1024]{1,0:T(8,128)(2,1)S(1)} collective-permute-done((bf16[128,1024]{1,0:T(8,128)(2,1)S(1)}, bf16[128,1024]{1,0:T(8,128)(2,1)S(1)}, u32[]{:S(2)}, u32[]{:S(2)}) %collective-permute-start.4) | collective-permute-done | bytes 262176 | tf_op jit(solution)/shard_map/ppermute | solution.py:379
  32.1 0.1 pad_maximum_fusion.tokens_ref
  32.2 3.4 %early_dispatch.1 = bf16[32,4,16,1152]{3,2,1,0:T(8,128)(2,1)S(1)} custom-call(s32[1]{0:T(128)} %bitcast.pair_ref, s32[4,6,128]{2,1,0:T(8,128)S(1)} %get-tuple-element.46.ids_ref, bf16[4,128,1024]{2,1,0:T(8,128)(2,1)S(1)} %pad_maximum_fusion.tokens_ref), custom_call_target="tpu_custom_call" | custom-call | flops 603979776 | bytes 4718592 | tf_op jit(solution)/shard_map/early_dispatch/pallas_call | solution.py:161
  35.6 2.2 copy-done.3
  37.8 3.7 %all-to-all-done.1 = bf16[32,32,1152]{2,1,0:T(8,128)(2,1)S(1)} async-done(((bf16[32,32,1152]{2,1,0:T(8,128)(2,1)}), bf16[32,32,1152]{2,1,0:T(8,128)(2,1)S(1)}, u32[]{:S(2)}, u32[]{:S(2)}) %all-to-all-start.1) | async-done | bytes 2359328 | tf_op jit(solution)/shard_map/all_to_all | solution.py:387
  41.5 6.9 %all-to-all-start = ((bf16[32,64,1152]{2,1,0:T(8,128)(2,1)}), bf16[32,64,1152]{2,1,0:T(8,128)(2,1)}, u32[]{:S(2)}, u32[]{:S(2)}) async-start(bf16[32,64,1152]{2,1,0:T(8,128)(2,1)} %bitcast.39), calls=%async_computation | async-start | bytes 9437184 | tf_op jit(solution)/shard_map/all_to_all | solution.py:387
  48.4 1.6 slice_bitcast_fusion
  50.0 2.9 %collective-permute-start.8 = (bf16[32,16,1152]{2,1,0:T(8,128)(2,1)}, bf16[32,16,1152]{2,1,0:T(8,128)(2,1)}, u32[]{:S(2)}, u32[]{:S(2)}) collective-permute-start(bf16[32,16,1152]{2,1,0:T(8,128)(2,1)} %get-tuple-element.37), channel_id=1, source_target_pairs={{0,2},{1,3},{2,0},{3,1},{4,6},{5,7},{6,4},{7,5},{8,10},{9,11},{10,... | collective-permute-start | bytes 3538952 | tf_op jit(solution)/shard_map/ppermute | solution.py:379
  52.9 0.4 collective-permute-start.7
  53.3 0.4 collective-permute-start.6
  53.7 3.1 %copy.27.gate_ref = bf16[1,2048,704]{2,1,0:T(8,128)(2,1)S(1)} copy(bf16[1,2048,704]{1,2,0:T(8,128)(2,1)} %param.9) | data formatting | bytes 5767168 | tf_op args[3]
  56.8 4.7 %copy.28.up_ref = bf16[1,2048,704]{2,1,0:T(8,128)(2,1)} copy(bf16[1,2048,704]{1,2,0:T(8,128)(2,1)} %param.10) | data formatting | bytes 5767168 | tf_op args[4]
  61.5 1.9 copy-done
  63.4 3.3 %first_ffn.4 = (f32[576,704]{1,0:T(8,128)S(1)}, f32[576,704]{1,0:T(8,128)S(1)}) custom-call(bf16[32,16,1152]{2,1,0:T(8,128)(2,1)} %get-tuple-element.38.late_ref, bf16[1,2048,704]{2,1,0:T(8,128)(2,1)S(1)} %copy.27.gate_ref, bf16[1,2048,704]{2,1,0:T(8,128)(2,1)S(1)} %copy-done), custom_call_target="tpu_custom_call" | custom-call | flops 1660944384 | bytes 3244032 | tf_op jit(solution)/shard_map/first_ffn/pallas_call | solution.py:212
  66.7 1.2 copy-done.8
  67.9 1.2 copy-done.10
  69.1 9.9 %collective-permute-done.8.late_ref = bf16[32,16,1152]{2,1,0:T(8,128)(2,1)} collective-permute-done((bf16[32,16,1152]{2,1,0:T(8,128)(2,1)}, bf16[32,16,1152]{2,1,0:T(8,128)(2,1)}, u32[]{:S(2)}, u32[]{:S(2)}) %collective-permute-start.8) | collective-permute-done | bytes 1179680 | tf_op jit(solution)/shard_map/ppermute | solution.py:379
  79.0 3.3 %first_ffn.7 = (f32[576,704]{1,0:T(8,128)S(1)}, f32[576,704]{1,0:T(8,128)S(1)}) custom-call(bf16[32,16,1152]{2,1,0:T(8,128)(2,1)} %collective-permute-done.8.late_ref, bf16[1,2048,704]{2,1,0:T(8,128)(2,1)S(1)} %copy.27.gate_ref, bf16[1,2048,704]{2,1,0:T(8,128)(2,1)S(1)} %copy-done), custom_call_target="tpu_custom_call" | custom-call | flops 1660944384 | bytes 3244032 | tf_op jit(solution)/shard_map/first_ffn/pallas_call | solution.py:212
  82.3 1.3 copy-done.4
  83.6 1.2 copy-done.6
  84.9 19.8 %collective-permute-done.7.late_ref = bf16[32,16,1152]{2,1,0:T(8,128)(2,1)} collective-permute-done((bf16[32,16,1152]{2,1,0:T(8,128)(2,1)}, bf16[32,16,1152]{2,1,0:T(8,128)(2,1)}, u32[]{:S(2)}, u32[]{:S(2)}) %collective-permute-start.7) | collective-permute-done | bytes 1179680 | tf_op jit(solution)/shard_map/ppermute | solution.py:379
  104.6 3.3 %first_ffn.6 = (f32[576,704]{1,0:T(8,128)S(1)}, f32[576,704]{1,0:T(8,128)S(1)}) custom-call(bf16[32,16,1152]{2,1,0:T(8,128)(2,1)} %collective-permute-done.7.late_ref, bf16[1,2048,704]{2,1,0:T(8,128)(2,1)S(1)} %copy.27.gate_ref, bf16[1,2048,704]{2,1,0:T(8,128)(2,1)S(1)} %copy-done), custom_call_target="tpu_custom_call" | custom-call | flops 1660944384 | bytes 3244032 | tf_op jit(solution)/shard_map/first_ffn/pallas_call | solution.py:212
  108.0 1.2 copy-done.12
  109.2 1.2 copy-done.14
  110.4 3.3 %first_ffn.5 = (f32[576,704]{1,0:T(8,128)S(1)}, f32[576,704]{1,0:T(8,128)S(1)}) custom-call(bf16[32,16,1152]{2,1,0:T(8,128)(2,1)} %collective-permute-done.6.late_ref, bf16[1,2048,704]{2,1,0:T(8,128)(2,1)S(1)} %copy.27.gate_ref, bf16[1,2048,704]{2,1,0:T(8,128)(2,1)S(1)} %copy-done), custom_call_target="tpu_custom_call" | custom-call | flops 1660944384 | bytes 3244032 | tf_op jit(solution)/shard_map/first_ffn/pallas_call | solution.py:212
  113.7 1.2 copy-done.16
  115.0 1.2 copy-done.18
  116.2 1.9 copy-done.1
  118.1 1.8 copy-done.2
  119.9 1.5 copy-done.5
  121.4 1.5 copy-done.7
  122.9 6.9 %second_ffn.4 = (bf16[32,16,1152]{2,1,0:T(8,128)(2,1)S(1)}, bf16[32,4,16,1152]{3,2,1,0:T(8,128)(2,1)}) custom-call(bf16[32,4,16,1152]{3,2,1,0:T(8,128)(2,1)} %bitcast.12.early_ref, f32[576,704]{1,0:T(8,128)S(1)} %copy-done.5, f32[576,704]{1,0:T(8,128)S(1)} %copy-done.7, bf16[1,2048,704]{2,1,0:T(8,128)(2,1)S(1)} %copy.27.gate_ref, ...), custom_call_target="tpu_custom_call" | custom-call | flops 3321888768 | bytes 5603328 | tf_op jit(solution)/shard_map/second_ffn/pallas_call | solution.py:253
  129.8 1.0 copy-done.26
  130.8 7.0 %second_ffn.5 = (bf16[32,16,1152]{2,1,0:T(8,128)(2,1)S(1)}, bf16[32,4,16,1152]{3,2,1,0:T(8,128)(2,1)}) custom-call(bf16[32,4,16,1152]{3,2,1,0:T(8,128)(2,1)} %bitcast.12.early_ref, f32[576,704]{1,0:T(8,128)S(1)} %copy-done.13, f32[576,704]{1,0:T(8,128)S(1)} %copy-done.15, bf16[1,2048,704]{2,1,0:T(8,128)(2,1)S(1)} %copy.27.gate_ref, ...), custom_call_target="tpu_custom_call", output_to_operand_aliasing={{1}: (6, {})} | custom-call | flops 3321888768 | bytes 5603328 | tf_op jit(solution)/shard_map/second_ffn/pallas_call | solution.py:253
  137.8 1.0 copy-done.28
  138.9 7.2 %second_ffn.6 = (bf16[32,16,1152]{2,1,0:T(8,128)(2,1)S(1)}, bf16[32,4,16,1152]{3,2,1,0:T(8,128)(2,1)}) custom-call(bf16[32,4,16,1152]{3,2,1,0:T(8,128)(2,1)} %bitcast.12.early_ref, f32[576,704]{1,0:T(8,128)S(1)} %copy-done.17, f32[576,704]{1,0:T(8,128)S(1)} %copy-done.19, bf16[1,2048,704]{2,1,0:T(8,128)(2,1)S(1)} %copy.27.gate_ref, ...), custom_call_target="tpu_custom_call", output_to_operand_aliasing={{1}: (6, {})} | custom-call | flops 3321888768 | bytes 5603328 | tf_op jit(solution)/shard_map/second_ffn/pallas_call | solution.py:253
  146.0 7.2 %second_ffn.7 = (bf16[32,16,1152]{2,1,0:T(8,128)(2,1)S(1)}, bf16[32,4,16,1152]{3,2,1,0:T(8,128)(2,1)}) custom-call(bf16[32,4,16,1152]{3,2,1,0:T(8,128)(2,1)} %bitcast.12.early_ref, f32[576,704]{1,0:T(8,128)S(1)} %copy-done.9, f32[576,704]{1,0:T(8,128)S(1)} %copy-done.11, bf16[1,2048,704]{2,1,0:T(8,128)(2,1)S(1)} %copy.27.gate_ref, ...), custom_call_target="tpu_custom_call", output_to_operand_aliasing={{1}: (6, {})} | custom-call | flops 3321888768 | bytes 5603328 | tf_op jit(solution)/shard_map/second_ffn/pallas_call | solution.py:253
  153.2 1.1 copy-done.20
  154.3 8.4 %all-to-all-start.3 = ((bf16[32,64,1152]{2,1,0:T(8,128)(2,1)}), bf16[32,64,1152]{2,1,0:T(8,128)(2,1)}, u32[]{:S(2)}, u32[]{:S(2)}) async-start(bf16[32,64,1152]{2,1,0:T(8,128)(2,1)} %bitcast.43), calls=%async_computation.3 | async-start | bytes 9437184 | tf_op jit(solution)/shard_map/all_to_all | solution.py:387
  162.8 0.1 collective-permute-start.11
  162.9 1.2 collective-permute-start.9
  164.1 2.6 %collective-permute-start.10 = (bf16[32,16,1152]{2,1,0:T(8,128)(2,1)S(1)}, bf16[32,16,1152]{2,1,0:T(8,128)(2,1)S(1)}, u32[]{:S(2)}, u32[]{:S(2)}) collective-permute-start(bf16[32,16,1152]{2,1,0:T(8,128)(2,1)S(1)} %copy-done.27), channel_id=1, source_target_pairs={{0,2},{1,3},{2,0},{3,1},{4,6},{5,7},{6,4},{7,5},{8,10},{9,11},{10,... | collective-permute-start | bytes 3538952 | tf_op jit(solution)/shard_map/ppermute | solution.py:379
  166.7 24.7 %collective-permute-done.11.d_ref = bf16[32,16,1152]{2,1,0:T(8,128)(2,1)S(1)} collective-permute-done((bf16[32,16,1152]{2,1,0:T(8,128)(2,1)}, bf16[32,16,1152]{2,1,0:T(8,128)(2,1)S(1)}, u32[]{:S(2)}, u32[]{:S(2)}) %collective-permute-start.11) | collective-permute-done | bytes 1179680 | tf_op jit(solution)/shard_map/ppermute | solution.py:379
  191.4 26.2 %collective-permute-done.10.c_ref = bf16[32,16,1152]{2,1,0:T(8,128)(2,1)S(1)} collective-permute-done((bf16[32,16,1152]{2,1,0:T(8,128)(2,1)S(1)}, bf16[32,16,1152]{2,1,0:T(8,128)(2,1)S(1)}, u32[]{:S(2)}, u32[]{:S(2)}) %collective-permute-start.10) | collective-permute-done | bytes 1179680 | tf_op jit(solution)/shard_map/ppermute | solution.py:379
  217.6 2.0 sum_halves.1
  219.5 8.5 %all-to-all-start.2 = ((bf16[32,32,1152]{2,1,0:T(8,128)(2,1)}), bf16[32,32,1152]{2,1,0:T(8,128)(2,1)S(1)}, u32[]{:S(2)}, u32[]{:S(2)}) async-start(bf16[32,32,1152]{2,1,0:T(8,128)(2,1)} %bitcast.17), calls=%async_computation.2 | async-start | bytes 4718592 | tf_op jit(solution)/shard_map/all_to_all | solution.py:387
  228.1 4.4 %early_combine.1 = bf16[4,128,1024]{2,1,0:T(8,128)(2,1)S(1)} custom-call(s32[1]{0:T(128)} %bitcast.pair_ref, s32[4,6,128]{2,1,0:T(8,128)S(1)} %get-tuple-element.46.ids_ref, f32[4,6,128]{2,1,0:T(8,128)S(1)} %get-tuple-element.45.gates_ref, bf16[32,4,16,1152]{3,2,1,0:T(8,128)(2,1)} %bitcast.20.rows_ref), custom_call_target="tpu_custom_call" | custom-call | flops 603979776 | bytes 4718592 | tf_op jit(solution)/shard_map/early_combine/pallas_call | solution.py:312
  232.5 0.9 slice_bitcast_fusion.2
  233.4 1.3 collective-permute-start.13
  234.6 2.6 collective-permute-start.14
  237.2 19.0 %all-to-all-done.2 = bf16[32,32,1152]{2,1,0:T(8,128)(2,1)S(1)} async-done(((bf16[32,32,1152]{2,1,0:T(8,128)(2,1)}), bf16[32,32,1152]{2,1,0:T(8,128)(2,1)S(1)}, u32[]{:S(2)}, u32[]{:S(2)}) %all-to-all-start.2) | async-done | bytes 2359328 | tf_op jit(solution)/shard_map/all_to_all | solution.py:387
  256.3 2.3 final_combine.1
  (60 shorter events, 0.2 us)
Async XLA Ops:
  0.0 1.0 copy-start.22
  1.0 0.7 copy-start.24
  4.9 8.4 %copy-start.25 = (s32[128,6]{0,1:T(8,128)S(1)}, s32[128,6]{0,1:T(8,128)}, u32[]{:S(2)}) copy-start(s32[128,6]{0,1:T(8,128)} %param.7) | copy-start | bytes 9220
  4.9 8.4 %copy-start.30 = (bf16[128,6]{0,1:T(8,128)(2,1)S(1)}, bf16[128,6]{0,1:T(8,128)(2,1)}, u32[]{:S(2)}) copy-start(bf16[128,6]{0,1:T(8,128)(2,1)} %param.8) | copy-start | bytes 4612
  4.9 12.5 %copy-start.23 = (bf16[128,2048]{1,0:T(8,128)(2,1)S(1)}, bf16[128,2048]{1,0:T(8,128)(2,1)}, u32[]{:S(2)}) copy-start(bf16[128,2048]{1,0:T(8,128)(2,1)} %tokens_ref.1) | copy-start | bytes 1572868
  4.9 36.6 %all-to-all-start.1 = ((bf16[32,32,1152]{2,1,0:T(8,128)(2,1)}), bf16[32,32,1152]{2,1,0:T(8,128)(2,1)S(1)}, u32[]{:S(2)}, u32[]{:S(2)}) async-start(bf16[32,32,1152]{2,1,0:T(8,128)(2,1)} %bitcast.13), calls=%async_computation.1 | async-start | bytes 4718592 | tf_op jit(solution)/shard_map/all_to_all | solution.py:387
  13.3 6.8 %collective-permute-start = (bf16[12,128]{1,0:T(8,128)(2,1)S(1)}, bf16[12,128]{1,0:T(8,128)(2,1)S(1)}, u32[]{:S(2)}, u32[]{:S(2)}) collective-permute-start(bf16[12,128]{1,0:T(8,128)(2,1)S(1)} %get-tuple-element.48), channel_id=1, source_target_pairs={{0,1},{1,0},{2,3},{3,2},{4,5},{5,4},{6,7},{7,6},{8,9},{9,8},{10,11... | collective-permute-start | bytes 9224 | tf_op jit(solution)/shard_map/ppermute | solution.py:379
  14.7 6.7 %collective-permute-start.1 = (bf16[12,128]{1,0:T(8,128)(2,1)S(1)}, bf16[12,128]{1,0:T(8,128)(2,1)S(1)}, u32[]{:S(2)}, u32[]{:S(2)}) collective-permute-start(bf16[12,128]{1,0:T(8,128)(2,1)S(1)} %get-tuple-element.48), channel_id=1, source_target_pairs={{0,2},{1,3},{2,0},{3,1},{4,6},{5,7},{6,4},{7,5},{8,10},{9,11},{10,... | collective-permute-start | bytes 9224 | tf_op jit(solution)/shard_map/ppermute | solution.py:379
  17.3 4.1 %collective-permute-start.2 = (bf16[12,128]{1,0:T(8,128)(2,1)S(1)}, bf16[12,128]{1,0:T(8,128)(2,1)S(1)}, u32[]{:S(2)}, u32[]{:S(2)}) collective-permute-start(bf16[12,128]{1,0:T(8,128)(2,1)S(1)} %get-tuple-element.48), channel_id=1, source_target_pairs={{0,3},{1,2},{2,1},{3,0},{4,7},{5,6},{6,5},{7,4},{8,11},{9,10},{10,... | collective-permute-start | bytes 9224 | tf_op jit(solution)/shard_map/ppermute | solution.py:379
  17.4 8.1 %collective-permute-start.5 = (bf16[128,1024]{1,0:T(8,128)(2,1)S(1)}, bf16[128,1024]{1,0:T(8,128)(2,1)S(1)}, u32[]{:S(2)}, u32[]{:S(2)}) collective-permute-start(bf16[128,1024]{1,0:T(8,128)(2,1)S(1)} %get-tuple-element.44), channel_id=1, source_target_pairs={{0,3},{1,2},{2,1},{3,0},{4,7},{5,6},{6,5},{7,4},{8,11},{9,10},{10,... | collective-permute-start | bytes 786440 | tf_op jit(solution)/shard_map/ppermute | solution.py:379
  20.1 6.4 %collective-permute-start.3 = (bf16[128,1024]{1,0:T(8,128)(2,1)S(1)}, bf16[128,1024]{1,0:T(8,128)(2,1)S(1)}, u32[]{:S(2)}, u32[]{:S(2)}) collective-permute-start(bf16[128,1024]{1,0:T(8,128)(2,1)S(1)} %get-tuple-element.44), channel_id=1, source_target_pairs={{0,1},{1,0},{2,3},{3,2},{4,5},{5,4},{6,7},{7,6},{8,9},{9,8},{10,11... | collective-permute-start | bytes 786440 | tf_op jit(solution)/shard_map/ppermute | solution.py:379
  20.1 11.9 %collective-permute-start.4 = (bf16[128,1024]{1,0:T(8,128)(2,1)S(1)}, bf16[128,1024]{1,0:T(8,128)(2,1)S(1)}, u32[]{:S(2)}, u32[]{:S(2)}) collective-permute-start(bf16[128,1024]{1,0:T(8,128)(2,1)S(1)} %get-tuple-element.44), channel_id=1, source_target_pairs={{0,2},{1,3},{2,0},{3,1},{4,6},{5,7},{6,4},{7,5},{8,10},{9,11},{10,... | collective-permute-start | bytes 786440 | tf_op jit(solution)/shard_map/ppermute | solution.py:379
  35.6 2.2 copy-start.3
  41.5 74.7 %all-to-all-start = ((bf16[32,64,1152]{2,1,0:T(8,128)(2,1)}), bf16[32,64,1152]{2,1,0:T(8,128)(2,1)}, u32[]{:S(2)}, u32[]{:S(2)}) async-start(bf16[32,64,1152]{2,1,0:T(8,128)(2,1)} %bitcast.39), calls=%async_computation | async-start | bytes 9437184 | tf_op jit(solution)/shard_map/all_to_all | solution.py:387
  50.0 29.0 %collective-permute-start.8 = (bf16[32,16,1152]{2,1,0:T(8,128)(2,1)}, bf16[32,16,1152]{2,1,0:T(8,128)(2,1)}, u32[]{:S(2)}, u32[]{:S(2)}) collective-permute-start(bf16[32,16,1152]{2,1,0:T(8,128)(2,1)} %get-tuple-element.37), channel_id=1, source_target_pairs={{0,2},{1,3},{2,0},{3,1},{4,6},{5,7},{6,4},{7,5},{8,10},{9,11},{10,... | collective-permute-start | bytes 3538952 | tf_op jit(solution)/shard_map/ppermute | solution.py:379
  52.9 51.7 %collective-permute-start.7 = (bf16[32,16,1152]{2,1,0:T(8,128)(2,1)}, bf16[32,16,1152]{2,1,0:T(8,128)(2,1)}, u32[]{:S(2)}, u32[]{:S(2)}) collective-permute-start(bf16[32,16,1152]{2,1,0:T(8,128)(2,1)} %get-tuple-element.38.late_ref), channel_id=1, source_target_pairs={{0,1},{1,0},{2,3},{3,2},{4,5},{5,4},{6,7},{7,6},{8,9},{9,8},{10,11... | collective-permute-start | bytes 3538952 | tf_op jit(solution)/shard_map/ppermute | solution.py:379
  53.3 57.1 %collective-permute-start.6 = (bf16[32,16,1152]{2,1,0:T(8,128)(2,1)}, bf16[32,16,1152]{2,1,0:T(8,128)(2,1)}, u32[]{:S(2)}, u32[]{:S(2)}) collective-permute-start(bf16[32,16,1152]{2,1,0:T(8,128)(2,1)} %get-tuple-element.37), channel_id=1, source_target_pairs={{0,3},{1,2},{2,1},{3,0},{4,7},{5,6},{6,5},{7,4},{8,11},{9,10},{10,... | collective-permute-start | bytes 3538952 | tf_op jit(solution)/shard_map/ppermute | solution.py:379
  61.5 1.9 copy-start
  66.7 1.2 copy-start.8
  67.9 1.2 copy-start.10
  82.3 1.3 copy-start.4
  83.6 1.2 copy-start.6
  107.9 1.2 copy-start.12
  109.2 1.2 copy-start.14
  113.7 1.3 copy-start.16
  115.0 1.2 copy-start.18
  116.2 1.9 copy-start.1
  118.1 1.8 copy-start.2
  119.9 1.5 copy-start.5
  121.4 1.5 copy-start.7
  122.9 8.0 %copy-start.13 = (f32[576,704]{1,0:T(8,128)S(1)}, f32[576,704]{1,0:T(8,128)}, u32[]{:S(2)}) copy-start(f32[576,704]{1,0:T(8,128)} %copy-done.12) | copy-start | bytes 4866052
  122.9 8.0 %copy-start.15 = (f32[576,704]{1,0:T(8,128)S(1)}, f32[576,704]{1,0:T(8,128)}, u32[]{:S(2)}) copy-start(f32[576,704]{1,0:T(8,128)} %copy-done.14) | copy-start | bytes 4866052
  129.8 1.0 copy-start.26
  130.8 8.0 %copy-start.17 = (f32[576,704]{1,0:T(8,128)S(1)}, f32[576,704]{1,0:T(8,128)}, u32[]{:S(2)}) copy-start(f32[576,704]{1,0:T(8,128)} %copy-done.16) | copy-start | bytes 4866052
  130.8 8.0 %copy-start.19 = (f32[576,704]{1,0:T(8,128)S(1)}, f32[576,704]{1,0:T(8,128)}, u32[]{:S(2)}) copy-start(f32[576,704]{1,0:T(8,128)} %copy-done.18) | copy-start | bytes 4866052
  137.8 1.0 copy-start.28
  138.9 7.2 %copy-start.9 = (f32[576,704]{1,0:T(8,128)S(1)}, f32[576,704]{1,0:T(8,128)}, u32[]{:S(2)}) copy-start(f32[576,704]{1,0:T(8,128)} %copy-done.8) | copy-start | bytes 4866052
  138.9 7.2 %copy-start.11 = (f32[576,704]{1,0:T(8,128)S(1)}, f32[576,704]{1,0:T(8,128)}, u32[]{:S(2)}) copy-start(f32[576,704]{1,0:T(8,128)} %copy-done.10) | copy-start | bytes 4866052
  146.0 7.2 %copy-start.29 = (bf16[32,16,1152]{2,1,0:T(8,128)(2,1)}, bf16[32,16,1152]{2,1,0:T(8,128)(2,1)S(1)}, u32[]{:S(2)}) copy-start(bf16[32,16,1152]{2,1,0:T(8,128)(2,1)S(1)} %get-tuple-element.35) | copy-start | bytes 3538948
  153.2 1.1 copy-start.20
  154.3 9.8 %copy-start.27 = (bf16[32,16,1152]{2,1,0:T(8,128)(2,1)S(1)}, bf16[32,16,1152]{2,1,0:T(8,128)(2,1)}, u32[]{:S(2)}) copy-start(bf16[32,16,1152]{2,1,0:T(8,128)(2,1)} %copy-done.26) | copy-start | bytes 3538948
  154.3 63.3 %copy-start.21 = (bf16[32,16,1152]{2,1,0:T(8,128)(2,1)S(1)}, bf16[32,16,1152]{2,1,0:T(8,128)(2,1)}, u32[]{:S(2)}) copy-start(bf16[32,16,1152]{2,1,0:T(8,128)(2,1)} %copy-done.20) | copy-start | bytes 3538948
  154.3 65.2 %all-to-all-start.3 = ((bf16[32,64,1152]{2,1,0:T(8,128)(2,1)}), bf16[32,64,1152]{2,1,0:T(8,128)(2,1)}, u32[]{:S(2)}, u32[]{:S(2)}) async-start(bf16[32,64,1152]{2,1,0:T(8,128)(2,1)} %bitcast.43), calls=%async_computation.3 | async-start | bytes 9437184 | tf_op jit(solution)/shard_map/all_to_all | solution.py:387
  162.8 28.6 %collective-permute-start.11 = (bf16[32,16,1152]{2,1,0:T(8,128)(2,1)}, bf16[32,16,1152]{2,1,0:T(8,128)(2,1)S(1)}, u32[]{:S(2)}, u32[]{:S(2)}) collective-permute-start(bf16[32,16,1152]{2,1,0:T(8,128)(2,1)} %copy-done.29), channel_id=1, source_target_pairs={{0,3},{1,2},{2,1},{3,0},{4,7},{5,6},{6,5},{7,4},{8,11},{9,10},{10,... | collective-permute-start | bytes 3538952 | tf_op jit(solution)/shard_map/ppermute | solution.py:379
  162.9 28.5 %collective-permute-start.9 = (bf16[32,16,1152]{2,1,0:T(8,128)(2,1)}, bf16[32,16,1152]{2,1,0:T(8,128)(2,1)S(1)}, u32[]{:S(2)}, u32[]{:S(2)}) collective-permute-start(bf16[32,16,1152]{2,1,0:T(8,128)(2,1)} %copy-done.28), channel_id=1, source_target_pairs={{0,1},{1,0},{2,3},{3,2},{4,5},{5,4},{6,7},{7,6},{8,9},{9,8},{10,11... | collective-permute-start | bytes 3538952 | tf_op jit(solution)/shard_map/ppermute | solution.py:379
  164.1 53.5 %collective-permute-start.10 = (bf16[32,16,1152]{2,1,0:T(8,128)(2,1)S(1)}, bf16[32,16,1152]{2,1,0:T(8,128)(2,1)S(1)}, u32[]{:S(2)}, u32[]{:S(2)}) collective-permute-start(bf16[32,16,1152]{2,1,0:T(8,128)(2,1)S(1)} %copy-done.27), channel_id=1, source_target_pairs={{0,2},{1,3},{2,0},{3,1},{4,6},{5,7},{6,4},{7,5},{8,10},{9,11},{10,... | collective-permute-start | bytes 3538952 | tf_op jit(solution)/shard_map/ppermute | solution.py:379
  219.5 36.7 %all-to-all-start.2 = ((bf16[32,32,1152]{2,1,0:T(8,128)(2,1)}), bf16[32,32,1152]{2,1,0:T(8,128)(2,1)S(1)}, u32[]{:S(2)}, u32[]{:S(2)}) async-start(bf16[32,32,1152]{2,1,0:T(8,128)(2,1)} %bitcast.17), calls=%async_computation.2 | async-start | bytes 4718592 | tf_op jit(solution)/shard_map/all_to_all | solution.py:387
  233.4 22.9 %collective-permute-start.12 = (bf16[128,1024]{1,0:T(8,128)(2,1)}, bf16[128,1024]{1,0:T(8,128)(2,1)S(1)}, u32[]{:S(2)}, u32[]{:S(2)}) collective-permute-start(bf16[128,1024]{1,0:T(8,128)(2,1)} %get-tuple-element.41), channel_id=1, source_target_pairs={{0,1},{1,0},{2,3},{3,2},{4,5},{5,4},{6,7},{7,6},{8,9},{9,8},{10,11... | collective-permute-start | bytes 786440 | tf_op jit(solution)/shard_map/ppermute | solution.py:379
  233.4 22.9 %collective-permute-start.13 = (bf16[128,1024]{1,0:T(8,128)(2,1)}, bf16[128,1024]{1,0:T(8,128)(2,1)S(1)}, u32[]{:S(2)}, u32[]{:S(2)}) collective-permute-start(bf16[128,1024]{1,0:T(8,128)(2,1)} %get-tuple-element.40), channel_id=1, source_target_pairs={{0,2},{1,3},{2,0},{3,1},{4,6},{5,7},{6,4},{7,5},{8,10},{9,11},{10,... | collective-permute-start | bytes 786440 | tf_op jit(solution)/shard_map/ppermute | solution.py:379
  234.6 21.6 %collective-permute-start.14 = (bf16[128,1024]{1,0:T(8,128)(2,1)}, bf16[128,1024]{1,0:T(8,128)(2,1)S(1)}, u32[]{:S(2)}, u32[]{:S(2)}) collective-permute-start(bf16[128,1024]{1,0:T(8,128)(2,1)} %get-tuple-element.39), channel_id=1, source_target_pairs={{0,3},{1,2},{2,1},{3,0},{4,7},{5,6},{6,5},{7,4},{8,11},{9,10},{10,... | collective-permute-start | bytes 786440 | tf_op jit(solution)/shard_map/ppermute | solution.py:379

commit v4 on v3

--- a/solution.py
+++ b/solution.py
@@ -12,7 +12,7 @@
 PIECES = 8
 TILE = MAIN * PIECES
 RING = 4
-ORDER = (2, 1, 3, 0)
+ORDER = (0, 1, 3, 2)
 
 
 def split_matrix():
@@ -178,97 +178,132 @@
     )(pair, ids_t, tokens)
 
 
-def unpack_chunks(block, rows_ref, matrix):
-    chunks, _, width = block.shape
-    half = rows_ref.shape[1]
+def ffn_kernel(*refs):
+    late_hbm, (early_hbm, gate_hbm, up_hbm, down_hbm) = refs[:RING], refs[RING : RING + 4]
+    late_out, early_out = refs[RING + 4 : 2 * RING + 4], refs[2 * RING + 4]
+    late_in, early_in, gate_w, up_w, down_w, late_made, early_made, in_sems, out_sems = refs[
+        2 * RING + 5 :
+    ]
+    _, chunks, _, width = late_in.shape
+    model = gate_w.shape[0]
+    half = model // 2
     main = chunks * MAIN
-    rows_ref[:main, :] = block[:, :, :half].reshape(main, half)
-    rows_ref[main:, :] = pieces_to_rows(block[:, :, half:].reshape(main, width - half), matrix)
-
-
-def pack_chunks(value, matrix):
-    half = value.shape[1]
-    chunks = value.shape[0] // CAP
-    main = chunks * MAIN
-    pieces = rows_to_pieces(value[main:], matrix).reshape(chunks, MAIN, half // PIECES)
-    return value[:main].reshape(chunks, MAIN, half), pieces
-
-
-def first_ffn_kernel(late_ref, gate_ref, up_ref, gate_out, up_out, rows_ref):
-    half = rows_ref.shape[1]
-    unpack_chunks(late_ref[...], rows_ref, split_matrix())
-    rows = rows_ref[...]
-    gate_out[...] = exact_dot(rows, gate_ref[0, :half, :])
-    up_out[...] = exact_dot(rows, up_ref[0, :half, :])
-
-
-def first_ffn(late, w_gate, w_up):
-    chunks, _, _ = late.shape
+    last = 2 * chunks
+    first, second = pl.ds(0, half), pl.ds(half, half)
+    body, tail = pl.ds(0, half), pl.ds(half, width - half)
+
+    reads = {}
+
+    def read(name, source, target):
+        reads[name] = pltpu.make_async_copy(source, target, in_sems.at[len(reads)])
+        reads[name].start()
+
+    def read_rows(j):
+        read(("late", j), late_hbm[j], late_in.at[j])
+        read(("early", j), early_hbm.at[:, j], early_in.at[j])
+
+    read("gate_first", gate_hbm.at[0, first], gate_w.at[first])
+    read(("late", ORDER[0]), late_hbm[ORDER[0]], late_in.at[ORDER[0]])
+    read("up_first", up_hbm.at[0, first], up_w.at[first])
+    read(("early", ORDER[0]), early_hbm.at[:, ORDER[0]], early_in.at[ORDER[0]])
+    read("gate_second", gate_hbm.at[0, second], gate_w.at[second])
+    read("up_second", up_hbm.at[0, second], up_w.at[second])
+    read("down", down_hbm.at[0], down_w)
+    for j in ORDER[1:]:
+        read_rows(j)
+
+    waited = set()
+
+    def ready(*names):
+        for name in names:
+            if name not in waited:
+                waited.add(name)
+                reads[name].wait()
+
+    writes = []
+
+    def write(source, target):
+        writes.append(pltpu.make_async_copy(source, target, out_sems.at[len(writes)]))
+        writes[-1].start()
+
+    def half_expert(late, early, j=None):
+        if j is not None:
+            ready("gate_first", ("late", j))
+        gate = exact_dot(late(), gate_w[:half, :])
+        ready("up_first")
+        up = exact_dot(late(), up_w[:half, :])
+        if j is not None:
+            ready(("early", j), "gate_second")
+        gate = gate + exact_dot(early(), gate_w[half:, :])
+        ready("up_second")
+        up = up + exact_dot(early(), up_w[half:, :])
+        hidden = (gate / (1.0 + jnp.exp(-gate)) * up).astype(jnp.bfloat16)
+        ready("down")
+        late_value = exact_dot(hidden, down_w[:, :half]).astype(jnp.bfloat16)
+        early_value = exact_dot(hidden, down_w[:, half:]).astype(jnp.bfloat16)
+        return late_value, early_value
+
+    for j in ORDER:
+        late_value, early_value = half_expert(
+            lambda: late_in[j, :, :, :half].reshape(main, half),
+            lambda: early_in[j, :, :, :half].reshape(main, half),
+            j,
+        )
+        late_made[j, :, :, :half] = late_value.reshape(chunks, MAIN, half)
+        write(late_made.at[j, :, :, body], late_out[j].at[:, :, body])
+        early_made[j, :, :, :half] = early_value.reshape(chunks, MAIN, half)
+        write(early_made.at[j, :, :, body], early_out.at[:, j, :, body])
+
+    matrix = split_matrix()
+
+    def gather_last(buffer):
+        return pieces_to_rows(buffer[:, :, :, half:].reshape(RING * main, width - half), matrix)
+
+    late_rows, early_rows = gather_last(late_in), gather_last(early_in)
+    late_value, early_value = half_expert(lambda: late_rows, lambda: early_rows)
+    for value, made in ((late_value, late_made), (early_value, early_made)):
+        for j in range(RING):
+            pieces = rows_to_pieces(value[last * j : last * (j + 1)], matrix)
+            made[j, :, :, half:] = pieces.reshape(chunks, MAIN, width - half)
+    for j in range(RING):
+        write(late_made.at[j, :, :, tail], late_out[j].at[:, :, tail])
+        write(early_made.at[j, :, :, tail], early_out.at[:, j, :, tail])
+    for copy in writes:
+        copy.wait()
+
+
+def half_ffn(late, early, w_gate, w_up, w_down):
+    chunks, _, width = late[0].shape
     model, hidden = w_gate.shape[1:]
-    rows = chunks * CAP
-    half = model // 2
-    on_chip = pl.BlockSpec(memory_space=pltpu.VMEM)
-    out = jax.ShapeDtypeStruct((rows, hidden), jnp.float32)
-    return pl.pallas_call(
-        first_ffn_kernel,
-        in_specs=[on_chip] * 3,
-        out_specs=[on_chip] * 2,
-        out_shape=[out, out],
-        scratch_shapes=[pltpu.VMEM((rows, half), jnp.bfloat16)],
-        cost_estimate=pl.CostEstimate(
-            flops=4 * rows * half * hidden, bytes_accessed=8 * rows * hidden, transcendentals=0
-        ),
-        compiler_params=pltpu.CompilerParams(vmem_limit_bytes=12 * 1024 * 1024),
-        name="first_ffn",
-    )(late, w_gate, w_up)
-
-
-def second_ffn_kernel(early_ref, gate_in, up_in, gate_ref, up_ref, down_ref, *refs):
-    late_out, early_out, rows_ref = refs[-3:]
-    half = rows_ref.shape[1]
-    matrix = split_matrix()
-    unpack_chunks(early_ref[:, 0], rows_ref, matrix)
-    rows = rows_ref[...]
-    gate = gate_in[...] + exact_dot(rows, gate_ref[0, half:, :])
-    up = up_in[...] + exact_dot(rows, up_ref[0, half:, :])
-    hidden = (gate / (1.0 + jnp.exp(-gate)) * up).astype(jnp.bfloat16)
-    value = exact_dot(hidden, down_ref[0, :, :half]).astype(jnp.bfloat16)
-    main, pieces = pack_chunks(value, matrix)
-    late_out[:, :, :half] = main
-    late_out[:, :, half:] = pieces
-    value = exact_dot(hidden, down_ref[0, :, half:]).astype(jnp.bfloat16)
-    main, pieces = pack_chunks(value, matrix)
-    early_out[:, 0, :, :half] = main
-    early_out[:, 0, :, half:] = pieces
-
-
-def second_ffn(j, early, gate, up, w_gate, w_up, w_down, early_out):
-    chunks, _, _, width = early.shape
-    model, hidden = w_gate.shape[1:]
-    rows = chunks * CAP
-    half = model // 2
-    on_chip = pl.BlockSpec(memory_space=pltpu.VMEM)
-    block = pl.BlockSpec((chunks, 1, MAIN, width), lambda i: (0, j, 0, 0))
-    held = [] if early_out is None else [early_out]
-    return pl.pallas_call(
-        second_ffn_kernel,
-        grid=(1,),
-        in_specs=[block] + [on_chip] * 5 + [pl.BlockSpec(memory_space=pl.ANY)] * len(held),
-        out_specs=[on_chip, block],
-        out_shape=[
-            jax.ShapeDtypeStruct((chunks, MAIN, width), jnp.bfloat16),
-            pltpu.HBM(early.shape, jnp.bfloat16),
+    rows = RING * chunks * CAP
+    outside = pl.BlockSpec(memory_space=pltpu.HBM)
+    buffer = pltpu.VMEM((RING, chunks, MAIN, width), jnp.bfloat16)
+    late_shape = jax.ShapeDtypeStruct(late[0].shape, jnp.bfloat16)
+    *late_out, early_out = pl.pallas_call(
+        ffn_kernel,
+        in_specs=[outside] * (RING + 4),
+        out_specs=[outside] * (RING + 1),
+        out_shape=[late_shape] * RING + [jax.ShapeDtypeStruct(early.shape, jnp.bfloat16)],
+        scratch_shapes=[
+            buffer,
+            buffer,
+            pltpu.VMEM((model, hidden), jnp.bfloat16),
+            pltpu.VMEM((model, hidden), jnp.bfloat16),
+            pltpu.VMEM((hidden, model), jnp.bfloat16),
+            buffer,
+            buffer,
+            pltpu.SemaphoreType.DMA((2 * RING + 5,)),
+            pltpu.SemaphoreType.DMA((4 * RING,)),
         ],
-        input_output_aliases={6: 1} if held else {},
-        scratch_shapes=[pltpu.VMEM((rows, half), jnp.bfloat16)],
-        cost_estimate=pl.CostEstimate(
-            flops=2 * rows * model * hidden + 4 * rows * half * hidden,
-            bytes_accessed=4 * rows * half + 8 * rows * hidden,
+        cost_estimate=pl.CostEstimate(
+            flops=6 * rows * model * hidden,
+            bytes_accessed=4 * rows * model + 6 * model * hidden,
             transcendentals=rows * hidden,
         ),
-        compiler_params=pltpu.CompilerParams(vmem_limit_bytes=20 * 1024 * 1024),
-        name="second_ffn",
-    )(early, gate, up, w_gate, w_up, w_down, *held)
+        compiler_params=pltpu.CompilerParams(vmem_limit_bytes=56 * 1024 * 1024),
+        name="half_ffn",
+    )(*late, early, w_gate, w_up, w_down)
+    return late_out, early_out
 
 
 def sum_halves_kernel(a_ref, b_ref, c_ref, d_ref, out_ref):
@@ -410,12 +445,10 @@
     early = early.reshape(chunks, RING, MAIN, width)
 
     late_in = (near, across(near, 1), across(far, 2), across(far, 3))
-    first = {j: first_ffn(late_in[j], w_gate, w_up) for j in (0, 1, 3, 2)}
-    early_out, late_back = None, [None] * RING
-    for j in ORDER:
-        late_out, early_out = second_ffn(j, early, *first[j], w_gate, w_up, w_down, early_out)
-        late_back[j] = across(late_out, j) if j else late_out
-
+    late_out, early_out = half_ffn(late_in, early, w_gate, w_up, w_down)
+    late_back = [late_out[0]]
+    for j in range(1, RING):
+        late_back.append(across(late_out[j], j))
     early_out = plane_exchange(early_out.reshape(chunks, RING * MAIN, width))
     late_back = plane_exchange(sum_halves(late_back).reshape(chunks, 2 * MAIN, width))
     partial = early_combine(

time: 262 us -> 246 us (0.939)
  local copies, waits for them, and re-layouts: 35.8 us -> 15.7 us
  waiting for transfers between devices: 114 us -> 130 us
  Pallas kernels: 56.7 us -> 45.5 us
    unnamed x64 -> x20, local copies, waits for them, and re-layouts: 33.2 us -> 11.4 us
    ppermute x15, waiting for transfers between devices: 91.2 us -> 110 us  [across(): return lax.ppermute(array, 'y', [(y, y ^ j) for y in range(RING)])]
    pallas_call x8 -> x1, Pallas kernels: 41.6 us -> 30.3 us  [half_ffn(): pl.pallas_call(ffn_kernel, in_specs=[outside] * (RING + 4), out_specs=[ou...]
  transfers between devices with their start and end apart: 19 -> 19, of which waited for: 9 -> 10; matrix products, arithmetic and copies ran while one was open for 4% -> 5% of each run, Pallas kernels for 9% -> 4%
where the time goes in v4:
time: 246 us; the launch traced here: 243 us
  waiting for transfers between devices  130 us (53%)
  starting transfers between devices  51.7 us (21%)
  Pallas kernels  45.5 us (18%)
  local copies, waits for them, and re-layouts  15.7 us (6%)
    ppermute x15, waiting for transfers between devices, across(): return lax.ppermute(array, 'y', [(y, y ^ j) for y in range(RING)])  110 us
    all_to_all x4, starting transfers between devices, plane_exchange(): return lax.all_to_all(array, PLANE, split_axis=0, concat_axis=0, tiled=True)  33.2 us
    pallas_call x1, Pallas kernels, half_ffn(): pl.pallas_call(ffn_kernel, in_specs=[outside] * (RING + 4), out_specs=[ou...  30.3 us
    all_to_all x4, waiting for transfers between devices, plane_exchange(): return lax.all_to_all(array, PLANE, split_axis=0, concat_axis=0, tiled=True)  20.2 us
    ppermute x15, starting transfers between devices, across(): return lax.ppermute(array, 'y', [(y, y ^ j) for y in range(RING)])  18.5 us
    unnamed x20, local copies, waits for them, and re-layouts  11.4 us
  transfers between devices with their start and end apart: 19, of which 10 were waited for; matrix products, arithmetic and copies ran while one was open for 5% of the time, Pallas kernels for 4%

profile of v4, /device:TPU:37, one launch (start us, length us, event | category | flops | bytes accessed | tf_op | source)
XLA Modules:
  0.0 243.3 jit_solution(12293732314047883950)
XLA Ops:
  0.0 0.0 copy-start.2
  0.0 1.0 copy-done.2
  1.0 0.0 copy-start.4
  1.0 0.7 copy-done.4
  1.7 3.2 %late_dispatch.1 = bf16[64,16,1152]{2,1,0:T(8,128)(2,1)} custom-call(s32[1]{0:T(128)} %bitcast.pair_ref, s32[6,128]{1,0:T(8,128)S(1)} %bitcast.41, bf16[128,2048]{1,0:T(8,128)(2,1)S(1)} %copy-done.2), custom_call_target="tpu_custom_call" | custom-call | flops 301989888 | bytes 2359296 | tf_op jit(solution)/shard_map/late_dispatch/pallas_call | solution.py:127
  4.9 8.4 %all-to-all-start = ((bf16[32,32,1152]{2,1,0:T(8,128)(2,1)}), bf16[32,32,1152]{2,1,0:T(8,128)(2,1)}, u32[]{:S(2)}, u32[]{:S(2)}) async-start(bf16[32,32,1152]{2,1,0:T(8,128)(2,1)} %bitcast.3), calls=%async_computation | async-start | bytes 4718592 | tf_op jit(solution)/shard_map/all_to_all | solution.py:422
  13.4 0.0 copy-done.5
  13.4 0.0 copy-done.7
  13.4 2.8 %collective-permute-start.5 = (bf16[12,128]{1,0:T(8,128)(2,1)S(1)}, bf16[12,128]{1,0:T(8,128)(2,1)S(1)}, u32[]{:S(2)}, u32[]{:S(2)}) collective-permute-start(bf16[12,128]{1,0:T(8,128)(2,1)S(1)} %get-tuple-element.26), channel_id=1, source_target_pairs={{0,3},{1,2},{2,1},{3,0},{4,7},{5,6},{6,5},{7,4},{8,11},{9,10},{10,... | collective-permute-start | bytes 9224 | tf_op jit(solution)/shard_map/ppermute | solution.py:414
  16.2 0.0 collective-permute-start.3
  16.2 1.3 collective-permute-start.4
  17.5 0.0 copy-done.3
  17.6 0.3 collective-permute-start.6
  17.8 3.6 %collective-permute-start.7 = (bf16[128,1024]{1,0:T(8,128)(2,1)S(1)}, bf16[128,1024]{1,0:T(8,128)(2,1)S(1)}, u32[]{:S(2)}, u32[]{:S(2)}) collective-permute-start(bf16[128,1024]{1,0:T(8,128)(2,1)S(1)} %get-tuple-element.22), channel_id=1, source_target_pairs={{0,2},{1,3},{2,0},{3,1},{4,6},{5,7},{6,4},{7,5},{8,10},{9,11},{10,... | collective-permute-start | bytes 786440 | tf_op jit(solution)/shard_map/ppermute | solution.py:414
  21.4 0.0 collective-permute-done.5
  21.4 0.1 collective-permute-start.8
  21.5 0.0 collective-permute-done.3
  21.5 0.0 collective-permute-done.4
  21.5 3.0 %collective-permute-done.6 = bf16[128,1024]{1,0:T(8,128)(2,1)S(1)} collective-permute-done((bf16[128,1024]{1,0:T(8,128)(2,1)S(1)}, bf16[128,1024]{1,0:T(8,128)(2,1)S(1)}, u32[]{:S(2)}, u32[]{:S(2)}) %collective-permute-start.6) | collective-permute-done | bytes 262176 | tf_op jit(solution)/shard_map/ppermute | solution.py:414
  24.5 7.7 %collective-permute-done.7 = bf16[128,1024]{1,0:T(8,128)(2,1)S(1)} collective-permute-done((bf16[128,1024]{1,0:T(8,128)(2,1)S(1)}, bf16[128,1024]{1,0:T(8,128)(2,1)S(1)}, u32[]{:S(2)}, u32[]{:S(2)}) %collective-permute-start.7) | collective-permute-done | bytes 262176 | tf_op jit(solution)/shard_map/ppermute | solution.py:414
  32.2 2.6 %collective-permute-done.8 = bf16[128,1024]{1,0:T(8,128)(2,1)S(1)} collective-permute-done((bf16[128,1024]{1,0:T(8,128)(2,1)S(1)}, bf16[128,1024]{1,0:T(8,128)(2,1)S(1)}, u32[]{:S(2)}, u32[]{:S(2)}) %collective-permute-start.8) | collective-permute-done | bytes 262176 | tf_op jit(solution)/shard_map/ppermute | solution.py:414
  34.8 0.1 pad_maximum_fusion.tokens_ref
  35.0 3.4 %early_dispatch.1 = bf16[32,4,16,1152]{3,2,1,0:T(8,128)(2,1)S(1)} custom-call(s32[1]{0:T(128)} %bitcast.pair_ref, s32[4,6,128]{2,1,0:T(8,128)S(1)} %get-tuple-element.24.ids_ref, bf16[4,128,1024]{2,1,0:T(8,128)(2,1)S(1)} %pad_maximum_fusion.tokens_ref), custom_call_target="tpu_custom_call" | custom-call | flops 603979776 | bytes 4718592 | tf_op jit(solution)/shard_map/early_dispatch/pallas_call | solution.py:161
  38.3 0.0 copy-start
  38.3 2.2 copy-done
  40.5 1.1 all-to-all-done
  41.6 8.1 %all-to-all-start.1 = ((bf16[32,64,1152]{2,1,0:T(8,128)(2,1)}), bf16[32,64,1152]{2,1,0:T(8,128)(2,1)}, u32[]{:S(2)}, u32[]{:S(2)}) async-start(bf16[32,64,1152]{2,1,0:T(8,128)(2,1)} %bitcast.39), calls=%async_computation.1 | async-start | bytes 9437184 | tf_op jit(solution)/shard_map/all_to_all | solution.py:422
  49.7 0.0 copy-start.6
  49.7 3.4 %slice_bitcast_fusion = (bf16[32,16,1152]{2,1,0:T(8,128)(2,1)}, bf16[32,16,1152]{2,1,0:T(8,128)(2,1)}) fusion(bf16[32,2,16,1152]{3,2,1,0:T(8,128)(2,1)} %bitcast.4), kind=kLoop, calls=%fused_computation | loop fusion | bytes 4718592 | tf_op jit(solution)/shard_map/squeeze | solution.py:438
  53.1 0.1 collective-permute-start
  53.2 2.6 %collective-permute-start.1 = (bf16[32,16,1152]{2,1,0:T(8,128)(2,1)}, bf16[32,16,1152]{2,1,0:T(8,128)(2,1)}, u32[]{:S(2)}, u32[]{:S(2)}) collective-permute-start(bf16[32,16,1152]{2,1,0:T(8,128)(2,1)} %get-tuple-element.15), channel_id=1, source_target_pairs={{0,2},{1,3},{2,0},{3,1},{4,6},{5,7},{6,4},{7,5},{8,10},{9,11},{10,... | collective-permute-start | bytes 3538952 | tf_op jit(solution)/shard_map/ppermute | solution.py:414
  55.9 1.1 collective-permute-start.2
  57.0 0.0 copy-done.6
  57.0 2.8 %copy.11.refs_5_ = bf16[1,2048,704]{2,1,0:T(8,128)(2,1)} copy(bf16[1,2048,704]{1,2,0:T(8,128)(2,1)S(1)} %copy-done.6) | data formatting | bytes 5767168 | tf_op args[3]
  59.8 4.6 %copy.12.refs_6_ = bf16[1,2048,704]{2,1,0:T(8,128)(2,1)} copy(bf16[1,2048,704]{1,2,0:T(8,128)(2,1)} %param.10) | data formatting | bytes 5767168 | tf_op args[4]
  64.4 16.1 %collective-permute-done.refs_1_ = bf16[32,16,1152]{2,1,0:T(8,128)(2,1)} collective-permute-done((bf16[32,16,1152]{2,1,0:T(8,128)(2,1)}, bf16[32,16,1152]{2,1,0:T(8,128)(2,1)}, u32[]{:S(2)}, u32[]{:S(2)}) %collective-permute-start) | collective-permute-done | bytes 1179680 | tf_op jit(solution)/shard_map/ppermute | solution.py:414
  80.5 26.6 %collective-permute-done.1.refs_2_ = bf16[32,16,1152]{2,1,0:T(8,128)(2,1)} collective-permute-done((bf16[32,16,1152]{2,1,0:T(8,128)(2,1)}, bf16[32,16,1152]{2,1,0:T(8,128)(2,1)}, u32[]{:S(2)}, u32[]{:S(2)}) %collective-permute-start.1) | collective-permute-done | bytes 1179680 | tf_op jit(solution)/shard_map/ppermute | solution.py:414
  107.2 2.1 collective-permute-done.2.refs_3_
  109.2 0.0 all-to-all-done.1
  109.2 30.3 %half_ffn.1 = (bf16[32,16,1152]{2,1,0:T(8,128)(2,1)}, bf16[32,16,1152]{2,1,0:T(8,128)(2,1)}, bf16[32,16,1152]{2,1,0:T(8,128)(2,1)}, bf16[32,16,1152]{2,1,0:T(8,128)(2,1)}, bf16[32,4,16,1152]{3,2,1,0:T(8,128)(2,1)}) custom-call(bf16[32,16,1152]{2,1,0:T(8,128)(2,1)} %get-tuple-element.16.refs_0_, bf16[32,16,1152]{2,1,0:T(8,128)(2,1)} %collective-permute-done.refs_1_, ...), custom_call_target="tpu_custom_call" | custom-call | flops 19931332608 | bytes 27525120 | tf_op jit(solution)/shard_map/half_ffn/pallas_call | solution.py:282
  139.6 0.0 copy-start.8
  139.6 0.0 copy-start.1
  139.6 9.0 %all-to-all-start.3 = ((bf16[32,64,1152]{2,1,0:T(8,128)(2,1)}), bf16[32,64,1152]{2,1,0:T(8,128)(2,1)}, u32[]{:S(2)}, u32[]{:S(2)}) async-start(bf16[32,64,1152]{2,1,0:T(8,128)(2,1)} %bitcast.43), calls=%async_computation.3 | async-start | bytes 9437184 | tf_op jit(solution)/shard_map/all_to_all | solution.py:422
  148.6 0.1 collective-permute-start.10
  148.7 1.2 collective-permute-start.11
  149.9 0.0 copy-done.8
  149.9 1.5 collective-permute-start.9
  151.3 26.2 %collective-permute-done.10.c_ref = bf16[32,16,1152]{2,1,0:T(8,128)(2,1)S(1)} collective-permute-done((bf16[32,16,1152]{2,1,0:T(8,128)(2,1)}, bf16[32,16,1152]{2,1,0:T(8,128)(2,1)S(1)}, u32[]{:S(2)}, u32[]{:S(2)}) %collective-permute-start.10) | collective-permute-done | bytes 1179680 | tf_op jit(solution)/shard_map/ppermute | solution.py:414
  177.6 25.6 %collective-permute-done.11.d_ref = bf16[32,16,1152]{2,1,0:T(8,128)(2,1)S(1)} collective-permute-done((bf16[32,16,1152]{2,1,0:T(8,128)(2,1)}, bf16[32,16,1152]{2,1,0:T(8,128)(2,1)S(1)}, u32[]{:S(2)}, u32[]{:S(2)}) %collective-permute-start.11) | collective-permute-done | bytes 1179680 | tf_op jit(solution)/shard_map/ppermute | solution.py:414
  203.2 0.0 collective-permute-done.9.b_ref
  203.2 0.0 copy-done.1
  203.2 1.9 sum_halves.1
  205.1 0.0 all-to-all-done.3
  205.1 7.7 %all-to-all-start.2 = ((bf16[32,32,1152]{2,1,0:T(8,128)(2,1)}), bf16[32,32,1152]{2,1,0:T(8,128)(2,1)S(1)}, u32[]{:S(2)}, u32[]{:S(2)}) async-start(bf16[32,32,1152]{2,1,0:T(8,128)(2,1)} %bitcast.17), calls=%async_computation.2 | async-start | bytes 4718592 | tf_op jit(solution)/shard_map/all_to_all | solution.py:422
  212.8 4.4 %early_combine.1 = bf16[4,128,1024]{2,1,0:T(8,128)(2,1)S(1)} custom-call(s32[1]{0:T(128)} %bitcast.pair_ref, s32[4,6,128]{2,1,0:T(8,128)S(1)} %get-tuple-element.24.ids_ref, f32[4,6,128]{2,1,0:T(8,128)S(1)} %get-tuple-element.23.gates_ref, bf16[32,4,16,1152]{3,2,1,0:T(8,128)(2,1)} %bitcast.20.rows_ref), custom_call_target="tpu_custom_call" | custom-call | flops 603979776 | bytes 4718592 | tf_op jit(solution)/shard_map/early_combine/pallas_call | solution.py:347
  217.2 0.9 slice_bitcast_fusion.2
  218.1 0.0 collective-permute-start.12
  218.1 2.3 collective-permute-start.13
  220.4 1.6 collective-permute-start.14
  221.9 19.0 %all-to-all-done.2 = bf16[32,32,1152]{2,1,0:T(8,128)(2,1)S(1)} async-done(((bf16[32,32,1152]{2,1,0:T(8,128)(2,1)}), bf16[32,32,1152]{2,1,0:T(8,128)(2,1)S(1)}, u32[]{:S(2)}, u32[]{:S(2)}) %all-to-all-start.2) | async-done | bytes 2359328 | tf_op jit(solution)/shard_map/all_to_all | solution.py:422
  241.0 0.0 collective-permute-done.12.refs_1_
  241.0 0.0 collective-permute-done.13.refs_2_
  241.0 0.0 collective-permute-done.14.refs_3_
  241.0 2.3 final_combine.1
  (9 shorter events, 0.1 us)
Async XLA Ops:
  0.0 1.0 copy-start.2
  1.0 0.7 copy-start.4
  4.9 8.5 %copy-start.5 = (s32[128,6]{0,1:T(8,128)S(1)}, s32[128,6]{0,1:T(8,128)}, u32[]{:S(2)}) copy-start(s32[128,6]{0,1:T(8,128)} %param.7) | copy-start | bytes 9220
  4.9 8.5 %copy-start.7 = (bf16[128,6]{0,1:T(8,128)(2,1)S(1)}, bf16[128,6]{0,1:T(8,128)(2,1)}, u32[]{:S(2)}) copy-start(bf16[128,6]{0,1:T(8,128)(2,1)} %param.8) | copy-start | bytes 4612
  4.9 12.6 %copy-start.3 = (bf16[128,2048]{1,0:T(8,128)(2,1)S(1)}, bf16[128,2048]{1,0:T(8,128)(2,1)}, u32[]{:S(2)}) copy-start(bf16[128,2048]{1,0:T(8,128)(2,1)} %tokens_ref.1) | copy-start | bytes 1572868
  4.9 36.7 %all-to-all-start = ((bf16[32,32,1152]{2,1,0:T(8,128)(2,1)}), bf16[32,32,1152]{2,1,0:T(8,128)(2,1)}, u32[]{:S(2)}, u32[]{:S(2)}) async-start(bf16[32,32,1152]{2,1,0:T(8,128)(2,1)} %bitcast.3), calls=%async_computation | async-start | bytes 4718592 | tf_op jit(solution)/shard_map/all_to_all | solution.py:422
  13.4 8.0 %collective-permute-start.5 = (bf16[12,128]{1,0:T(8,128)(2,1)S(1)}, bf16[12,128]{1,0:T(8,128)(2,1)S(1)}, u32[]{:S(2)}, u32[]{:S(2)}) collective-permute-start(bf16[12,128]{1,0:T(8,128)(2,1)S(1)} %get-tuple-element.26), channel_id=1, source_target_pairs={{0,3},{1,2},{2,1},{3,0},{4,7},{5,6},{6,5},{7,4},{8,11},{9,10},{10,... | collective-permute-start | bytes 9224 | tf_op jit(solution)/shard_map/ppermute | solution.py:414
  16.2 5.3 %collective-permute-start.3 = (bf16[12,128]{1,0:T(8,128)(2,1)S(1)}, bf16[12,128]{1,0:T(8,128)(2,1)S(1)}, u32[]{:S(2)}, u32[]{:S(2)}) collective-permute-start(bf16[12,128]{1,0:T(8,128)(2,1)S(1)} %get-tuple-element.26), channel_id=1, source_target_pairs={{0,1},{1,0},{2,3},{3,2},{4,5},{5,4},{6,7},{7,6},{8,9},{9,8},{10,11... | collective-permute-start | bytes 9224 | tf_op jit(solution)/shard_map/ppermute | solution.py:414
  16.2 5.3 %collective-permute-start.4 = (bf16[12,128]{1,0:T(8,128)(2,1)S(1)}, bf16[12,128]{1,0:T(8,128)(2,1)S(1)}, u32[]{:S(2)}, u32[]{:S(2)}) collective-permute-start(bf16[12,128]{1,0:T(8,128)(2,1)S(1)} %get-tuple-element.26), channel_id=1, source_target_pairs={{0,2},{1,3},{2,0},{3,1},{4,6},{5,7},{6,4},{7,5},{8,10},{9,11},{10,... | collective-permute-start | bytes 9224 | tf_op jit(solution)/shard_map/ppermute | solution.py:414
  17.6 7.0 %collective-permute-start.6 = (bf16[128,1024]{1,0:T(8,128)(2,1)S(1)}, bf16[128,1024]{1,0:T(8,128)(2,1)S(1)}, u32[]{:S(2)}, u32[]{:S(2)}) collective-permute-start(bf16[128,1024]{1,0:T(8,128)(2,1)S(1)} %get-tuple-element.22), channel_id=1, source_target_pairs={{0,1},{1,0},{2,3},{3,2},{4,5},{5,4},{6,7},{7,6},{8,9},{9,8},{10,11... | collective-permute-start | bytes 786440 | tf_op jit(solution)/shard_map/ppermute | solution.py:414
  17.8 14.4 %collective-permute-start.7 = (bf16[128,1024]{1,0:T(8,128)(2,1)S(1)}, bf16[128,1024]{1,0:T(8,128)(2,1)S(1)}, u32[]{:S(2)}, u32[]{:S(2)}) collective-permute-start(bf16[128,1024]{1,0:T(8,128)(2,1)S(1)} %get-tuple-element.22), channel_id=1, source_target_pairs={{0,2},{1,3},{2,0},{3,1},{4,6},{5,7},{6,4},{7,5},{8,10},{9,11},{10,... | collective-permute-start | bytes 786440 | tf_op jit(solution)/shard_map/ppermute | solution.py:414
  21.4 13.4 %collective-permute-start.8 = (bf16[128,1024]{1,0:T(8,128)(2,1)S(1)}, bf16[128,1024]{1,0:T(8,128)(2,1)S(1)}, u32[]{:S(2)}, u32[]{:S(2)}) collective-permute-start(bf16[128,1024]{1,0:T(8,128)(2,1)S(1)} %get-tuple-element.22), channel_id=1, source_target_pairs={{0,3},{1,2},{2,1},{3,0},{4,7},{5,6},{6,5},{7,4},{8,11},{9,10},{10,... | collective-permute-start | bytes 786440 | tf_op jit(solution)/shard_map/ppermute | solution.py:414
  38.3 2.2 copy-start
  41.6 67.6 %all-to-all-start.1 = ((bf16[32,64,1152]{2,1,0:T(8,128)(2,1)}), bf16[32,64,1152]{2,1,0:T(8,128)(2,1)}, u32[]{:S(2)}, u32[]{:S(2)}) async-start(bf16[32,64,1152]{2,1,0:T(8,128)(2,1)} %bitcast.39), calls=%async_computation.1 | async-start | bytes 9437184 | tf_op jit(solution)/shard_map/all_to_all | solution.py:422
  49.7 7.2 %copy-start.6 = (bf16[1,2048,704]{1,2,0:T(8,128)(2,1)S(1)}, bf16[1,2048,704]{1,2,0:T(8,128)(2,1)}, u32[]{:S(2)}) copy-start(bf16[1,2048,704]{1,2,0:T(8,128)(2,1)} %param.9) | copy-start | bytes 8650756
  53.1 27.4 %collective-permute-start = (bf16[32,16,1152]{2,1,0:T(8,128)(2,1)}, bf16[32,16,1152]{2,1,0:T(8,128)(2,1)}, u32[]{:S(2)}, u32[]{:S(2)}) collective-permute-start(bf16[32,16,1152]{2,1,0:T(8,128)(2,1)} %get-tuple-element.16.refs_0_), channel_id=1, source_target_pairs={{0,1},{1,0},{2,3},{3,2},{4,5},{5,4},{6,7},{7,6},{8,9},{9,8},{10,11... | collective-permute-start | bytes 3538952 | tf_op jit(solution)/shard_map/ppermute | solution.py:414
  53.2 53.9 %collective-permute-start.1 = (bf16[32,16,1152]{2,1,0:T(8,128)(2,1)}, bf16[32,16,1152]{2,1,0:T(8,128)(2,1)}, u32[]{:S(2)}, u32[]{:S(2)}) collective-permute-start(bf16[32,16,1152]{2,1,0:T(8,128)(2,1)} %get-tuple-element.15), channel_id=1, source_target_pairs={{0,2},{1,3},{2,0},{3,1},{4,6},{5,7},{6,4},{7,5},{8,10},{9,11},{10,... | collective-permute-start | bytes 3538952 | tf_op jit(solution)/shard_map/ppermute | solution.py:414
  55.9 53.4 %collective-permute-start.2 = (bf16[32,16,1152]{2,1,0:T(8,128)(2,1)}, bf16[32,16,1152]{2,1,0:T(8,128)(2,1)}, u32[]{:S(2)}, u32[]{:S(2)}) collective-permute-start(bf16[32,16,1152]{2,1,0:T(8,128)(2,1)} %get-tuple-element.15), channel_id=1, source_target_pairs={{0,3},{1,2},{2,1},{3,0},{4,7},{5,6},{6,5},{7,4},{8,11},{9,10},{10,... | collective-permute-start | bytes 3538952 | tf_op jit(solution)/shard_map/ppermute | solution.py:414
  139.6 10.3 %copy-start.8 = (bf16[32,16,1152]{2,1,0:T(8,128)(2,1)S(1)}, bf16[32,16,1152]{2,1,0:T(8,128)(2,1)}, u32[]{:S(2)}) copy-start(bf16[32,16,1152]{2,1,0:T(8,128)(2,1)} %get-tuple-element.11) | copy-start | bytes 3538948
  139.6 63.6 %copy-start.1 = (bf16[32,16,1152]{2,1,0:T(8,128)(2,1)S(1)}, bf16[32,16,1152]{2,1,0:T(8,128)(2,1)}, u32[]{:S(2)}) copy-start(bf16[32,16,1152]{2,1,0:T(8,128)(2,1)} %get-tuple-element.10.a_ref) | copy-start | bytes 3538948
  139.6 65.5 %all-to-all-start.3 = ((bf16[32,64,1152]{2,1,0:T(8,128)(2,1)}), bf16[32,64,1152]{2,1,0:T(8,128)(2,1)}, u32[]{:S(2)}, u32[]{:S(2)}) async-start(bf16[32,64,1152]{2,1,0:T(8,128)(2,1)} %bitcast.43), calls=%async_computation.3 | async-start | bytes 9437184 | tf_op jit(solution)/shard_map/all_to_all | solution.py:422
  148.6 29.0 %collective-permute-start.10 = (bf16[32,16,1152]{2,1,0:T(8,128)(2,1)}, bf16[32,16,1152]{2,1,0:T(8,128)(2,1)S(1)}, u32[]{:S(2)}, u32[]{:S(2)}) collective-permute-start(bf16[32,16,1152]{2,1,0:T(8,128)(2,1)} %get-tuple-element.12), channel_id=1, source_target_pairs={{0,2},{1,3},{2,0},{3,1},{4,6},{5,7},{6,4},{7,5},{8,10},{9,11},{10,... | collective-permute-start | bytes 3538952 | tf_op jit(solution)/shard_map/ppermute | solution.py:414
  148.7 54.5 %collective-permute-start.11 = (bf16[32,16,1152]{2,1,0:T(8,128)(2,1)}, bf16[32,16,1152]{2,1,0:T(8,128)(2,1)S(1)}, u32[]{:S(2)}, u32[]{:S(2)}) collective-permute-start(bf16[32,16,1152]{2,1,0:T(8,128)(2,1)} %get-tuple-element.13), channel_id=1, source_target_pairs={{0,3},{1,2},{2,1},{3,0},{4,7},{5,6},{6,5},{7,4},{8,11},{9,10},{10,... | collective-permute-start | bytes 3538952 | tf_op jit(solution)/shard_map/ppermute | solution.py:414
  149.9 53.3 %collective-permute-start.9 = (bf16[32,16,1152]{2,1,0:T(8,128)(2,1)S(1)}, bf16[32,16,1152]{2,1,0:T(8,128)(2,1)S(1)}, u32[]{:S(2)}, u32[]{:S(2)}) collective-permute-start(bf16[32,16,1152]{2,1,0:T(8,128)(2,1)S(1)} %copy-done.8), channel_id=1, source_target_pairs={{0,1},{1,0},{2,3},{3,2},{4,5},{5,4},{6,7},{7,6},{8,9},{9,8},{10,11... | collective-permute-start | bytes 3538952 | tf_op jit(solution)/shard_map/ppermute | solution.py:414
  205.1 35.9 %all-to-all-start.2 = ((bf16[32,32,1152]{2,1,0:T(8,128)(2,1)}), bf16[32,32,1152]{2,1,0:T(8,128)(2,1)S(1)}, u32[]{:S(2)}, u32[]{:S(2)}) async-start(bf16[32,32,1152]{2,1,0:T(8,128)(2,1)} %bitcast.17), calls=%async_computation.2 | async-start | bytes 4718592 | tf_op jit(solution)/shard_map/all_to_all | solution.py:422
  218.1 22.9 %collective-permute-start.12 = (bf16[128,1024]{1,0:T(8,128)(2,1)}, bf16[128,1024]{1,0:T(8,128)(2,1)S(1)}, u32[]{:S(2)}, u32[]{:S(2)}) collective-permute-start(bf16[128,1024]{1,0:T(8,128)(2,1)} %get-tuple-element.19), channel_id=1, source_target_pairs={{0,1},{1,0},{2,3},{3,2},{4,5},{5,4},{6,7},{7,6},{8,9},{9,8},{10,11... | collective-permute-start | bytes 786440 | tf_op jit(solution)/shard_map/ppermute | solution.py:414
  218.1 22.9 %collective-permute-start.13 = (bf16[128,1024]{1,0:T(8,128)(2,1)}, bf16[128,1024]{1,0:T(8,128)(2,1)S(1)}, u32[]{:S(2)}, u32[]{:S(2)}) collective-permute-start(bf16[128,1024]{1,0:T(8,128)(2,1)} %get-tuple-element.18), channel_id=1, source_target_pairs={{0,2},{1,3},{2,0},{3,1},{4,6},{5,7},{6,4},{7,5},{8,10},{9,11},{10,... | collective-permute-start | bytes 786440 | tf_op jit(solution)/shard_map/ppermute | solution.py:414
  220.4 20.6 %collective-permute-start.14 = (bf16[128,1024]{1,0:T(8,128)(2,1)}, bf16[128,1024]{1,0:T(8,128)(2,1)S(1)}, u32[]{:S(2)}, u32[]{:S(2)}) collective-permute-start(bf16[128,1024]{1,0:T(8,128)(2,1)} %get-tuple-element.17), channel_id=1, source_target_pairs={{0,3},{1,2},{2,1},{3,0},{4,7},{5,6},{6,5},{7,4},{8,11},{9,10},{10,... | collective-permute-start | bytes 786440 | tf_op jit(solution)/shard_map/ppermute | solution.py:414

commit v5 on v4

--- a/solution.py
+++ b/solution.py
@@ -12,7 +12,7 @@
 PIECES = 8
 TILE = MAIN * PIECES
 RING = 4
-ORDER = (0, 1, 3, 2)
+BATCHES = ((0, 1), (3, 2))
 
 
 def split_matrix():
@@ -140,7 +140,6 @@
             bytes_accessed=2 * experts * MAIN * width,
             transcendentals=0,
         ),
-        compiler_params=pltpu.CompilerParams(vmem_limit_bytes=12 * 1024 * 1024),
         name="late_dispatch",
     )(pair, ids_t, tokens)
 
@@ -173,19 +172,16 @@
             bytes_accessed=2 * ring * chunks * MAIN * width,
             transcendentals=0,
         ),
-        compiler_params=pltpu.CompilerParams(vmem_limit_bytes=12 * 1024 * 1024),
         name="early_dispatch",
     )(pair, ids_t, tokens)
 
 
 def ffn_kernel(*refs):
-    late_hbm, (early_hbm, gate_hbm, up_hbm, down_hbm) = refs[:RING], refs[RING : RING + 4]
-    late_out, early_out = refs[RING + 4 : 2 * RING + 4], refs[2 * RING + 4]
-    late_in, early_in, gate_w, up_w, down_w, late_made, early_made, in_sems, out_sems = refs[
-        2 * RING + 5 :
-    ]
-    _, chunks, _, width = late_in.shape
-    model = gate_w.shape[0]
+    late_in, early_in, gate_w, up_w, down_w, late_made, early_made, in_sems, out_sems = refs[-9:]
+    places, chunks, _, width = late_in.shape
+    late_hbm, late_out, early_out = refs[:places], refs[places + 4 : -10], refs[-10]
+    early_hbm, gate_hbm, up_hbm, down_hbm = refs[places : places + 4]
+    model = gate_w.shape[1]
     half = model // 2
     main = chunks * MAIN
     last = 2 * chunks
@@ -202,14 +198,14 @@
         read(("late", j), late_hbm[j], late_in.at[j])
         read(("early", j), early_hbm.at[:, j], early_in.at[j])
 
-    read("gate_first", gate_hbm.at[0, first], gate_w.at[first])
-    read(("late", ORDER[0]), late_hbm[ORDER[0]], late_in.at[ORDER[0]])
-    read("up_first", up_hbm.at[0, first], up_w.at[first])
-    read(("early", ORDER[0]), early_hbm.at[:, ORDER[0]], early_in.at[ORDER[0]])
-    read("gate_second", gate_hbm.at[0, second], gate_w.at[second])
-    read("up_second", up_hbm.at[0, second], up_w.at[second])
+    read("gate_first", gate_hbm.at[0, :, first], gate_w.at[:, first])
+    read(("late", 0), late_hbm[0], late_in.at[0])
+    read("up_first", up_hbm.at[0, :, first], up_w.at[:, first])
+    read(("early", 0), early_hbm.at[:, 0], early_in.at[0])
+    read("gate_second", gate_hbm.at[0, :, second], gate_w.at[:, second])
+    read("up_second", up_hbm.at[0, :, second], up_w.at[:, second])
     read("down", down_hbm.at[0], down_w)
-    for j in ORDER[1:]:
+    for j in range(1, places):
         read_rows(j)
 
     waited = set()
@@ -229,21 +225,21 @@
     def half_expert(late, early, j=None):
         if j is not None:
             ready("gate_first", ("late", j))
-        gate = exact_dot(late(), gate_w[:half, :])
+        gate = exact_dot(late(), gate_w[:, :half], ((1,), (1,)))
         ready("up_first")
-        up = exact_dot(late(), up_w[:half, :])
+        up = exact_dot(late(), up_w[:, :half], ((1,), (1,)))
         if j is not None:
             ready(("early", j), "gate_second")
-        gate = gate + exact_dot(early(), gate_w[half:, :])
+        gate = gate + exact_dot(early(), gate_w[:, half:], ((1,), (1,)))
         ready("up_second")
-        up = up + exact_dot(early(), up_w[half:, :])
+        up = up + exact_dot(early(), up_w[:, half:], ((1,), (1,)))
         hidden = (gate / (1.0 + jnp.exp(-gate)) * up).astype(jnp.bfloat16)
         ready("down")
         late_value = exact_dot(hidden, down_w[:, :half]).astype(jnp.bfloat16)
         early_value = exact_dot(hidden, down_w[:, half:]).astype(jnp.bfloat16)
         return late_value, early_value
 
-    for j in ORDER:
+    for j in range(places):
         late_value, early_value = half_expert(
             lambda: late_in[j, :, :, :half].reshape(main, half),
             lambda: early_in[j, :, :, :half].reshape(main, half),
@@ -257,15 +253,15 @@
     matrix = split_matrix()
 
     def gather_last(buffer):
-        return pieces_to_rows(buffer[:, :, :, half:].reshape(RING * main, width - half), matrix)
+        return pieces_to_rows(buffer[:, :, :, half:].reshape(places * main, width - half), matrix)
 
     late_rows, early_rows = gather_last(late_in), gather_last(early_in)
     late_value, early_value = half_expert(lambda: late_rows, lambda: early_rows)
     for value, made in ((late_value, late_made), (early_value, early_made)):
-        for j in range(RING):
+        for j in range(places):
             pieces = rows_to_pieces(value[last * j : last * (j + 1)], matrix)
             made[j, :, :, half:] = pieces.reshape(chunks, MAIN, width - half)
-    for j in range(RING):
+    for j in range(places):
         write(late_made.at[j, :, :, tail], late_out[j].at[:, :, tail])
         write(early_made.at[j, :, :, tail], early_out.at[:, j, :, tail])
     for copy in writes:
@@ -273,27 +269,28 @@
 
 
 def half_ffn(late, early, w_gate, w_up, w_down):
+    places = len(late)
     chunks, _, width = late[0].shape
     model, hidden = w_gate.shape[1:]
-    rows = RING * chunks * CAP
+    rows = places * chunks * CAP
     outside = pl.BlockSpec(memory_space=pltpu.HBM)
-    buffer = pltpu.VMEM((RING, chunks, MAIN, width), jnp.bfloat16)
+    buffer = pltpu.VMEM((places, chunks, MAIN, width), jnp.bfloat16)
     late_shape = jax.ShapeDtypeStruct(late[0].shape, jnp.bfloat16)
     *late_out, early_out = pl.pallas_call(
         ffn_kernel,
-        in_specs=[outside] * (RING + 4),
-        out_specs=[outside] * (RING + 1),
-        out_shape=[late_shape] * RING + [jax.ShapeDtypeStruct(early.shape, jnp.bfloat16)],
+        in_specs=[outside] * (places + 4),
+        out_specs=[outside] * (places + 1),
+        out_shape=[late_shape] * places + [jax.ShapeDtypeStruct(early.shape, jnp.bfloat16)],
         scratch_shapes=[
             buffer,
             buffer,
-            pltpu.VMEM((model, hidden), jnp.bfloat16),
-            pltpu.VMEM((model, hidden), jnp.bfloat16),
+            pltpu.VMEM((hidden, model), jnp.bfloat16),
+            pltpu.VMEM((hidden, model), jnp.bfloat16),
             pltpu.VMEM((hidden, model), jnp.bfloat16),
             buffer,
             buffer,
-            pltpu.SemaphoreType.DMA((2 * RING + 5,)),
-            pltpu.SemaphoreType.DMA((4 * RING,)),
+            pltpu.SemaphoreType.DMA((2 * places + 5,)),
+            pltpu.SemaphoreType.DMA((4 * places,)),
         ],
         cost_estimate=pl.CostEstimate(
             flops=6 * rows * model * hidden,
@@ -302,7 +299,7 @@
         ),
         compiler_params=pltpu.CompilerParams(vmem_limit_bytes=56 * 1024 * 1024),
         name="half_ffn",
-    )(*late, early, w_gate, w_up, w_down)
+    )(*late, early, w_gate.swapaxes(1, 2), w_up.swapaxes(1, 2), w_down)
     return late_out, early_out
 
 
@@ -414,8 +411,11 @@
     return lax.ppermute(array, "y", [(y, y ^ j) for y in range(RING)])
 
 
-def gather_ring(array):
-    return jnp.stack([array] + [across(array, j) for j in range(1, RING)])
+def at_places(array):
+    arrays = [array]
+    for j in range(1, RING):
+        arrays.append(across(array, j))
+    return arrays
 
 
 def plane_exchange(array):
@@ -437,24 +437,37 @@
     late = late.reshape(chunks, 2, MAIN, width)
     near, far = late[:, 0], late[:, 1]
 
-    routing = gather_ring(jnp.concatenate([ids_t.astype(jnp.bfloat16), gates_t], axis=0))
-    ids_ring = routing[:, :top].astype(jnp.int32)
-    gates_ring = routing[:, top:].astype(jnp.float32)
-    early = early_dispatch(pair, ids_ring, gather_ring(tokens[:, half:]), chunks)
-    early = plane_exchange(early.reshape(chunks, RING * MAIN, width))
-    early = early.reshape(chunks, RING, MAIN, width)
-
-    late_in = (near, across(near, 1), across(far, 2), across(far, 3))
-    late_out, early_out = half_ffn(late_in, early, w_gate, w_up, w_down)
-    late_back = [late_out[0]]
+    routing = at_places(jnp.concatenate([ids_t.astype(jnp.bfloat16), gates_t], axis=0))
+    tokens_at = at_places(tokens[:, half:])
+    late_in = [near]
     for j in range(1, RING):
-        late_back.append(across(late_out[j], j))
-    early_out = plane_exchange(early_out.reshape(chunks, RING * MAIN, width))
+        late_in.append(across(near if j == 1 else far, j))
+    late_back, parts = [None] * RING, [None] * RING
+    arrived, ids_ring, gates_ring = [], [], []
+    for batch, places in enumerate(BATCHES):
+        table = jnp.stack([routing[j] for j in places])
+        ids_ring.append(table[:, :top].astype(jnp.int32))
+        gates_ring.append(table[:, top:].astype(jnp.float32))
+        tokens_here = jnp.stack([tokens_at[j] for j in places])
+        early = early_dispatch(pair, ids_ring[batch], tokens_here, chunks)
+        early = plane_exchange(early.reshape(chunks, len(places) * MAIN, width))
+        arrived.append(early.reshape(chunks, len(places), MAIN, width))
+
+    early_back = []
+    for batch, places in enumerate(BATCHES):
+        late_out, early_out = half_ffn(
+            [late_in[j] for j in places], arrived[batch], w_gate, w_up, w_down
+        )
+        for j, rows in zip(places, late_out):
+            late_back[j] = across(rows, j) if j else rows
+        early_back.append(plane_exchange(early_out.reshape(chunks, -1, width)))
+
     late_back = plane_exchange(sum_halves(late_back).reshape(chunks, 2 * MAIN, width))
-    partial = early_combine(
-        pair, ids_ring, gates_ring, early_out.reshape(chunks, RING, MAIN, width)
-    )
-    parts = [partial[0]] + [across(partial[j], j) for j in range(1, RING)]
+    for batch, places in enumerate(BATCHES):
+        rows = early_back[batch].reshape(chunks, len(places), MAIN, width)
+        partial = early_combine(pair, ids_ring[batch], gates_ring[batch], rows)
+        for i, j in enumerate(places):
+            parts[j] = across(partial[i], j) if j else partial[i]
     return final_combine(
         pair, ids_t, gates_t.astype(jnp.float32), late_back.reshape(experts, MAIN, width), parts
     )

time: 246 us -> 321 us (1.30)
  waiting for transfers between devices: 130 us -> 188 us
  starting transfers between devices: 51.7 us -> 66.3 us
  local copies, waits for them, and re-layouts: 15.7 us -> 2.37 us
  Pallas kernels: 45.5 us -> 58.5 us
    ppermute x15, waiting for transfers between devices: 110 us -> 152 us  [across(): return lax.ppermute(array, 'y', [(y, y ^ j) for y in range(RING)])]
    all_to_all x4 -> x6, waiting for transfers between devices: 20.2 us -> 35.8 us  [plane_exchange(): return lax.all_to_all(array, PLANE, split_axis=0, concat_axis=0, tiled=True)]
    all_to_all x4 -> x6, starting transfers between devices: 33.2 us -> 46.3 us  [plane_exchange(): return lax.all_to_all(array, PLANE, split_axis=0, concat_axis=0, tiled=True)]
    unnamed x20 -> x22, local copies, waits for them, and re-layouts: 11.4 us -> 2.07 us
    pallas_call x1 -> x2, Pallas kernels: 30.3 us -> 37.5 us  [half_ffn(): pl.pallas_call(ffn_kernel, in_specs=[outside] * (places + 4), out_specs=[...]
    pallas_call x1 -> x2, Pallas kernels: 3.37 us -> 7.12 us  [early_dispatch(): pl.pallas_call(early_dispatch_kernel, grid=(ring,), in_specs=[pl.BlockSpe...]
  transfers between devices with their start and end apart: 19 -> 21, of which waited for: 10 -> 12; matrix products, arithmetic and copies ran while one was open for 5% -> 1% of each run, Pallas kernels for 4% -> 16%
where the time goes in v5:
time: 321 us; the launch traced here: 318 us
  waiting for transfers between devices  188 us (59%)
  starting transfers between devices  66.3 us (21%)
  Pallas kernels  58.5 us (18%)
    ppermute x15, waiting for transfers between devices, across(): return lax.ppermute(array, 'y', [(y, y ^ j) for y in range(RING)])  152 us
    all_to_all x6, starting transfers between devices, plane_exchange(): return lax.all_to_all(array, PLANE, split_axis=0, concat_axis=0, tiled=True)  46.3 us
    pallas_call x2, Pallas kernels, half_ffn(): pl.pallas_call(ffn_kernel, in_specs=[outside] * (places + 4), out_specs=[...  37.5 us
    all_to_all x6, waiting for transfers between devices, plane_exchange(): return lax.all_to_all(array, PLANE, split_axis=0, concat_axis=0, tiled=True)  35.8 us
    ppermute x15, starting transfers between devices, across(): return lax.ppermute(array, 'y', [(y, y ^ j) for y in range(RING)])  20 us
    pallas_call x2, Pallas kernels, early_dispatch(): pl.pallas_call(early_dispatch_kernel, grid=(ring,), in_specs=[pl.BlockSpe...  7.12 us
  transfers between devices with their start and end apart: 21, of which 12 were waited for; matrix products, arithmetic and copies ran while one was open for 1% of the time, Pallas kernels for 16%

profile of v5, /device:TPU:37, one launch (start us, length us, event | category | flops | bytes accessed | tf_op | source)
XLA Modules:
  0.0 318.0 jit_solution(16621315312981513340)
XLA Ops:
  0.0 4.1 %late_dispatch.1 = bf16[64,16,1152]{2,1,0:T(8,128)(2,1)} custom-call(s32[1]{0:T(128)} %bitcast.pair_ref, s32[6,128]{1,0:T(8,128)} %bitcast.46, bf16[128,2048]{1,0:T(8,128)(2,1)} %tokens_ref.1), custom_call_target="tpu_custom_call" | custom-call | flops 301989888 | bytes 2359296 | tf_op jit(solution)/shard_map/late_dispatch/pallas_call | solution.py:127
  4.1 8.4 %all-to-all-start = ((bf16[32,32,1152]{2,1,0:T(8,128)(2,1)}), bf16[32,32,1152]{2,1,0:T(8,128)(2,1)S(1)}, u32[]{:S(2)}, u32[]{:S(2)}) async-start(bf16[32,32,1152]{2,1,0:T(8,128)(2,1)} %bitcast.49), calls=%async_computation | async-start | bytes 4718592 | tf_op jit(solution)/shard_map/all_to_all | solution.py:422
  12.5 0.0 copy-done.5
  12.5 0.1 slice_bitcast_fusion.6
  12.6 2.8 collective-permute-start.8
  15.4 0.3 collective-permute-start.9
  15.8 0.0 copy-done.3
  15.8 2.0 collective-permute-start.6
  17.8 0.8 collective-permute-start.7
  18.6 8.7 %collective-permute-done.6 = bf16[12,128]{1,0:T(8,128)(2,1)S(1)} collective-permute-done((bf16[12,128]{1,0:T(8,128)(2,1)S(1)}, bf16[12,128]{1,0:T(8,128)(2,1)S(1)}, u32[]{:S(2)}, u32[]{:S(2)}) %collective-permute-start.6) | collective-permute-done | bytes 3104 | tf_op jit(solution)/shard_map/ppermute | solution.py:411
  27.3 0.0 collective-permute-done.7
  27.3 0.6 fusion.4
  27.9 0.0 collective-permute-done.8
  27.9 0.0 collective-permute-done.9
  27.9 0.8 pad_maximum_fusion.1.tokens_ref
  28.7 3.6 %early_dispatch.3 = bf16[32,2,16,1152]{3,2,1,0:T(8,128)(2,1)} custom-call(s32[1]{0:T(128)} %bitcast.pair_ref, s32[2,6,128]{2,1,0:T(8,128)} %get-tuple-element.26.ids_ref, bf16[2,128,1024]{2,1,0:T(8,128)(2,1)} %pad_maximum_fusion.1.tokens_ref), custom_call_target="tpu_custom_call" | custom-call | flops 301989888 | bytes 2359296 | tf_op jit(solution)/shard_map/early_dispatch/pallas_call | solution.py:160
  32.3 8.4 %all-to-all-done = bf16[32,32,1152]{2,1,0:T(8,128)(2,1)S(1)} async-done(((bf16[32,32,1152]{2,1,0:T(8,128)(2,1)}), bf16[32,32,1152]{2,1,0:T(8,128)(2,1)S(1)}, u32[]{:S(2)}, u32[]{:S(2)}) %all-to-all-start) | async-done | bytes 2359328 | tf_op jit(solution)/shard_map/all_to_all | solution.py:422
  40.7 6.9 %all-to-all-start.2 = ((bf16[32,32,1152]{2,1,0:T(8,128)(2,1)}), bf16[32,32,1152]{2,1,0:T(8,128)(2,1)}, u32[]{:S(2)}, u32[]{:S(2)}) async-start(bf16[32,32,1152]{2,1,0:T(8,128)(2,1)} %bitcast.50), calls=%async_computation.2 | async-start | bytes 4718592 | tf_op jit(solution)/shard_map/all_to_all | solution.py:422
  47.7 1.4 collective-permute-start.2
  49.0 0.2 collective-permute-start.1
  49.2 6.2 %collective-permute-done.1 = bf16[12,128]{1,0:T(8,128)(2,1)S(1)} collective-permute-done((bf16[12,128]{1,0:T(8,128)(2,1)S(1)}, bf16[12,128]{1,0:T(8,128)(2,1)S(1)}, u32[]{:S(2)}, u32[]{:S(2)}) %collective-permute-start.1) | collective-permute-done | bytes 3104 | tf_op jit(solution)/shard_map/ppermute | solution.py:411
  55.4 0.6 fusion.5
  56.0 0.0 collective-permute-done.2
  56.0 0.8 pad_maximum_fusion.tokens_ref
  56.8 3.5 %early_dispatch.2 = bf16[32,2,16,1152]{3,2,1,0:T(8,128)(2,1)} custom-call(s32[1]{0:T(128)} %bitcast.pair_ref, s32[2,6,128]{2,1,0:T(8,128)} %get-tuple-element.28.ids_ref, bf16[2,128,1024]{2,1,0:T(8,128)(2,1)} %pad_maximum_fusion.tokens_ref), custom_call_target="tpu_custom_call" | custom-call | flops 301989888 | bytes 2359296 | tf_op jit(solution)/shard_map/early_dispatch/pallas_call | solution.py:160
  60.4 15.5 %all-to-all-done.2 = bf16[32,32,1152]{2,1,0:T(8,128)(2,1)} async-done(((bf16[32,32,1152]{2,1,0:T(8,128)(2,1)}), bf16[32,32,1152]{2,1,0:T(8,128)(2,1)}, u32[]{:S(2)}, u32[]{:S(2)}) %all-to-all-start.2) | async-done | bytes 2359328 | tf_op jit(solution)/shard_map/all_to_all | solution.py:422
  75.9 6.9 %all-to-all-start.1 = ((bf16[32,32,1152]{2,1,0:T(8,128)(2,1)}), bf16[32,32,1152]{2,1,0:T(8,128)(2,1)}, u32[]{:S(2)}, u32[]{:S(2)}) async-start(bf16[32,32,1152]{2,1,0:T(8,128)(2,1)} %bitcast.51), calls=%async_computation.1 | async-start | bytes 4718592 | tf_op jit(solution)/shard_map/all_to_all | solution.py:422
  82.8 0.2 slice_bitcast_fusion
  83.0 0.0 copy-start.6
  83.0 3.0 collective-permute-start.5
  86.0 0.8 collective-permute-start.4
  86.8 25.0 %collective-permute-done.5.refs_1_ = bf16[32,16,1152]{2,1,0:T(8,128)(2,1)S(1)} collective-permute-done((bf16[32,16,1152]{2,1,0:T(8,128)(2,1)S(1)}, bf16[32,16,1152]{2,1,0:T(8,128)(2,1)S(1)}, u32[]{:S(2)}, u32[]{:S(2)}) %collective-permute-start.5) | collective-permute-done | bytes 1179680 | tf_op jit(solution)/shard_map/ppermute | solution.py:411
  111.8 26.0 %collective-permute-done.4.refs_0_ = bf16[32,16,1152]{2,1,0:T(8,128)(2,1)S(1)} collective-permute-done((bf16[32,16,1152]{2,1,0:T(8,128)(2,1)S(1)}, bf16[32,16,1152]{2,1,0:T(8,128)(2,1)S(1)}, u32[]{:S(2)}, u32[]{:S(2)}) %collective-permute-start.4) | collective-permute-done | bytes 1179680 | tf_op jit(solution)/shard_map/ppermute | solution.py:411
  137.8 1.0 copy-done.9
  138.8 18.8 %half_ffn.3 = (bf16[32,16,1152]{2,1,0:T(8,128)(2,1)}, bf16[32,16,1152]{2,1,0:T(8,128)(2,1)}, bf16[32,2,16,1152]{3,2,1,0:T(8,128)(2,1)}) custom-call(bf16[32,16,1152]{2,1,0:T(8,128)(2,1)} %copy-done.9, bf16[32,16,1152]{2,1,0:T(8,128)(2,1)} %copy-done.8, bf16[32,2,16,1152]{3,2,1,0:T(8,128)(2,1)} %bitcast.20.refs_2_, bf16[1,704,2048]{2,1,0:T(8,128)(2,1)} %bitcast.61, ...), custom_call_target="tpu_custom_call" | custom-call | flops 9965666304 | bytes 18087936 | tf_op jit(solution)/shard_map/half_ffn/pallas_call | solution.py:279
  157.6 0.0 all-to-all-done.1
  157.6 7.5 %all-to-all-start.5 = ((bf16[32,32,1152]{2,1,0:T(8,128)(2,1)}), bf16[32,32,1152]{2,1,0:T(8,128)(2,1)S(1)}, u32[]{:S(2)}, u32[]{:S(2)}) async-start(bf16[32,32,1152]{2,1,0:T(8,128)(2,1)} %bitcast.53), calls=%async_computation.5 | async-start | bytes 4718592 | tf_op jit(solution)/shard_map/all_to_all | solution.py:422
  165.1 1.6 collective-permute-start
  166.7 25.8 %collective-permute-done.refs_1_ = bf16[32,16,1152]{2,1,0:T(8,128)(2,1)S(1)} collective-permute-done((bf16[32,16,1152]{2,1,0:T(8,128)(2,1)S(1)}, bf16[32,16,1152]{2,1,0:T(8,128)(2,1)S(1)}, u32[]{:S(2)}, u32[]{:S(2)}) %collective-permute-start) | collective-permute-done | bytes 1179680 | tf_op jit(solution)/shard_map/ppermute | solution.py:411
  192.6 1.0 copy-done.10
  193.6 18.7 %half_ffn.2 = (bf16[32,16,1152]{2,1,0:T(8,128)(2,1)}, bf16[32,16,1152]{2,1,0:T(8,128)(2,1)}, bf16[32,2,16,1152]{3,2,1,0:T(8,128)(2,1)}) custom-call(bf16[32,16,1152]{2,1,0:T(8,128)(2,1)} %copy-done.6, bf16[32,16,1152]{2,1,0:T(8,128)(2,1)} %copy-done.10, bf16[32,2,16,1152]{3,2,1,0:T(8,128)(2,1)} %bitcast.11.refs_2_, bf16[1,704,2048]{2,1,0:T(8,128)(2,1)} %bitcast.62, ...), custom_call_target="tpu_custom_call" | custom-call | flops 9965666304 | bytes 18087936 | tf_op jit(solution)/shard_map/half_ffn/pallas_call | solution.py:279
  212.3 0.0 all-to-all-done.5
  212.3 0.0 copy-start
  212.3 8.4 %all-to-all-start.4 = ((bf16[32,32,1152]{2,1,0:T(8,128)(2,1)}), bf16[32,32,1152]{2,1,0:T(8,128)(2,1)}, u32[]{:S(2)}, u32[]{:S(2)}) async-start(bf16[32,32,1152]{2,1,0:T(8,128)(2,1)} %bitcast.52), calls=%async_computation.4 | async-start | bytes 4718592 | tf_op jit(solution)/shard_map/all_to_all | solution.py:422
  220.8 2.5 collective-permute-start.10
  223.3 1.2 collective-permute-start.11
  224.6 0.0 collective-permute-start.3
  224.6 25.2 %collective-permute-done.10.c_ref = bf16[32,16,1152]{2,1,0:T(8,128)(2,1)S(1)} collective-permute-done((bf16[32,16,1152]{2,1,0:T(8,128)(2,1)}, bf16[32,16,1152]{2,1,0:T(8,128)(2,1)S(1)}, u32[]{:S(2)}, u32[]{:S(2)}) %collective-permute-start.10) | collective-permute-done | bytes 1179680 | tf_op jit(solution)/shard_map/ppermute | solution.py:411
  249.8 26.0 %collective-permute-done.11.d_ref = bf16[32,16,1152]{2,1,0:T(8,128)(2,1)S(1)} collective-permute-done((bf16[32,16,1152]{2,1,0:T(8,128)(2,1)}, bf16[32,16,1152]{2,1,0:T(8,128)(2,1)S(1)}, u32[]{:S(2)}, u32[]{:S(2)}) %collective-permute-start.11) | collective-permute-done | bytes 1179680 | tf_op jit(solution)/shard_map/ppermute | solution.py:411
  275.8 0.0 collective-permute-done.3.b_ref
  275.8 0.0 copy-done
  275.8 2.0 sum_halves.1
  277.8 0.0 all-to-all-done.4
  277.8 8.1 %all-to-all-start.3 = ((bf16[32,32,1152]{2,1,0:T(8,128)(2,1)}), bf16[32,32,1152]{2,1,0:T(8,128)(2,1)}, u32[]{:S(2)}, u32[]{:S(2)}) async-start(bf16[32,32,1152]{2,1,0:T(8,128)(2,1)} %bitcast.21), calls=%async_computation.3 | async-start | bytes 4718592 | tf_op jit(solution)/shard_map/all_to_all | solution.py:422
  285.9 1.4 early_combine.3
  287.3 2.4 collective-permute-start.14
  289.7 0.3 collective-permute-start.13
  290.1 2.4 early_combine.2
  292.6 0.6 collective-permute-start.12
  293.2 8.6 %collective-permute-done.14.refs_3_ = bf16[128,1024]{1,0:T(8,128)(2,1)S(1)} collective-permute-done((bf16[128,1024]{1,0:T(8,128)(2,1)S(1)}, bf16[128,1024]{1,0:T(8,128)(2,1)S(1)}, u32[]{:S(2)}, u32[]{:S(2)}) %collective-permute-start.14) | collective-permute-done | bytes 262176 | tf_op jit(solution)/shard_map/ppermute | solution.py:411
  301.8 0.0 collective-permute-done.13.refs_2_
  301.8 0.4 collective-permute-done.12.refs_1_
  302.2 11.9 %all-to-all-done.3 = bf16[32,32,1152]{2,1,0:T(8,128)(2,1)} async-done(((bf16[32,32,1152]{2,1,0:T(8,128)(2,1)}), bf16[32,32,1152]{2,1,0:T(8,128)(2,1)}, u32[]{:S(2)}, u32[]{:S(2)}) %all-to-all-start.3) | async-done | bytes 2359328 | tf_op jit(solution)/shard_map/all_to_all | solution.py:422
  314.1 3.9 %final_combine.1 = bf16[128,2048]{1,0:T(8,128)(2,1)} custom-call(s32[1]{0:T(128)} %bitcast.pair_ref, s32[6,128]{1,0:T(8,128)S(1)} %bitcast.47, f32[6,128]{1,0:T(8,128)S(1)} %bitcast_convert_fusion.gates_ref, bf16[64,16,1152]{2,1,0:T(8,128)(2,1)} %bitcast.22.rows_ref, bf16[128,1024]{1,0:T(8,128)(2,1)S(1)} %get-tuple-element.22.refs_0_, ...), custom_call_target="tpu_custom_call" | custom-call | flops 301989888 | bytes 2359296 | tf_op jit(solution)/shard_map/final_combine/pallas_call | solution.py:391
  (20 shorter events, 0.1 us)
Async XLA Ops:
  4.1 8.4 %copy-start.5 = (bf16[128,2048]{1,0:T(8,128)(2,1)S(1)}, bf16[128,2048]{1,0:T(8,128)(2,1)}, u32[]{:S(2)}) copy-start(bf16[128,2048]{1,0:T(8,128)(2,1)} %tokens_ref.1) | copy-start | bytes 1572868
  4.1 11.7 %copy-start.3 = (s32[128,6]{0,1:T(8,128)S(1)}, s32[128,6]{0,1:T(8,128)}, u32[]{:S(2)}) copy-start(s32[128,6]{0,1:T(8,128)} %param.7) | copy-start | bytes 9220
  4.1 11.7 %copy-start.7 = (bf16[128,6]{0,1:T(8,128)(2,1)S(1)}, bf16[128,6]{0,1:T(8,128)(2,1)}, u32[]{:S(2)}) copy-start(bf16[128,6]{0,1:T(8,128)(2,1)} %param.8) | copy-start | bytes 4612
  4.1 36.6 %all-to-all-start = ((bf16[32,32,1152]{2,1,0:T(8,128)(2,1)}), bf16[32,32,1152]{2,1,0:T(8,128)(2,1)S(1)}, u32[]{:S(2)}, u32[]{:S(2)}) async-start(bf16[32,32,1152]{2,1,0:T(8,128)(2,1)} %bitcast.49), calls=%async_computation | async-start | bytes 4718592 | tf_op jit(solution)/shard_map/all_to_all | solution.py:422
  12.6 15.3 %collective-permute-start.8 = (bf16[128,1024]{1,0:T(8,128)(2,1)S(1)}, bf16[128,1024]{1,0:T(8,128)(2,1)S(1)}, u32[]{:S(2)}, u32[]{:S(2)}) collective-permute-start(bf16[128,1024]{1,0:T(8,128)(2,1)S(1)} %get-tuple-element.24), channel_id=1, source_target_pairs={{0,3},{1,2},{2,1},{3,0},{4,7},{5,6},{6,5},{7,4},{8,11},{9,10},{10,... | collective-permute-start | bytes 786440 | tf_op jit(solution)/shard_map/ppermute | solution.py:411
  15.4 12.5 %collective-permute-start.9 = (bf16[128,1024]{1,0:T(8,128)(2,1)S(1)}, bf16[128,1024]{1,0:T(8,128)(2,1)S(1)}, u32[]{:S(2)}, u32[]{:S(2)}) collective-permute-start(bf16[128,1024]{1,0:T(8,128)(2,1)S(1)} %get-tuple-element.24), channel_id=1, source_target_pairs={{0,2},{1,3},{2,0},{3,1},{4,6},{5,7},{6,4},{7,5},{8,10},{9,11},{10,... | collective-permute-start | bytes 786440 | tf_op jit(solution)/shard_map/ppermute | solution.py:411
  15.8 11.5 %collective-permute-start.6 = (bf16[12,128]{1,0:T(8,128)(2,1)S(1)}, bf16[12,128]{1,0:T(8,128)(2,1)S(1)}, u32[]{:S(2)}, u32[]{:S(2)}) collective-permute-start(bf16[12,128]{1,0:T(8,128)(2,1)S(1)} %get-tuple-element.29), channel_id=1, source_target_pairs={{0,3},{1,2},{2,1},{3,0},{4,7},{5,6},{6,5},{7,4},{8,11},{9,10},{10,... | collective-permute-start | bytes 9224 | tf_op jit(solution)/shard_map/ppermute | solution.py:411
  17.8 9.5 %collective-permute-start.7 = (bf16[12,128]{1,0:T(8,128)(2,1)S(1)}, bf16[12,128]{1,0:T(8,128)(2,1)S(1)}, u32[]{:S(2)}, u32[]{:S(2)}) collective-permute-start(bf16[12,128]{1,0:T(8,128)(2,1)S(1)} %get-tuple-element.29), channel_id=1, source_target_pairs={{0,2},{1,3},{2,0},{3,1},{4,6},{5,7},{6,4},{7,5},{8,10},{9,11},{10,... | collective-permute-start | bytes 9224 | tf_op jit(solution)/shard_map/ppermute | solution.py:411
  40.7 35.2 %all-to-all-start.2 = ((bf16[32,32,1152]{2,1,0:T(8,128)(2,1)}), bf16[32,32,1152]{2,1,0:T(8,128)(2,1)}, u32[]{:S(2)}, u32[]{:S(2)}) async-start(bf16[32,32,1152]{2,1,0:T(8,128)(2,1)} %bitcast.50), calls=%async_computation.2 | async-start | bytes 4718592 | tf_op jit(solution)/shard_map/all_to_all | solution.py:422
  47.7 8.3 %collective-permute-start.2 = (bf16[128,1024]{1,0:T(8,128)(2,1)S(1)}, bf16[128,1024]{1,0:T(8,128)(2,1)S(1)}, u32[]{:S(2)}, u32[]{:S(2)}) collective-permute-start(bf16[128,1024]{1,0:T(8,128)(2,1)S(1)} %get-tuple-element.24), channel_id=1, source_target_pairs={{0,1},{1,0},{2,3},{3,2},{4,5},{5,4},{6,7},{7,6},{8,9},{9,8},{10,11... | collective-permute-start | bytes 786440 | tf_op jit(solution)/shard_map/ppermute | solution.py:411
  49.0 6.4 %collective-permute-start.1 = (bf16[12,128]{1,0:T(8,128)(2,1)S(1)}, bf16[12,128]{1,0:T(8,128)(2,1)S(1)}, u32[]{:S(2)}, u32[]{:S(2)}) collective-permute-start(bf16[12,128]{1,0:T(8,128)(2,1)S(1)} %get-tuple-element.29), channel_id=1, source_target_pairs={{0,1},{1,0},{2,3},{3,2},{4,5},{5,4},{6,7},{7,6},{8,9},{9,8},{10,11... | collective-permute-start | bytes 9224 | tf_op jit(solution)/shard_map/ppermute | solution.py:411
  75.9 81.7 %all-to-all-start.1 = ((bf16[32,32,1152]{2,1,0:T(8,128)(2,1)}), bf16[32,32,1152]{2,1,0:T(8,128)(2,1)}, u32[]{:S(2)}, u32[]{:S(2)}) async-start(bf16[32,32,1152]{2,1,0:T(8,128)(2,1)} %bitcast.51), calls=%async_computation.1 | async-start | bytes 4718592 | tf_op jit(solution)/shard_map/all_to_all | solution.py:422
  83.0 82.1 %copy-start.6 = (bf16[32,16,1152]{2,1,0:T(8,128)(2,1)}, bf16[32,16,1152]{2,1,0:T(8,128)(2,1)S(1)}, u32[]{:S(2)}) copy-start(bf16[32,16,1152]{2,1,0:T(8,128)(2,1)S(1)} %get-tuple-element.18.refs_0_) | copy-start | bytes 3538948
  83.0 28.8 %collective-permute-start.5 = (bf16[32,16,1152]{2,1,0:T(8,128)(2,1)S(1)}, bf16[32,16,1152]{2,1,0:T(8,128)(2,1)S(1)}, u32[]{:S(2)}, u32[]{:S(2)}) collective-permute-start(bf16[32,16,1152]{2,1,0:T(8,128)(2,1)S(1)} %get-tuple-element.17), channel_id=1, source_target_pairs={{0,2},{1,3},{2,0},{3,1},{4,6},{5,7},{6,4},{7,5},{8,10},{9,11},{10,... | collective-permute-start | bytes 3538952 | tf_op jit(solution)/shard_map/ppermute | solution.py:411
  86.0 51.8 %collective-permute-start.4 = (bf16[32,16,1152]{2,1,0:T(8,128)(2,1)S(1)}, bf16[32,16,1152]{2,1,0:T(8,128)(2,1)S(1)}, u32[]{:S(2)}, u32[]{:S(2)}) collective-permute-start(bf16[32,16,1152]{2,1,0:T(8,128)(2,1)S(1)} %get-tuple-element.17), channel_id=1, source_target_pairs={{0,3},{1,2},{2,1},{3,0},{4,7},{5,6},{6,5},{7,4},{8,11},{9,10},{10,... | collective-permute-start | bytes 3538952 | tf_op jit(solution)/shard_map/ppermute | solution.py:411
  111.8 26.0 %copy-start.8 = (bf16[32,16,1152]{2,1,0:T(8,128)(2,1)}, bf16[32,16,1152]{2,1,0:T(8,128)(2,1)S(1)}, u32[]{:S(2)}) copy-start(bf16[32,16,1152]{2,1,0:T(8,128)(2,1)S(1)} %collective-permute-done.5.refs_1_) | copy-start | bytes 3538948
  137.8 1.0 copy-start.9
  157.6 54.7 %all-to-all-start.5 = ((bf16[32,32,1152]{2,1,0:T(8,128)(2,1)}), bf16[32,32,1152]{2,1,0:T(8,128)(2,1)S(1)}, u32[]{:S(2)}, u32[]{:S(2)}) async-start(bf16[32,32,1152]{2,1,0:T(8,128)(2,1)} %bitcast.53), calls=%async_computation.5 | async-start | bytes 4718592 | tf_op jit(solution)/shard_map/all_to_all | solution.py:422
  165.1 27.4 %collective-permute-start = (bf16[32,16,1152]{2,1,0:T(8,128)(2,1)S(1)}, bf16[32,16,1152]{2,1,0:T(8,128)(2,1)S(1)}, u32[]{:S(2)}, u32[]{:S(2)}) collective-permute-start(bf16[32,16,1152]{2,1,0:T(8,128)(2,1)S(1)} %get-tuple-element.18.refs_0_), channel_id=1, source_target_pairs={{0,1},{1,0},{2,3},{3,2},{4,5},{5,4},{6,7},{7,6},{8,9},{9,8},{10,11... | collective-permute-start | bytes 3538952 | tf_op jit(solution)/shard_map/ppermute | solution.py:411
  192.5 1.0 copy-start.10
  212.3 63.4 %copy-start = (bf16[32,16,1152]{2,1,0:T(8,128)(2,1)S(1)}, bf16[32,16,1152]{2,1,0:T(8,128)(2,1)}, u32[]{:S(2)}) copy-start(bf16[32,16,1152]{2,1,0:T(8,128)(2,1)} %get-tuple-element.11.a_ref) | copy-start | bytes 3538948
  212.3 65.5 %all-to-all-start.4 = ((bf16[32,32,1152]{2,1,0:T(8,128)(2,1)}), bf16[32,32,1152]{2,1,0:T(8,128)(2,1)}, u32[]{:S(2)}, u32[]{:S(2)}) async-start(bf16[32,32,1152]{2,1,0:T(8,128)(2,1)} %bitcast.52), calls=%async_computation.4 | async-start | bytes 4718592 | tf_op jit(solution)/shard_map/all_to_all | solution.py:422
  220.8 29.0 %collective-permute-start.10 = (bf16[32,16,1152]{2,1,0:T(8,128)(2,1)}, bf16[32,16,1152]{2,1,0:T(8,128)(2,1)S(1)}, u32[]{:S(2)}, u32[]{:S(2)}) collective-permute-start(bf16[32,16,1152]{2,1,0:T(8,128)(2,1)} %get-tuple-element.13), channel_id=1, source_target_pairs={{0,2},{1,3},{2,0},{3,1},{4,6},{5,7},{6,4},{7,5},{8,10},{9,11},{10,... | collective-permute-start | bytes 3538952 | tf_op jit(solution)/shard_map/ppermute | solution.py:411
  223.3 52.4 %collective-permute-start.11 = (bf16[32,16,1152]{2,1,0:T(8,128)(2,1)}, bf16[32,16,1152]{2,1,0:T(8,128)(2,1)S(1)}, u32[]{:S(2)}, u32[]{:S(2)}) collective-permute-start(bf16[32,16,1152]{2,1,0:T(8,128)(2,1)} %get-tuple-element.14), channel_id=1, source_target_pairs={{0,3},{1,2},{2,1},{3,0},{4,7},{5,6},{6,5},{7,4},{8,11},{9,10},{10,... | collective-permute-start | bytes 3538952 | tf_op jit(solution)/shard_map/ppermute | solution.py:411
  224.6 51.2 %collective-permute-start.3 = (bf16[32,16,1152]{2,1,0:T(8,128)(2,1)}, bf16[32,16,1152]{2,1,0:T(8,128)(2,1)S(1)}, u32[]{:S(2)}, u32[]{:S(2)}) collective-permute-start(bf16[32,16,1152]{2,1,0:T(8,128)(2,1)} %get-tuple-element.12), channel_id=1, source_target_pairs={{0,1},{1,0},{2,3},{3,2},{4,5},{5,4},{6,7},{7,6},{8,9},{9,8},{10,11... | collective-permute-start | bytes 3538952 | tf_op jit(solution)/shard_map/ppermute | solution.py:411
  277.8 8.1 %copy-start.1 = (s32[2,6,128]{2,1,0:T(8,128)S(1)}, s32[2,6,128]{2,1,0:T(8,128)}, u32[]{:S(2)}) copy-start(s32[2,6,128]{2,1,0:T(8,128)} %get-tuple-element.26.ids_ref) | copy-start | bytes 18436
  277.8 36.3 %all-to-all-start.3 = ((bf16[32,32,1152]{2,1,0:T(8,128)(2,1)}), bf16[32,32,1152]{2,1,0:T(8,128)(2,1)}, u32[]{:S(2)}, u32[]{:S(2)}) async-start(bf16[32,32,1152]{2,1,0:T(8,128)(2,1)} %bitcast.21), calls=%async_computation.3 | async-start | bytes 4718592 | tf_op jit(solution)/shard_map/all_to_all | solution.py:422
  285.9 4.2 %copy-start.2 = (s32[2,6,128]{2,1,0:T(8,128)S(1)}, s32[2,6,128]{2,1,0:T(8,128)}, u32[]{:S(2)}) copy-start(s32[2,6,128]{2,1,0:T(8,128)} %get-tuple-element.28.ids_ref) | copy-start | bytes 18436
  285.9 4.2 %copy-start.4 = (f32[2,6,128]{2,1,0:T(8,128)S(1)}, f32[2,6,128]{2,1,0:T(8,128)}, u32[]{:S(2)}) copy-start(f32[2,6,128]{2,1,0:T(8,128)} %get-tuple-element.27.gates_ref) | copy-start | bytes 18436
  287.3 14.5 %collective-permute-start.14 = (bf16[128,1024]{1,0:T(8,128)(2,1)S(1)}, bf16[128,1024]{1,0:T(8,128)(2,1)S(1)}, u32[]{:S(2)}, u32[]{:S(2)}) collective-permute-start(bf16[128,1024]{1,0:T(8,128)(2,1)S(1)} %get-tuple-element.19), channel_id=1, source_target_pairs={{0,3},{1,2},{2,1},{3,0},{4,7},{5,6},{6,5},{7,4},{8,11},{9,10},{10,... | collective-permute-start | bytes 786440 | tf_op jit(solution)/shard_map/ppermute | solution.py:411
  289.7 12.1 %collective-permute-start.13 = (bf16[128,1024]{1,0:T(8,128)(2,1)S(1)}, bf16[128,1024]{1,0:T(8,128)(2,1)S(1)}, u32[]{:S(2)}, u32[]{:S(2)}) collective-permute-start(bf16[128,1024]{1,0:T(8,128)(2,1)S(1)} %get-tuple-element.20), channel_id=1, source_target_pairs={{0,2},{1,3},{2,0},{3,1},{4,6},{5,7},{6,4},{7,5},{8,10},{9,11},{10,... | collective-permute-start | bytes 786440 | tf_op jit(solution)/shard_map/ppermute | solution.py:411
  292.6 9.6 %collective-permute-start.12 = (bf16[128,1024]{1,0:T(8,128)(2,1)S(1)}, bf16[128,1024]{1,0:T(8,128)(2,1)S(1)}, u32[]{:S(2)}, u32[]{:S(2)}) collective-permute-start(bf16[128,1024]{1,0:T(8,128)(2,1)S(1)} %get-tuple-element.21), channel_id=1, source_target_pairs={{0,1},{1,0},{2,3},{3,2},{4,5},{5,4},{6,7},{7,6},{8,9},{9,8},{10,11... | collective-permute-start | bytes 786440 | tf_op jit(solution)/shard_map/ppermute | solution.py:411

commit v6 on v5

--- a/solution.py
+++ b/solution.py
@@ -12,7 +12,7 @@
 PIECES = 8
 TILE = MAIN * PIECES
 RING = 4
-BATCHES = ((0, 1), (3, 2))
+BATCHES = ((1, 3), (0, 2))
 
 
 def split_matrix():
@@ -297,7 +297,7 @@
             bytes_accessed=4 * rows * model + 6 * model * hidden,
             transcendentals=rows * hidden,
         ),
-        compiler_params=pltpu.CompilerParams(vmem_limit_bytes=56 * 1024 * 1024),
+        compiler_params=pltpu.CompilerParams(vmem_limit_bytes=62 * 1024 * 1024),
         name="half_ffn",
     )(*late, early, w_gate.swapaxes(1, 2), w_up.swapaxes(1, 2), w_down)
     return late_out, early_out
@@ -357,7 +357,6 @@
             bytes_accessed=2 * ring * chunks * MAIN * width,
             transcendentals=0,
         ),
-        compiler_params=pltpu.CompilerParams(vmem_limit_bytes=12 * 1024 * 1024),
         name="early_combine",
     )(pair, ids_t, gates_t, rows)
 

time: 321 us -> 298 us (0.928)
  waiting for transfers between devices: 188 us -> 159 us
  local copies, waits for them, and re-layouts: 2.37 us -> 7.29 us
    ppermute x15, waiting for transfers between devices: 152 us -> 124 us  [across(): return lax.ppermute(array, 'y', [(y, y ^ j) for y in range(RING)])]
  transfers between devices with their start and end apart: 21 -> 21, of which waited for: 12 -> 14; matrix products, arithmetic and copies ran while one was open for 1% -> 2% of each run, Pallas kernels for 16% -> 18%
where the time goes in v6:
time: 298 us; the launch traced here: 295 us
  waiting for transfers between devices  159 us (53%)
  starting transfers between devices  66.4 us (22%)
  Pallas kernels  59.3 us (20%)
  local copies, waits for them, and re-layouts  7.29 us (2%)
    ppermute x15, waiting for transfers between devices, across(): return lax.ppermute(array, 'y', [(y, y ^ j) for y in range(RING)])  124 us
    all_to_all x6, starting transfers between devices, plane_exchange(): return lax.all_to_all(array, PLANE, split_axis=0, concat_axis=0, tiled=True)  46.9 us
    pallas_call x2, Pallas kernels, half_ffn(): pl.pallas_call(ffn_kernel, in_specs=[outside] * (places + 4), out_specs=[...  37.6 us
    all_to_all x6, waiting for transfers between devices, plane_exchange(): return lax.all_to_all(array, PLANE, split_axis=0, concat_axis=0, tiled=True)  35.3 us
    ppermute x15, starting transfers between devices, across(): return lax.ppermute(array, 'y', [(y, y ^ j) for y in range(RING)])  19.5 us
    pallas_call x2, Pallas kernels, early_dispatch(): pl.pallas_call(early_dispatch_kernel, grid=(ring,), in_specs=[pl.BlockSpe...  7.14 us
    pallas_call x2, Pallas kernels, early_combine(): pl.pallas_call(early_combine_kernel, grid=(ring,), in_specs=[pl.BlockSpec...  6.25 us
  transfers between devices with their start and end apart: 21, of which 14 were waited for; matrix products, arithmetic and copies ran while one was open for 2% of the time, Pallas kernels for 18%

profile of v6, /device:TPU:37, one launch (start us, length us, event | category | flops | bytes accessed | tf_op | source)
XLA Modules:
  0.0 295.1 jit_solution(14041952952621763044)
XLA Ops:
  0.0 4.1 %late_dispatch.1 = bf16[64,16,1152]{2,1,0:T(8,128)(2,1)} custom-call(s32[1]{0:T(128)} %bitcast.pair_ref, s32[6,128]{1,0:T(8,128)} %bitcast.46, bf16[128,2048]{1,0:T(8,128)(2,1)} %tokens_ref.1), custom_call_target="tpu_custom_call" | custom-call | flops 301989888 | bytes 2359296 | tf_op jit(solution)/shard_map/late_dispatch/pallas_call | solution.py:127
  4.1 8.4 %all-to-all-start = ((bf16[32,32,1152]{2,1,0:T(8,128)(2,1)}), bf16[32,32,1152]{2,1,0:T(8,128)(2,1)S(1)}, u32[]{:S(2)}, u32[]{:S(2)}) async-start(bf16[32,32,1152]{2,1,0:T(8,128)(2,1)} %bitcast.50), calls=%async_computation | async-start | bytes 4718592 | tf_op jit(solution)/shard_map/all_to_all | solution.py:421
  12.6 0.0 copy-done.2
  12.6 0.1 slice_bitcast_fusion.6
  12.6 3.0 %collective-permute-start.2 = (bf16[128,1024]{1,0:T(8,128)(2,1)S(1)}, bf16[128,1024]{1,0:T(8,128)(2,1)S(1)}, u32[]{:S(2)}, u32[]{:S(2)}) collective-permute-start(bf16[128,1024]{1,0:T(8,128)(2,1)S(1)} %get-tuple-element.24), channel_id=1, source_target_pairs={{0,2},{1,3},{2,0},{3,1},{4,6},{5,7},{6,4},{7,5},{8,10},{9,11},{10,... | collective-permute-start | bytes 786440 | tf_op jit(solution)/shard_map/ppermute | solution.py:410
  15.7 0.1 collective-permute-start.1
  15.8 6.0 %collective-permute-done.1 = bf16[12,128]{1,0:T(8,128)(2,1)S(1)} collective-permute-done((bf16[12,128]{1,0:T(8,128)(2,1)S(1)}, bf16[12,128]{1,0:T(8,128)(2,1)S(1)}, u32[]{:S(2)}, u32[]{:S(2)}) %collective-permute-start.1) | collective-permute-done | bytes 3104 | tf_op jit(solution)/shard_map/ppermute | solution.py:410
  21.8 0.6 fusion.5
  22.4 0.0 collective-permute-done.2
  22.4 0.8 pad_maximum_fusion.tokens_ref
  23.2 3.6 %early_dispatch.2 = bf16[32,2,16,1152]{3,2,1,0:T(8,128)(2,1)} custom-call(s32[1]{0:T(128)} %bitcast.pair_ref, s32[2,6,128]{2,1,0:T(8,128)} %get-tuple-element.28.ids_ref, bf16[2,128,1024]{2,1,0:T(8,128)(2,1)} %pad_maximum_fusion.tokens_ref), custom_call_target="tpu_custom_call" | custom-call | flops 301989888 | bytes 2359296 | tf_op jit(solution)/shard_map/early_dispatch/pallas_call | solution.py:160
  26.8 13.9 %all-to-all-done = bf16[32,32,1152]{2,1,0:T(8,128)(2,1)S(1)} async-done(((bf16[32,32,1152]{2,1,0:T(8,128)(2,1)}), bf16[32,32,1152]{2,1,0:T(8,128)(2,1)S(1)}, u32[]{:S(2)}, u32[]{:S(2)}) %all-to-all-start) | async-done | bytes 2359328 | tf_op jit(solution)/shard_map/all_to_all | solution.py:421
  40.7 6.9 %all-to-all-start.1 = ((bf16[32,32,1152]{2,1,0:T(8,128)(2,1)}), bf16[32,32,1152]{2,1,0:T(8,128)(2,1)}, u32[]{:S(2)}, u32[]{:S(2)}) async-start(bf16[32,32,1152]{2,1,0:T(8,128)(2,1)} %bitcast.49), calls=%async_computation.1 | async-start | bytes 4718592 | tf_op jit(solution)/shard_map/all_to_all | solution.py:421
  47.7 1.4 collective-permute-start.7
  49.1 1.9 collective-permute-start.8
  51.0 0.4 collective-permute-start.5
  51.4 0.6 collective-permute-start.6
  52.0 3.5 %collective-permute-done.5 = bf16[12,128]{1,0:T(8,128)(2,1)S(1)} collective-permute-done((bf16[12,128]{1,0:T(8,128)(2,1)S(1)}, bf16[12,128]{1,0:T(8,128)(2,1)S(1)}, u32[]{:S(2)}, u32[]{:S(2)}) %collective-permute-start.5) | collective-permute-done | bytes 3104 | tf_op jit(solution)/shard_map/ppermute | solution.py:410
  55.4 2.2 collective-permute-done.6
  57.7 0.6 fusion.4
  58.3 0.0 collective-permute-done.7
  58.3 0.0 collective-permute-done.8
  58.3 0.8 pad_maximum_fusion.1.tokens_ref
  59.1 3.5 %early_dispatch.3 = bf16[32,2,16,1152]{3,2,1,0:T(8,128)(2,1)} custom-call(s32[1]{0:T(128)} %bitcast.pair_ref, s32[2,6,128]{2,1,0:T(8,128)} %get-tuple-element.26.ids_ref, bf16[2,128,1024]{2,1,0:T(8,128)(2,1)} %pad_maximum_fusion.1.tokens_ref), custom_call_target="tpu_custom_call" | custom-call | flops 301989888 | bytes 2359296 | tf_op jit(solution)/shard_map/early_dispatch/pallas_call | solution.py:160
  62.7 13.3 %all-to-all-done.1 = bf16[32,32,1152]{2,1,0:T(8,128)(2,1)} async-done(((bf16[32,32,1152]{2,1,0:T(8,128)(2,1)}), bf16[32,32,1152]{2,1,0:T(8,128)(2,1)}, u32[]{:S(2)}, u32[]{:S(2)}) %all-to-all-start.1) | async-done | bytes 2359328 | tf_op jit(solution)/shard_map/all_to_all | solution.py:421
  75.9 6.9 %all-to-all-start.2 = ((bf16[32,32,1152]{2,1,0:T(8,128)(2,1)}), bf16[32,32,1152]{2,1,0:T(8,128)(2,1)}, u32[]{:S(2)}, u32[]{:S(2)}) async-start(bf16[32,32,1152]{2,1,0:T(8,128)(2,1)} %bitcast.51), calls=%async_computation.2 | async-start | bytes 4718592 | tf_op jit(solution)/shard_map/all_to_all | solution.py:421
  82.9 1.3 slice_bitcast_fusion
  84.1 1.0 copy-done.4
  85.2 2.9 collective-permute-start
  88.1 25.7 %collective-permute-done.refs_1_ = bf16[32,16,1152]{2,1,0:T(8,128)(2,1)S(1)} collective-permute-done((bf16[32,16,1152]{2,1,0:T(8,128)(2,1)S(1)}, bf16[32,16,1152]{2,1,0:T(8,128)(2,1)S(1)}, u32[]{:S(2)}, u32[]{:S(2)}) %collective-permute-start) | collective-permute-done | bytes 1179680 | tf_op jit(solution)/shard_map/ppermute | solution.py:410
  113.8 1.0 copy-done.10
  114.8 18.8 %half_ffn.2 = (bf16[32,16,1152]{2,1,0:T(8,128)(2,1)}, bf16[32,16,1152]{2,1,0:T(8,128)(2,1)}, bf16[32,2,16,1152]{3,2,1,0:T(8,128)(2,1)}) custom-call(bf16[32,16,1152]{2,1,0:T(8,128)(2,1)} %get-tuple-element.18.refs_0_, bf16[32,16,1152]{2,1,0:T(8,128)(2,1)} %copy-done.10, bf16[32,2,16,1152]{3,2,1,0:T(8,128)(2,1)} %bitcast.12.refs_2_, ...), custom_call_target="tpu_custom_call" | custom-call | flops 9965666304 | bytes 18087936 | tf_op jit(solution)/shard_map/half_ffn/pallas_call | solution.py:279
  133.6 0.0 all-to-all-done.2
  133.6 0.0 copy-start.5
  133.7 8.4 %all-to-all-start.4 = ((bf16[32,32,1152]{2,1,0:T(8,128)(2,1)}), bf16[32,32,1152]{2,1,0:T(8,128)(2,1)}, u32[]{:S(2)}, u32[]{:S(2)}) async-start(bf16[32,32,1152]{2,1,0:T(8,128)(2,1)} %bitcast.53), calls=%async_computation.4 | async-start | bytes 4718592 | tf_op jit(solution)/shard_map/all_to_all | solution.py:421
  142.1 2.8 collective-permute-start.4
  144.9 0.0 collective-permute-start.3
  144.9 25.7 %collective-permute-done.4.refs_1_ = bf16[32,16,1152]{2,1,0:T(8,128)(2,1)S(1)} collective-permute-done((bf16[32,16,1152]{2,1,0:T(8,128)(2,1)S(1)}, bf16[32,16,1152]{2,1,0:T(8,128)(2,1)S(1)}, u32[]{:S(2)}, u32[]{:S(2)}) %collective-permute-start.4) | collective-permute-done | bytes 1179680 | tf_op jit(solution)/shard_map/ppermute | solution.py:410
  170.7 1.1 collective-permute-done.3.refs_0_
  171.8 1.0 copy-done.9
  172.8 18.8 %half_ffn.3 = (bf16[32,16,1152]{2,1,0:T(8,128)(2,1)}, bf16[32,16,1152]{2,1,0:T(8,128)(2,1)}, bf16[32,2,16,1152]{3,2,1,0:T(8,128)(2,1)}) custom-call(bf16[32,16,1152]{2,1,0:T(8,128)(2,1)} %copy-done.9, bf16[32,16,1152]{2,1,0:T(8,128)(2,1)} %copy-done.8, bf16[32,2,16,1152]{3,2,1,0:T(8,128)(2,1)} %bitcast.20.refs_2_, bf16[1,704,2048]{2,1,0:T(8,128)(2,1)} %bitcast.62, ...), custom_call_target="tpu_custom_call" | custom-call | flops 9965666304 | bytes 18087936 | tf_op jit(solution)/shard_map/half_ffn/pallas_call | solution.py:279
  191.6 0.0 all-to-all-done.4
  191.6 8.7 %all-to-all-start.5 = ((bf16[32,32,1152]{2,1,0:T(8,128)(2,1)}), bf16[32,32,1152]{2,1,0:T(8,128)(2,1)}, u32[]{:S(2)}, u32[]{:S(2)}) async-start(bf16[32,32,1152]{2,1,0:T(8,128)(2,1)} %bitcast.52), calls=%async_computation.5 | async-start | bytes 4718592 | tf_op jit(solution)/shard_map/all_to_all | solution.py:421
  200.4 1.3 collective-permute-start.10
  201.7 1.6 collective-permute-start.9
  203.3 0.4 collective-permute-start.11
  203.7 25.4 %collective-permute-done.10.c_ref = bf16[32,16,1152]{2,1,0:T(8,128)(2,1)S(1)} collective-permute-done((bf16[32,16,1152]{2,1,0:T(8,128)(2,1)S(1)}, bf16[32,16,1152]{2,1,0:T(8,128)(2,1)S(1)}, u32[]{:S(2)}, u32[]{:S(2)}) %collective-permute-start.10) | collective-permute-done | bytes 1179680 | tf_op jit(solution)/shard_map/ppermute | solution.py:410
  229.1 25.1 %collective-permute-done.9.b_ref = bf16[32,16,1152]{2,1,0:T(8,128)(2,1)S(1)} collective-permute-done((bf16[32,16,1152]{2,1,0:T(8,128)(2,1)}, bf16[32,16,1152]{2,1,0:T(8,128)(2,1)S(1)}, u32[]{:S(2)}, u32[]{:S(2)}) %collective-permute-start.9) | collective-permute-done | bytes 1179680 | tf_op jit(solution)/shard_map/ppermute | solution.py:410
  254.3 0.9 collective-permute-done.11.d_ref
  255.1 2.0 sum_halves.1
  257.1 0.0 all-to-all-done.5
  257.1 7.5 %all-to-all-start.3 = ((bf16[32,32,1152]{2,1,0:T(8,128)(2,1)}), bf16[32,32,1152]{2,1,0:T(8,128)(2,1)S(1)}, u32[]{:S(2)}, u32[]{:S(2)}) async-start(bf16[32,32,1152]{2,1,0:T(8,128)(2,1)} %bitcast.21), calls=%async_computation.3 | async-start | bytes 4718592 | tf_op jit(solution)/shard_map/all_to_all | solution.py:421
  264.6 3.1 %early_combine.2 = bf16[2,128,1024]{2,1,0:T(8,128)(2,1)} custom-call(s32[1]{0:T(128)} %bitcast.pair_ref, s32[2,6,128]{2,1,0:T(8,128)} %get-tuple-element.28.ids_ref, f32[2,6,128]{2,1,0:T(8,128)} %get-tuple-element.27.gates_ref, bf16[32,2,16,1152]{3,2,1,0:T(8,128)(2,1)} %bitcast.24.rows_ref), custom_call_target="tpu_custom_call" | custom-call | flops 301989888 | bytes 2359296 | tf_op jit(solution)/shard_map/early_combine/pallas_call | solution.py:344
  267.7 1.8 slice_bitcast_fusion.3
  269.5 1.2 collective-permute-start.13
  270.7 3.1 %early_combine.3 = bf16[2,128,1024]{2,1,0:T(8,128)(2,1)} custom-call(s32[1]{0:T(128)} %bitcast.pair_ref, s32[2,6,128]{2,1,0:T(8,128)} %get-tuple-element.26.ids_ref, f32[2,6,128]{2,1,0:T(8,128)} %get-tuple-element.25.gates_ref, bf16[32,2,16,1152]{3,2,1,0:T(8,128)(2,1)} %bitcast.27.rows_ref), custom_call_target="tpu_custom_call" | custom-call | flops 301989888 | bytes 2359296 | tf_op jit(solution)/shard_map/early_combine/pallas_call | solution.py:344
  273.9 1.1 slice_bitcast_fusion.2
  274.9 1.3 collective-permute-start.14
  276.2 0.5 collective-permute-start.12
  276.7 2.0 collective-permute-done.13.refs_2_
  278.7 6.0 %collective-permute-done.14.refs_3_ = bf16[128,1024]{1,0:T(8,128)(2,1)S(1)} collective-permute-done((bf16[128,1024]{1,0:T(8,128)(2,1)S(1)}, bf16[128,1024]{1,0:T(8,128)(2,1)S(1)}, u32[]{:S(2)}, u32[]{:S(2)}) %collective-permute-start.14) | collective-permute-done | bytes 262176 | tf_op jit(solution)/shard_map/ppermute | solution.py:410
  284.7 0.0 collective-permute-done.12.refs_1_
  284.7 8.1 %all-to-all-done.3 = bf16[32,32,1152]{2,1,0:T(8,128)(2,1)S(1)} async-done(((bf16[32,32,1152]{2,1,0:T(8,128)(2,1)}), bf16[32,32,1152]{2,1,0:T(8,128)(2,1)S(1)}, u32[]{:S(2)}, u32[]{:S(2)}) %all-to-all-start.3) | async-done | bytes 2359328 | tf_op jit(solution)/shard_map/all_to_all | solution.py:421
  292.8 2.3 final_combine.1
  (20 shorter events, 0.0 us)
Async XLA Ops:
  4.1 8.4 %copy-start.2 = (bf16[128,2048]{1,0:T(8,128)(2,1)S(1)}, bf16[128,2048]{1,0:T(8,128)(2,1)}, u32[]{:S(2)}) copy-start(bf16[128,2048]{1,0:T(8,128)(2,1)} %tokens_ref.1) | copy-start | bytes 1572868
  4.1 11.5 %copy-start.1 = (s32[128,6]{0,1:T(8,128)S(1)}, s32[128,6]{0,1:T(8,128)}, u32[]{:S(2)}) copy-start(s32[128,6]{0,1:T(8,128)} %param.7) | copy-start | bytes 9220
  4.1 11.5 %copy-start.6 = (bf16[128,6]{0,1:T(8,128)(2,1)S(1)}, bf16[128,6]{0,1:T(8,128)(2,1)}, u32[]{:S(2)}) copy-start(bf16[128,6]{0,1:T(8,128)(2,1)} %param.8) | copy-start | bytes 4612
  4.1 36.6 %all-to-all-start = ((bf16[32,32,1152]{2,1,0:T(8,128)(2,1)}), bf16[32,32,1152]{2,1,0:T(8,128)(2,1)S(1)}, u32[]{:S(2)}, u32[]{:S(2)}) async-start(bf16[32,32,1152]{2,1,0:T(8,128)(2,1)} %bitcast.50), calls=%async_computation | async-start | bytes 4718592 | tf_op jit(solution)/shard_map/all_to_all | solution.py:421
  12.6 9.8 %collective-permute-start.2 = (bf16[128,1024]{1,0:T(8,128)(2,1)S(1)}, bf16[128,1024]{1,0:T(8,128)(2,1)S(1)}, u32[]{:S(2)}, u32[]{:S(2)}) collective-permute-start(bf16[128,1024]{1,0:T(8,128)(2,1)S(1)} %get-tuple-element.24), channel_id=1, source_target_pairs={{0,2},{1,3},{2,0},{3,1},{4,6},{5,7},{6,4},{7,5},{8,10},{9,11},{10,... | collective-permute-start | bytes 786440 | tf_op jit(solution)/shard_map/ppermute | solution.py:410
  15.7 6.1 %collective-permute-start.1 = (bf16[12,128]{1,0:T(8,128)(2,1)S(1)}, bf16[12,128]{1,0:T(8,128)(2,1)S(1)}, u32[]{:S(2)}, u32[]{:S(2)}) collective-permute-start(bf16[12,128]{1,0:T(8,128)(2,1)S(1)} %get-tuple-element.29), channel_id=1, source_target_pairs={{0,2},{1,3},{2,0},{3,1},{4,6},{5,7},{6,4},{7,5},{8,10},{9,11},{10,... | collective-permute-start | bytes 9224 | tf_op jit(solution)/shard_map/ppermute | solution.py:410
  40.7 35.2 %all-to-all-start.1 = ((bf16[32,32,1152]{2,1,0:T(8,128)(2,1)}), bf16[32,32,1152]{2,1,0:T(8,128)(2,1)}, u32[]{:S(2)}, u32[]{:S(2)}) async-start(bf16[32,32,1152]{2,1,0:T(8,128)(2,1)} %bitcast.49), calls=%async_computation.1 | async-start | bytes 4718592 | tf_op jit(solution)/shard_map/all_to_all | solution.py:421
  47.7 10.6 %collective-permute-start.7 = (bf16[128,1024]{1,0:T(8,128)(2,1)S(1)}, bf16[128,1024]{1,0:T(8,128)(2,1)S(1)}, u32[]{:S(2)}, u32[]{:S(2)}) collective-permute-start(bf16[128,1024]{1,0:T(8,128)(2,1)S(1)} %get-tuple-element.24), channel_id=1, source_target_pairs={{0,1},{1,0},{2,3},{3,2},{4,5},{5,4},{6,7},{7,6},{8,9},{9,8},{10,11... | collective-permute-start | bytes 786440 | tf_op jit(solution)/shard_map/ppermute | solution.py:410
  49.1 9.2 %collective-permute-start.8 = (bf16[128,1024]{1,0:T(8,128)(2,1)S(1)}, bf16[128,1024]{1,0:T(8,128)(2,1)S(1)}, u32[]{:S(2)}, u32[]{:S(2)}) collective-permute-start(bf16[128,1024]{1,0:T(8,128)(2,1)S(1)} %get-tuple-element.24), channel_id=1, source_target_pairs={{0,3},{1,2},{2,1},{3,0},{4,7},{5,6},{6,5},{7,4},{8,11},{9,10},{10,... | collective-permute-start | bytes 786440 | tf_op jit(solution)/shard_map/ppermute | solution.py:410
  51.0 4.5 %collective-permute-start.5 = (bf16[12,128]{1,0:T(8,128)(2,1)S(1)}, bf16[12,128]{1,0:T(8,128)(2,1)S(1)}, u32[]{:S(2)}, u32[]{:S(2)}) collective-permute-start(bf16[12,128]{1,0:T(8,128)(2,1)S(1)} %get-tuple-element.29), channel_id=1, source_target_pairs={{0,1},{1,0},{2,3},{3,2},{4,5},{5,4},{6,7},{7,6},{8,9},{9,8},{10,11... | collective-permute-start | bytes 9224 | tf_op jit(solution)/shard_map/ppermute | solution.py:410
  51.4 6.3 %collective-permute-start.6 = (bf16[12,128]{1,0:T(8,128)(2,1)S(1)}, bf16[12,128]{1,0:T(8,128)(2,1)S(1)}, u32[]{:S(2)}, u32[]{:S(2)}) collective-permute-start(bf16[12,128]{1,0:T(8,128)(2,1)S(1)} %get-tuple-element.29), channel_id=1, source_target_pairs={{0,3},{1,2},{2,1},{3,0},{4,7},{5,6},{6,5},{7,4},{8,11},{9,10},{10,... | collective-permute-start | bytes 9224 | tf_op jit(solution)/shard_map/ppermute | solution.py:410
  75.9 57.7 %all-to-all-start.2 = ((bf16[32,32,1152]{2,1,0:T(8,128)(2,1)}), bf16[32,32,1152]{2,1,0:T(8,128)(2,1)}, u32[]{:S(2)}, u32[]{:S(2)}) async-start(bf16[32,32,1152]{2,1,0:T(8,128)(2,1)} %bitcast.51), calls=%async_computation.2 | async-start | bytes 4718592 | tf_op jit(solution)/shard_map/all_to_all | solution.py:421
  84.1 1.0 copy-start.4
  85.2 28.6 %collective-permute-start = (bf16[32,16,1152]{2,1,0:T(8,128)(2,1)S(1)}, bf16[32,16,1152]{2,1,0:T(8,128)(2,1)S(1)}, u32[]{:S(2)}, u32[]{:S(2)}) collective-permute-start(bf16[32,16,1152]{2,1,0:T(8,128)(2,1)S(1)} %get-tuple-element.17), channel_id=1, source_target_pairs={{0,2},{1,3},{2,0},{3,1},{4,6},{5,7},{6,4},{7,5},{8,10},{9,11},{10,... | collective-permute-start | bytes 3538952 | tf_op jit(solution)/shard_map/ppermute | solution.py:410
  113.8 1.0 copy-start.10
  133.6 8.5 %copy-start.5 = (bf16[32,16,1152]{2,1,0:T(8,128)(2,1)S(1)}, bf16[32,16,1152]{2,1,0:T(8,128)(2,1)}, u32[]{:S(2)}) copy-start(bf16[32,16,1152]{2,1,0:T(8,128)(2,1)} %copy-done.4) | copy-start | bytes 3538948
  133.7 11.3 %copy-start.3 = (bf16[32,16,1152]{2,1,0:T(8,128)(2,1)S(1)}, bf16[32,16,1152]{2,1,0:T(8,128)(2,1)}, u32[]{:S(2)}) copy-start(bf16[32,16,1152]{2,1,0:T(8,128)(2,1)} %get-tuple-element.18.refs_0_) | copy-start | bytes 3538948
  133.7 57.9 %all-to-all-start.4 = ((bf16[32,32,1152]{2,1,0:T(8,128)(2,1)}), bf16[32,32,1152]{2,1,0:T(8,128)(2,1)}, u32[]{:S(2)}, u32[]{:S(2)}) async-start(bf16[32,32,1152]{2,1,0:T(8,128)(2,1)} %bitcast.53), calls=%async_computation.4 | async-start | bytes 4718592 | tf_op jit(solution)/shard_map/all_to_all | solution.py:421
  142.1 28.6 %collective-permute-start.4 = (bf16[32,16,1152]{2,1,0:T(8,128)(2,1)S(1)}, bf16[32,16,1152]{2,1,0:T(8,128)(2,1)S(1)}, u32[]{:S(2)}, u32[]{:S(2)}) collective-permute-start(bf16[32,16,1152]{2,1,0:T(8,128)(2,1)S(1)} %copy-done.5), channel_id=1, source_target_pairs={{0,3},{1,2},{2,1},{3,0},{4,7},{5,6},{6,5},{7,4},{8,11},{9,10},{10,... | collective-permute-start | bytes 3538952 | tf_op jit(solution)/shard_map/ppermute | solution.py:410
  144.9 26.9 %collective-permute-start.3 = (bf16[32,16,1152]{2,1,0:T(8,128)(2,1)S(1)}, bf16[32,16,1152]{2,1,0:T(8,128)(2,1)S(1)}, u32[]{:S(2)}, u32[]{:S(2)}) collective-permute-start(bf16[32,16,1152]{2,1,0:T(8,128)(2,1)S(1)} %copy-done.3), channel_id=1, source_target_pairs={{0,1},{1,0},{2,3},{3,2},{4,5},{5,4},{6,7},{7,6},{8,9},{9,8},{10,11... | collective-permute-start | bytes 3538952 | tf_op jit(solution)/shard_map/ppermute | solution.py:410
  170.7 1.1 copy-start.8
  171.8 1.0 copy-start.9
  191.6 8.8 %copy-start.7 = (bf16[32,16,1152]{2,1,0:T(8,128)(2,1)S(1)}, bf16[32,16,1152]{2,1,0:T(8,128)(2,1)}, u32[]{:S(2)}) copy-start(bf16[32,16,1152]{2,1,0:T(8,128)(2,1)} %get-tuple-element.13) | copy-start | bytes 3538948
  191.6 63.5 %copy-start = (bf16[32,16,1152]{2,1,0:T(8,128)(2,1)S(1)}, bf16[32,16,1152]{2,1,0:T(8,128)(2,1)}, u32[]{:S(2)}) copy-start(bf16[32,16,1152]{2,1,0:T(8,128)(2,1)} %get-tuple-element.11.a_ref) | copy-start | bytes 3538948
  191.6 65.5 %all-to-all-start.5 = ((bf16[32,32,1152]{2,1,0:T(8,128)(2,1)}), bf16[32,32,1152]{2,1,0:T(8,128)(2,1)}, u32[]{:S(2)}, u32[]{:S(2)}) async-start(bf16[32,32,1152]{2,1,0:T(8,128)(2,1)} %bitcast.52), calls=%async_computation.5 | async-start | bytes 4718592 | tf_op jit(solution)/shard_map/all_to_all | solution.py:421
  200.4 28.8 %collective-permute-start.10 = (bf16[32,16,1152]{2,1,0:T(8,128)(2,1)S(1)}, bf16[32,16,1152]{2,1,0:T(8,128)(2,1)S(1)}, u32[]{:S(2)}, u32[]{:S(2)}) collective-permute-start(bf16[32,16,1152]{2,1,0:T(8,128)(2,1)S(1)} %copy-done.7), channel_id=1, source_target_pairs={{0,2},{1,3},{2,0},{3,1},{4,6},{5,7},{6,4},{7,5},{8,10},{9,11},{10,... | collective-permute-start | bytes 3538952 | tf_op jit(solution)/shard_map/ppermute | solution.py:410
  201.7 52.6 %collective-permute-start.9 = (bf16[32,16,1152]{2,1,0:T(8,128)(2,1)}, bf16[32,16,1152]{2,1,0:T(8,128)(2,1)S(1)}, u32[]{:S(2)}, u32[]{:S(2)}) collective-permute-start(bf16[32,16,1152]{2,1,0:T(8,128)(2,1)} %get-tuple-element.12), channel_id=1, source_target_pairs={{0,1},{1,0},{2,3},{3,2},{4,5},{5,4},{6,7},{7,6},{8,9},{9,8},{10,11... | collective-permute-start | bytes 3538952 | tf_op jit(solution)/shard_map/ppermute | solution.py:410
  203.3 51.8 %collective-permute-start.11 = (bf16[32,16,1152]{2,1,0:T(8,128)(2,1)}, bf16[32,16,1152]{2,1,0:T(8,128)(2,1)S(1)}, u32[]{:S(2)}, u32[]{:S(2)}) collective-permute-start(bf16[32,16,1152]{2,1,0:T(8,128)(2,1)} %get-tuple-element.14), channel_id=1, source_target_pairs={{0,3},{1,2},{2,1},{3,0},{4,7},{5,6},{6,5},{7,4},{8,11},{9,10},{10,... | collective-permute-start | bytes 3538952 | tf_op jit(solution)/shard_map/ppermute | solution.py:410
  257.1 35.7 %all-to-all-start.3 = ((bf16[32,32,1152]{2,1,0:T(8,128)(2,1)}), bf16[32,32,1152]{2,1,0:T(8,128)(2,1)S(1)}, u32[]{:S(2)}, u32[]{:S(2)}) async-start(bf16[32,32,1152]{2,1,0:T(8,128)(2,1)} %bitcast.21), calls=%async_computation.3 | async-start | bytes 4718592 | tf_op jit(solution)/shard_map/all_to_all | solution.py:421
  269.5 9.2 %collective-permute-start.13 = (bf16[128,1024]{1,0:T(8,128)(2,1)}, bf16[128,1024]{1,0:T(8,128)(2,1)S(1)}, u32[]{:S(2)}, u32[]{:S(2)}) collective-permute-start(bf16[128,1024]{1,0:T(8,128)(2,1)} %get-tuple-element.21), channel_id=1, source_target_pairs={{0,2},{1,3},{2,0},{3,1},{4,6},{5,7},{6,4},{7,5},{8,10},{9,11},{10,... | collective-permute-start | bytes 786440 | tf_op jit(solution)/shard_map/ppermute | solution.py:410
  274.9 9.8 %collective-permute-start.14 = (bf16[128,1024]{1,0:T(8,128)(2,1)S(1)}, bf16[128,1024]{1,0:T(8,128)(2,1)S(1)}, u32[]{:S(2)}, u32[]{:S(2)}) collective-permute-start(bf16[128,1024]{1,0:T(8,128)(2,1)S(1)} %get-tuple-element.19), channel_id=1, source_target_pairs={{0,3},{1,2},{2,1},{3,0},{4,7},{5,6},{6,5},{7,4},{8,11},{9,10},{10,... | collective-permute-start | bytes 786440 | tf_op jit(solution)/shard_map/ppermute | solution.py:410
  276.2 8.5 %collective-permute-start.12 = (bf16[128,1024]{1,0:T(8,128)(2,1)S(1)}, bf16[128,1024]{1,0:T(8,128)(2,1)S(1)}, u32[]{:S(2)}, u32[]{:S(2)}) collective-permute-start(bf16[128,1024]{1,0:T(8,128)(2,1)S(1)} %get-tuple-element.20), channel_id=1, source_target_pairs={{0,1},{1,0},{2,3},{3,2},{4,5},{5,4},{6,7},{7,6},{8,9},{9,8},{10,11... | collective-permute-start | bytes 786440 | tf_op jit(solution)/shard_map/ppermute | solution.py:410

commit v7 on v6

--- a/solution.py
+++ b/solution.py
@@ -123,7 +123,7 @@
     count, model = tokens.shape
     half = model // 2
     width = half * CAP // MAIN
-    block = 16
+    block = 32
     return pl.pallas_call(
         late_dispatch_kernel,
         grid=(experts // block,),
@@ -362,21 +362,14 @@
 
 
 def final_kernel(pair_ref, ids_ref, gates_ref, rows_ref, *refs):
-    parts, (out_ref, slot_ref, weight_ref) = refs[:RING], refs[RING:]
+    parts, out_ref = refs[:RING], refs[RING]
     experts = rows_ref.shape[0]
     half = parts[0].shape[1]
-    block = 16
-    expert = near_first(*slot_ref.shape, pair_ref[0])
+    expert = near_first(experts, ids_ref.shape[1], pair_ref[0])
     slot, weight = slots_of(ids_ref[...], expert, gates_ref[...])
-    slot_ref[...] = slot
-    weight_ref[...] = weight
-    total = jnp.zeros((slot.shape[1], half), jnp.float32)
-    for first in range(0, experts, block):
-        here = slice(first, first + block)
-        main = rows_ref[here, :, :half].reshape(block * MAIN, half)
-        pieces = rows_ref[here, :, half:].reshape(block * MAIN, half // PIECES)
-        total += combine_rows(slot_ref[here, :], weight_ref[here, :], main, pieces)
-    out_ref[:, :half] = total.astype(jnp.bfloat16)
+    main = rows_ref[:, :, :half].reshape(experts * MAIN, half)
+    pieces = rows_ref[:, :, half:].reshape(experts * MAIN, half // PIECES)
+    out_ref[:, :half] = combine_rows(slot, weight, main, pieces).astype(jnp.bfloat16)
     total = parts[0][...].astype(jnp.float32)
     for part in parts[1:]:
         total += part[...].astype(jnp.float32)
@@ -392,10 +385,6 @@
         in_specs=[pl.BlockSpec(memory_space=pltpu.SMEM)] + [on_chip] * (3 + RING),
         out_specs=on_chip,
         out_shape=jax.ShapeDtypeStruct((count, 2 * half), jnp.bfloat16),
-        scratch_shapes=[
-            pltpu.VMEM((experts, count), jnp.float32),
-            pltpu.VMEM((experts, count), jnp.float32),
-        ],
         cost_estimate=pl.CostEstimate(
             flops=2 * experts * CAP * count * half,
             bytes_accessed=2 * experts * MAIN * width,
@@ -426,7 +415,7 @@
     experts = 2 * chunks
     top = expert_ids.shape[1]
     half = tokens.shape[1] // 2
-    pair = (lax.axis_index("y") // 2).astype(jnp.int32).reshape(1)
+    pair = (lax.axis_index("y") >> 1).astype(jnp.int32).reshape(1)
     ids_t = expert_ids.T
     gates_t = gate_weights.T
 

time: 298 us -> 296 us (level)
  no operation moved by 1% of the time
where the time goes in v7:
time: 296 us; the launch traced here: 293 us
  waiting for transfers between devices  159 us (54%)
  starting transfers between devices  66.5 us (22%)
  Pallas kernels  57.9 us (20%)
  local copies, waits for them, and re-layouts  6.22 us (2%)
    ppermute x15, waiting for transfers between devices, across(): return lax.ppermute(array, 'y', [(y, y ^ j) for y in range(RING)])  124 us
    all_to_all x6, starting transfers between devices, plane_exchange(): return lax.all_to_all(array, PLANE, split_axis=0, concat_axis=0, tiled=True)  47.1 us
    pallas_call x2, Pallas kernels, half_ffn(): pl.pallas_call(ffn_kernel, in_specs=[outside] * (places + 4), out_specs=[...  37.5 us
    all_to_all x6, waiting for transfers between devices, plane_exchange(): return lax.all_to_all(array, PLANE, split_axis=0, concat_axis=0, tiled=True)  35.4 us
    ppermute x15, starting transfers between devices, across(): return lax.ppermute(array, 'y', [(y, y ^ j) for y in range(RING)])  19.4 us
    pallas_call x2, Pallas kernels, early_dispatch(): pl.pallas_call(early_dispatch_kernel, grid=(ring,), in_specs=[pl.BlockSpe...  7.1 us
    pallas_call x2, Pallas kernels, early_combine(): pl.pallas_call(early_combine_kernel, grid=(ring,), in_specs=[pl.BlockSpec...  6.25 us
  transfers between devices with their start and end apart: 21, of which 14 were waited for; matrix products, arithmetic and copies ran while one was open for 2% of the time, Pallas kernels for 18%

profile of v7, /device:TPU:37, one launch (start us, length us, event | category | flops | bytes accessed | tf_op | source)
XLA Modules:
  0.0 292.8 jit_solution(1091824454139809081)
XLA Ops:
  0.0 3.4 %late_dispatch.1 = bf16[64,16,1152]{2,1,0:T(8,128)(2,1)} custom-call(s32[1]{0:T(128)} %bitcast.pair_ref, s32[6,128]{1,0:T(8,128)} %bitcast.46, bf16[128,2048]{1,0:T(8,128)(2,1)} %tokens_ref.1), custom_call_target="tpu_custom_call" | custom-call | flops 301989888 | bytes 2359296 | tf_op jit(solution)/shard_map/late_dispatch/pallas_call | solution.py:127
  3.4 8.4 %all-to-all-start = ((bf16[32,32,1152]{2,1,0:T(8,128)(2,1)}), bf16[32,32,1152]{2,1,0:T(8,128)(2,1)S(1)}, u32[]{:S(2)}, u32[]{:S(2)}) async-start(bf16[32,32,1152]{2,1,0:T(8,128)(2,1)} %bitcast.50), calls=%async_computation | async-start | bytes 4718592 | tf_op jit(solution)/shard_map/all_to_all | solution.py:410
  11.9 3.0 %collective-permute-start.2 = (bf16[128,1024]{1,0:T(8,128)(2,1)S(1)}, bf16[128,1024]{1,0:T(8,128)(2,1)S(1)}, u32[]{:S(2)}, u32[]{:S(2)}) collective-permute-start(bf16[128,1024]{1,0:T(8,128)(2,1)S(1)} %get-tuple-element.24), channel_id=1, source_target_pairs={{0,2},{1,3},{2,0},{3,1},{4,6},{5,7},{6,4},{7,5},{8,10},{9,11},{10,... | collective-permute-start | bytes 786440 | tf_op jit(solution)/shard_map/ppermute | solution.py:399
  14.9 0.0 copy-done.1
  14.9 0.1 collective-permute-start.1
  15.0 6.0 %collective-permute-done.1 = bf16[12,128]{1,0:T(8,128)(2,1)S(1)} collective-permute-done((bf16[12,128]{1,0:T(8,128)(2,1)S(1)}, bf16[12,128]{1,0:T(8,128)(2,1)S(1)}, u32[]{:S(2)}, u32[]{:S(2)}) %collective-permute-start.1) | collective-permute-done | bytes 3104 | tf_op jit(solution)/shard_map/ppermute | solution.py:399
  21.0 0.6 fusion.5
  21.6 0.0 collective-permute-done.2
  21.6 0.8 pad_maximum_fusion.tokens_ref
  22.5 3.5 %early_dispatch.2 = bf16[32,2,16,1152]{3,2,1,0:T(8,128)(2,1)} custom-call(s32[1]{0:T(128)} %bitcast.pair_ref, s32[2,6,128]{2,1,0:T(8,128)} %get-tuple-element.28.ids_ref, bf16[2,128,1024]{2,1,0:T(8,128)(2,1)} %pad_maximum_fusion.tokens_ref), custom_call_target="tpu_custom_call" | custom-call | flops 301989888 | bytes 2359296 | tf_op jit(solution)/shard_map/early_dispatch/pallas_call | solution.py:160
  26.0 14.0 %all-to-all-done = bf16[32,32,1152]{2,1,0:T(8,128)(2,1)S(1)} async-done(((bf16[32,32,1152]{2,1,0:T(8,128)(2,1)}), bf16[32,32,1152]{2,1,0:T(8,128)(2,1)S(1)}, u32[]{:S(2)}, u32[]{:S(2)}) %all-to-all-start) | async-done | bytes 2359328 | tf_op jit(solution)/shard_map/all_to_all | solution.py:410
  40.0 6.9 %all-to-all-start.1 = ((bf16[32,32,1152]{2,1,0:T(8,128)(2,1)}), bf16[32,32,1152]{2,1,0:T(8,128)(2,1)}, u32[]{:S(2)}, u32[]{:S(2)}) async-start(bf16[32,32,1152]{2,1,0:T(8,128)(2,1)} %bitcast.49), calls=%async_computation.1 | async-start | bytes 4718592 | tf_op jit(solution)/shard_map/all_to_all | solution.py:410
  46.9 1.4 collective-permute-start.7
  48.3 1.9 collective-permute-start.8
  50.2 0.4 collective-permute-start.5
  50.6 0.6 collective-permute-start.6
  51.2 3.5 %collective-permute-done.5 = bf16[12,128]{1,0:T(8,128)(2,1)S(1)} collective-permute-done((bf16[12,128]{1,0:T(8,128)(2,1)S(1)}, bf16[12,128]{1,0:T(8,128)(2,1)S(1)}, u32[]{:S(2)}, u32[]{:S(2)}) %collective-permute-start.5) | collective-permute-done | bytes 3104 | tf_op jit(solution)/shard_map/ppermute | solution.py:399
  54.7 2.2 collective-permute-done.6
  56.9 0.6 fusion.4
  57.5 0.0 collective-permute-done.7
  57.5 0.0 collective-permute-done.8
  57.5 0.8 pad_maximum_fusion.1.tokens_ref
  58.4 3.6 %early_dispatch.3 = bf16[32,2,16,1152]{3,2,1,0:T(8,128)(2,1)} custom-call(s32[1]{0:T(128)} %bitcast.pair_ref, s32[2,6,128]{2,1,0:T(8,128)} %get-tuple-element.26.ids_ref, bf16[2,128,1024]{2,1,0:T(8,128)(2,1)} %pad_maximum_fusion.1.tokens_ref), custom_call_target="tpu_custom_call" | custom-call | flops 301989888 | bytes 2359296 | tf_op jit(solution)/shard_map/early_dispatch/pallas_call | solution.py:160
  61.9 13.3 %all-to-all-done.1 = bf16[32,32,1152]{2,1,0:T(8,128)(2,1)} async-done(((bf16[32,32,1152]{2,1,0:T(8,128)(2,1)}), bf16[32,32,1152]{2,1,0:T(8,128)(2,1)}, u32[]{:S(2)}, u32[]{:S(2)}) %all-to-all-start.1) | async-done | bytes 2359328 | tf_op jit(solution)/shard_map/all_to_all | solution.py:410
  75.2 6.9 %all-to-all-start.2 = ((bf16[32,32,1152]{2,1,0:T(8,128)(2,1)}), bf16[32,32,1152]{2,1,0:T(8,128)(2,1)}, u32[]{:S(2)}, u32[]{:S(2)}) async-start(bf16[32,32,1152]{2,1,0:T(8,128)(2,1)} %bitcast.51), calls=%async_computation.2 | async-start | bytes 4718592 | tf_op jit(solution)/shard_map/all_to_all | solution.py:410
  82.1 1.3 slice_bitcast_fusion
  83.4 2.9 collective-permute-start
  86.3 25.7 %collective-permute-done.refs_1_ = bf16[32,16,1152]{2,1,0:T(8,128)(2,1)S(1)} collective-permute-done((bf16[32,16,1152]{2,1,0:T(8,128)(2,1)S(1)}, bf16[32,16,1152]{2,1,0:T(8,128)(2,1)S(1)}, u32[]{:S(2)}, u32[]{:S(2)}) %collective-permute-start) | collective-permute-done | bytes 1179680 | tf_op jit(solution)/shard_map/ppermute | solution.py:399
  112.0 1.0 copy-done.9
  113.1 18.8 %half_ffn.2 = (bf16[32,16,1152]{2,1,0:T(8,128)(2,1)}, bf16[32,16,1152]{2,1,0:T(8,128)(2,1)}, bf16[32,2,16,1152]{3,2,1,0:T(8,128)(2,1)}) custom-call(bf16[32,16,1152]{2,1,0:T(8,128)(2,1)} %get-tuple-element.18.refs_0_, bf16[32,16,1152]{2,1,0:T(8,128)(2,1)} %copy-done.9, bf16[32,2,16,1152]{3,2,1,0:T(8,128)(2,1)} %bitcast.12.refs_2_, ...), custom_call_target="tpu_custom_call" | custom-call | flops 9965666304 | bytes 18087936 | tf_op jit(solution)/shard_map/half_ffn/pallas_call | solution.py:279
  131.8 0.0 all-to-all-done.2
  131.9 8.4 %all-to-all-start.4 = ((bf16[32,32,1152]{2,1,0:T(8,128)(2,1)}), bf16[32,32,1152]{2,1,0:T(8,128)(2,1)}, u32[]{:S(2)}, u32[]{:S(2)}) async-start(bf16[32,32,1152]{2,1,0:T(8,128)(2,1)} %bitcast.53), calls=%async_computation.4 | async-start | bytes 4718592 | tf_op jit(solution)/shard_map/all_to_all | solution.py:410
  140.3 2.8 collective-permute-start.4
  143.1 0.0 collective-permute-start.3
  143.1 25.7 %collective-permute-done.4.refs_1_ = bf16[32,16,1152]{2,1,0:T(8,128)(2,1)S(1)} collective-permute-done((bf16[32,16,1152]{2,1,0:T(8,128)(2,1)S(1)}, bf16[32,16,1152]{2,1,0:T(8,128)(2,1)S(1)}, u32[]{:S(2)}, u32[]{:S(2)}) %collective-permute-start.4) | collective-permute-done | bytes 1179680 | tf_op jit(solution)/shard_map/ppermute | solution.py:399
  168.9 1.1 collective-permute-done.3.refs_0_
  170.0 1.0 copy-done.8
  171.0 18.7 %half_ffn.3 = (bf16[32,16,1152]{2,1,0:T(8,128)(2,1)}, bf16[32,16,1152]{2,1,0:T(8,128)(2,1)}, bf16[32,2,16,1152]{3,2,1,0:T(8,128)(2,1)}) custom-call(bf16[32,16,1152]{2,1,0:T(8,128)(2,1)} %copy-done.8, bf16[32,16,1152]{2,1,0:T(8,128)(2,1)} %copy-done.7, bf16[32,2,16,1152]{3,2,1,0:T(8,128)(2,1)} %bitcast.20.refs_2_, bf16[1,704,2048]{2,1,0:T(8,128)(2,1)} %bitcast.62, ...), custom_call_target="tpu_custom_call" | custom-call | flops 9965666304 | bytes 18087936 | tf_op jit(solution)/shard_map/half_ffn/pallas_call | solution.py:279
  189.8 0.0 all-to-all-done.4
  189.8 0.0 copy-start.5
  189.8 0.0 copy-start.6
  189.8 0.0 copy-start
  189.8 8.9 %all-to-all-start.5 = ((bf16[32,32,1152]{2,1,0:T(8,128)(2,1)}), bf16[32,32,1152]{2,1,0:T(8,128)(2,1)}, u32[]{:S(2)}, u32[]{:S(2)}) async-start(bf16[32,32,1152]{2,1,0:T(8,128)(2,1)} %bitcast.52), calls=%async_computation.5 | async-start | bytes 4718592 | tf_op jit(solution)/shard_map/all_to_all | solution.py:410
  198.7 1.3 collective-permute-start.10
  199.9 1.6 collective-permute-start.9
  201.6 0.4 collective-permute-start.11
  202.0 25.4 %collective-permute-done.10.c_ref = bf16[32,16,1152]{2,1,0:T(8,128)(2,1)S(1)} collective-permute-done((bf16[32,16,1152]{2,1,0:T(8,128)(2,1)S(1)}, bf16[32,16,1152]{2,1,0:T(8,128)(2,1)S(1)}, u32[]{:S(2)}, u32[]{:S(2)}) %collective-permute-start.10) | collective-permute-done | bytes 1179680 | tf_op jit(solution)/shard_map/ppermute | solution.py:399
  227.4 25.1 %collective-permute-done.9.b_ref = bf16[32,16,1152]{2,1,0:T(8,128)(2,1)S(1)} collective-permute-done((bf16[32,16,1152]{2,1,0:T(8,128)(2,1)}, bf16[32,16,1152]{2,1,0:T(8,128)(2,1)S(1)}, u32[]{:S(2)}, u32[]{:S(2)}) %collective-permute-start.9) | collective-permute-done | bytes 1179680 | tf_op jit(solution)/shard_map/ppermute | solution.py:399
  252.5 0.9 collective-permute-done.11.d_ref
  253.4 2.0 sum_halves.1
  255.4 0.0 all-to-all-done.5
  255.4 7.5 %all-to-all-start.3 = ((bf16[32,32,1152]{2,1,0:T(8,128)(2,1)}), bf16[32,32,1152]{2,1,0:T(8,128)(2,1)S(1)}, u32[]{:S(2)}, u32[]{:S(2)}) async-start(bf16[32,32,1152]{2,1,0:T(8,128)(2,1)} %bitcast.21), calls=%async_computation.3 | async-start | bytes 4718592 | tf_op jit(solution)/shard_map/all_to_all | solution.py:410
  262.9 3.1 %early_combine.2 = bf16[2,128,1024]{2,1,0:T(8,128)(2,1)} custom-call(s32[1]{0:T(128)} %bitcast.pair_ref, s32[2,6,128]{2,1,0:T(8,128)} %get-tuple-element.28.ids_ref, f32[2,6,128]{2,1,0:T(8,128)} %get-tuple-element.27.gates_ref, bf16[32,2,16,1152]{3,2,1,0:T(8,128)(2,1)} %bitcast.24.rows_ref), custom_call_target="tpu_custom_call" | custom-call | flops 301989888 | bytes 2359296 | tf_op jit(solution)/shard_map/early_combine/pallas_call | solution.py:344
  266.0 1.8 slice_bitcast_fusion.3
  267.8 1.2 collective-permute-start.13
  269.0 3.1 %early_combine.3 = bf16[2,128,1024]{2,1,0:T(8,128)(2,1)} custom-call(s32[1]{0:T(128)} %bitcast.pair_ref, s32[2,6,128]{2,1,0:T(8,128)} %get-tuple-element.26.ids_ref, f32[2,6,128]{2,1,0:T(8,128)} %get-tuple-element.25.gates_ref, bf16[32,2,16,1152]{3,2,1,0:T(8,128)(2,1)} %bitcast.27.rows_ref), custom_call_target="tpu_custom_call" | custom-call | flops 301989888 | bytes 2359296 | tf_op jit(solution)/shard_map/early_combine/pallas_call | solution.py:344
  272.1 1.1 slice_bitcast_fusion.2
  273.2 1.3 collective-permute-start.14
  274.5 0.5 collective-permute-start.12
  275.0 2.0 collective-permute-done.13.refs_2_
  277.0 6.0 %collective-permute-done.14.refs_3_ = bf16[128,1024]{1,0:T(8,128)(2,1)S(1)} collective-permute-done((bf16[128,1024]{1,0:T(8,128)(2,1)S(1)}, bf16[128,1024]{1,0:T(8,128)(2,1)S(1)}, u32[]{:S(2)}, u32[]{:S(2)}) %collective-permute-start.14) | collective-permute-done | bytes 262176 | tf_op jit(solution)/shard_map/ppermute | solution.py:399
  283.0 0.0 collective-permute-done.12.refs_1_
  283.0 8.1 %all-to-all-done.3 = bf16[32,32,1152]{2,1,0:T(8,128)(2,1)S(1)} async-done(((bf16[32,32,1152]{2,1,0:T(8,128)(2,1)}), bf16[32,32,1152]{2,1,0:T(8,128)(2,1)S(1)}, u32[]{:S(2)}, u32[]{:S(2)}) %all-to-all-start.3) | async-done | bytes 2359328 | tf_op jit(solution)/shard_map/all_to_all | solution.py:410
  291.1 1.7 final_combine.1
  (18 shorter events, 0.1 us)
Async XLA Ops:
  3.4 8.4 %copy-start.2 = (bf16[128,2048]{1,0:T(8,128)(2,1)S(1)}, bf16[128,2048]{1,0:T(8,128)(2,1)}, u32[]{:S(2)}) copy-start(bf16[128,2048]{1,0:T(8,128)(2,1)} %tokens_ref.1) | copy-start | bytes 1572868
  3.4 11.5 %copy-start.1 = (s32[128,6]{0,1:T(8,128)S(1)}, s32[128,6]{0,1:T(8,128)}, u32[]{:S(2)}) copy-start(s32[128,6]{0,1:T(8,128)} %param.7) | copy-start | bytes 9220
  3.4 11.5 %copy-start.4 = (bf16[128,6]{0,1:T(8,128)(2,1)S(1)}, bf16[128,6]{0,1:T(8,128)(2,1)}, u32[]{:S(2)}) copy-start(bf16[128,6]{0,1:T(8,128)(2,1)} %param.8) | copy-start | bytes 4612
  3.4 36.6 %all-to-all-start = ((bf16[32,32,1152]{2,1,0:T(8,128)(2,1)}), bf16[32,32,1152]{2,1,0:T(8,128)(2,1)S(1)}, u32[]{:S(2)}, u32[]{:S(2)}) async-start(bf16[32,32,1152]{2,1,0:T(8,128)(2,1)} %bitcast.50), calls=%async_computation | async-start | bytes 4718592 | tf_op jit(solution)/shard_map/all_to_all | solution.py:410
  11.9 9.8 %collective-permute-start.2 = (bf16[128,1024]{1,0:T(8,128)(2,1)S(1)}, bf16[128,1024]{1,0:T(8,128)(2,1)S(1)}, u32[]{:S(2)}, u32[]{:S(2)}) collective-permute-start(bf16[128,1024]{1,0:T(8,128)(2,1)S(1)} %get-tuple-element.24), channel_id=1, source_target_pairs={{0,2},{1,3},{2,0},{3,1},{4,6},{5,7},{6,4},{7,5},{8,10},{9,11},{10,... | collective-permute-start | bytes 786440 | tf_op jit(solution)/shard_map/ppermute | solution.py:399
  14.9 6.1 %collective-permute-start.1 = (bf16[12,128]{1,0:T(8,128)(2,1)S(1)}, bf16[12,128]{1,0:T(8,128)(2,1)S(1)}, u32[]{:S(2)}, u32[]{:S(2)}) collective-permute-start(bf16[12,128]{1,0:T(8,128)(2,1)S(1)} %get-tuple-element.29), channel_id=1, source_target_pairs={{0,2},{1,3},{2,0},{3,1},{4,6},{5,7},{6,4},{7,5},{8,10},{9,11},{10,... | collective-permute-start | bytes 9224 | tf_op jit(solution)/shard_map/ppermute | solution.py:399
  40.0 35.2 %all-to-all-start.1 = ((bf16[32,32,1152]{2,1,0:T(8,128)(2,1)}), bf16[32,32,1152]{2,1,0:T(8,128)(2,1)}, u32[]{:S(2)}, u32[]{:S(2)}) async-start(bf16[32,32,1152]{2,1,0:T(8,128)(2,1)} %bitcast.49), calls=%async_computation.1 | async-start | bytes 4718592 | tf_op jit(solution)/shard_map/all_to_all | solution.py:410
  46.9 10.6 %collective-permute-start.7 = (bf16[128,1024]{1,0:T(8,128)(2,1)S(1)}, bf16[128,1024]{1,0:T(8,128)(2,1)S(1)}, u32[]{:S(2)}, u32[]{:S(2)}) collective-permute-start(bf16[128,1024]{1,0:T(8,128)(2,1)S(1)} %get-tuple-element.24), channel_id=1, source_target_pairs={{0,1},{1,0},{2,3},{3,2},{4,5},{5,4},{6,7},{7,6},{8,9},{9,8},{10,11... | collective-permute-start | bytes 786440 | tf_op jit(solution)/shard_map/ppermute | solution.py:399
  48.3 9.2 %collective-permute-start.8 = (bf16[128,1024]{1,0:T(8,128)(2,1)S(1)}, bf16[128,1024]{1,0:T(8,128)(2,1)S(1)}, u32[]{:S(2)}, u32[]{:S(2)}) collective-permute-start(bf16[128,1024]{1,0:T(8,128)(2,1)S(1)} %get-tuple-element.24), channel_id=1, source_target_pairs={{0,3},{1,2},{2,1},{3,0},{4,7},{5,6},{6,5},{7,4},{8,11},{9,10},{10,... | collective-permute-start | bytes 786440 | tf_op jit(solution)/shard_map/ppermute | solution.py:399
  50.2 4.5 %collective-permute-start.5 = (bf16[12,128]{1,0:T(8,128)(2,1)S(1)}, bf16[12,128]{1,0:T(8,128)(2,1)S(1)}, u32[]{:S(2)}, u32[]{:S(2)}) collective-permute-start(bf16[12,128]{1,0:T(8,128)(2,1)S(1)} %get-tuple-element.29), channel_id=1, source_target_pairs={{0,1},{1,0},{2,3},{3,2},{4,5},{5,4},{6,7},{7,6},{8,9},{9,8},{10,11... | collective-permute-start | bytes 9224 | tf_op jit(solution)/shard_map/ppermute | solution.py:399
  50.6 6.3 %collective-permute-start.6 = (bf16[12,128]{1,0:T(8,128)(2,1)S(1)}, bf16[12,128]{1,0:T(8,128)(2,1)S(1)}, u32[]{:S(2)}, u32[]{:S(2)}) collective-permute-start(bf16[12,128]{1,0:T(8,128)(2,1)S(1)} %get-tuple-element.29), channel_id=1, source_target_pairs={{0,3},{1,2},{2,1},{3,0},{4,7},{5,6},{6,5},{7,4},{8,11},{9,10},{10,... | collective-permute-start | bytes 9224 | tf_op jit(solution)/shard_map/ppermute | solution.py:399
  75.2 56.7 %all-to-all-start.2 = ((bf16[32,32,1152]{2,1,0:T(8,128)(2,1)}), bf16[32,32,1152]{2,1,0:T(8,128)(2,1)}, u32[]{:S(2)}, u32[]{:S(2)}) async-start(bf16[32,32,1152]{2,1,0:T(8,128)(2,1)} %bitcast.51), calls=%async_computation.2 | async-start | bytes 4718592 | tf_op jit(solution)/shard_map/all_to_all | solution.py:410
  83.4 28.6 %collective-permute-start = (bf16[32,16,1152]{2,1,0:T(8,128)(2,1)S(1)}, bf16[32,16,1152]{2,1,0:T(8,128)(2,1)S(1)}, u32[]{:S(2)}, u32[]{:S(2)}) collective-permute-start(bf16[32,16,1152]{2,1,0:T(8,128)(2,1)S(1)} %get-tuple-element.17), channel_id=1, source_target_pairs={{0,2},{1,3},{2,0},{3,1},{4,6},{5,7},{6,4},{7,5},{8,10},{9,11},{10,... | collective-permute-start | bytes 3538952 | tf_op jit(solution)/shard_map/ppermute | solution.py:399
  112.0 1.0 copy-start.9
  131.9 11.3 %copy-start.3 = (bf16[32,16,1152]{2,1,0:T(8,128)(2,1)S(1)}, bf16[32,16,1152]{2,1,0:T(8,128)(2,1)}, u32[]{:S(2)}) copy-start(bf16[32,16,1152]{2,1,0:T(8,128)(2,1)} %get-tuple-element.18.refs_0_) | copy-start | bytes 3538948
  131.9 57.9 %all-to-all-start.4 = ((bf16[32,32,1152]{2,1,0:T(8,128)(2,1)}), bf16[32,32,1152]{2,1,0:T(8,128)(2,1)}, u32[]{:S(2)}, u32[]{:S(2)}) async-start(bf16[32,32,1152]{2,1,0:T(8,128)(2,1)} %bitcast.53), calls=%async_computation.4 | async-start | bytes 4718592 | tf_op jit(solution)/shard_map/all_to_all | solution.py:410
  140.3 28.5 %collective-permute-start.4 = (bf16[32,16,1152]{2,1,0:T(8,128)(2,1)S(1)}, bf16[32,16,1152]{2,1,0:T(8,128)(2,1)S(1)}, u32[]{:S(2)}, u32[]{:S(2)}) collective-permute-start(bf16[32,16,1152]{2,1,0:T(8,128)(2,1)S(1)} %get-tuple-element.17), channel_id=1, source_target_pairs={{0,3},{1,2},{2,1},{3,0},{4,7},{5,6},{6,5},{7,4},{8,11},{9,10},{10,... | collective-permute-start | bytes 3538952 | tf_op jit(solution)/shard_map/ppermute | solution.py:399
  143.1 26.9 %collective-permute-start.3 = (bf16[32,16,1152]{2,1,0:T(8,128)(2,1)S(1)}, bf16[32,16,1152]{2,1,0:T(8,128)(2,1)S(1)}, u32[]{:S(2)}, u32[]{:S(2)}) collective-permute-start(bf16[32,16,1152]{2,1,0:T(8,128)(2,1)S(1)} %copy-done.3), channel_id=1, source_target_pairs={{0,1},{1,0},{2,3},{3,2},{4,5},{5,4},{6,7},{7,6},{8,9},{9,8},{10,11... | collective-permute-start | bytes 3538952 | tf_op jit(solution)/shard_map/ppermute | solution.py:399
  168.9 1.1 copy-start.7
  170.0 1.0 copy-start.8
  189.8 8.9 %copy-start.5 = (bf16[32,16,1152]{2,1,0:T(8,128)(2,1)S(1)}, bf16[32,16,1152]{2,1,0:T(8,128)(2,1)}, u32[]{:S(2)}) copy-start(bf16[32,16,1152]{2,1,0:T(8,128)(2,1)} %get-tuple-element.13) | copy-start | bytes 3538948
  189.8 11.8 %copy-start.6 = (bf16[32,16,1152]{2,1,0:T(8,128)(2,1)S(1)}, bf16[32,16,1152]{2,1,0:T(8,128)(2,1)}, u32[]{:S(2)}) copy-start(bf16[32,16,1152]{2,1,0:T(8,128)(2,1)} %get-tuple-element.14) | copy-start | bytes 3538948
  189.8 63.6 %copy-start = (bf16[32,16,1152]{2,1,0:T(8,128)(2,1)S(1)}, bf16[32,16,1152]{2,1,0:T(8,128)(2,1)}, u32[]{:S(2)}) copy-start(bf16[32,16,1152]{2,1,0:T(8,128)(2,1)} %get-tuple-element.11.a_ref) | copy-start | bytes 3538948
  189.8 65.6 %all-to-all-start.5 = ((bf16[32,32,1152]{2,1,0:T(8,128)(2,1)}), bf16[32,32,1152]{2,1,0:T(8,128)(2,1)}, u32[]{:S(2)}, u32[]{:S(2)}) async-start(bf16[32,32,1152]{2,1,0:T(8,128)(2,1)} %bitcast.52), calls=%async_computation.5 | async-start | bytes 4718592 | tf_op jit(solution)/shard_map/all_to_all | solution.py:410
  198.7 28.8 %collective-permute-start.10 = (bf16[32,16,1152]{2,1,0:T(8,128)(2,1)S(1)}, bf16[32,16,1152]{2,1,0:T(8,128)(2,1)S(1)}, u32[]{:S(2)}, u32[]{:S(2)}) collective-permute-start(bf16[32,16,1152]{2,1,0:T(8,128)(2,1)S(1)} %copy-done.5), channel_id=1, source_target_pairs={{0,2},{1,3},{2,0},{3,1},{4,6},{5,7},{6,4},{7,5},{8,10},{9,11},{10,... | collective-permute-start | bytes 3538952 | tf_op jit(solution)/shard_map/ppermute | solution.py:399
  199.9 52.6 %collective-permute-start.9 = (bf16[32,16,1152]{2,1,0:T(8,128)(2,1)}, bf16[32,16,1152]{2,1,0:T(8,128)(2,1)S(1)}, u32[]{:S(2)}, u32[]{:S(2)}) collective-permute-start(bf16[32,16,1152]{2,1,0:T(8,128)(2,1)} %get-tuple-element.12), channel_id=1, source_target_pairs={{0,1},{1,0},{2,3},{3,2},{4,5},{5,4},{6,7},{7,6},{8,9},{9,8},{10,11... | collective-permute-start | bytes 3538952 | tf_op jit(solution)/shard_map/ppermute | solution.py:399
  201.6 51.9 %collective-permute-start.11 = (bf16[32,16,1152]{2,1,0:T(8,128)(2,1)S(1)}, bf16[32,16,1152]{2,1,0:T(8,128)(2,1)S(1)}, u32[]{:S(2)}, u32[]{:S(2)}) collective-permute-start(bf16[32,16,1152]{2,1,0:T(8,128)(2,1)S(1)} %copy-done.6), channel_id=1, source_target_pairs={{0,3},{1,2},{2,1},{3,0},{4,7},{5,6},{6,5},{7,4},{8,11},{9,10},{10,... | collective-permute-start | bytes 3538952 | tf_op jit(solution)/shard_map/ppermute | solution.py:399
  255.4 35.7 %all-to-all-start.3 = ((bf16[32,32,1152]{2,1,0:T(8,128)(2,1)}), bf16[32,32,1152]{2,1,0:T(8,128)(2,1)S(1)}, u32[]{:S(2)}, u32[]{:S(2)}) async-start(bf16[32,32,1152]{2,1,0:T(8,128)(2,1)} %bitcast.21), calls=%async_computation.3 | async-start | bytes 4718592 | tf_op jit(solution)/shard_map/all_to_all | solution.py:410
  267.8 9.2 %collective-permute-start.13 = (bf16[128,1024]{1,0:T(8,128)(2,1)}, bf16[128,1024]{1,0:T(8,128)(2,1)S(1)}, u32[]{:S(2)}, u32[]{:S(2)}) collective-permute-start(bf16[128,1024]{1,0:T(8,128)(2,1)} %get-tuple-element.21), channel_id=1, source_target_pairs={{0,2},{1,3},{2,0},{3,1},{4,6},{5,7},{6,4},{7,5},{8,10},{9,11},{10,... | collective-permute-start | bytes 786440 | tf_op jit(solution)/shard_map/ppermute | solution.py:399
  273.2 9.8 %collective-permute-start.14 = (bf16[128,1024]{1,0:T(8,128)(2,1)S(1)}, bf16[128,1024]{1,0:T(8,128)(2,1)S(1)}, u32[]{:S(2)}, u32[]{:S(2)}) collective-permute-start(bf16[128,1024]{1,0:T(8,128)(2,1)S(1)} %get-tuple-element.19), channel_id=1, source_target_pairs={{0,3},{1,2},{2,1},{3,0},{4,7},{5,6},{6,5},{7,4},{8,11},{9,10},{10,... | collective-permute-start | bytes 786440 | tf_op jit(solution)/shard_map/ppermute | solution.py:399
  274.5 8.5 %collective-permute-start.12 = (bf16[128,1024]{1,0:T(8,128)(2,1)S(1)}, bf16[128,1024]{1,0:T(8,128)(2,1)S(1)}, u32[]{:S(2)}, u32[]{:S(2)}) collective-permute-start(bf16[128,1024]{1,0:T(8,128)(2,1)S(1)} %get-tuple-element.20), channel_id=1, source_target_pairs={{0,1},{1,0},{2,3},{3,2},{4,5},{5,4},{6,7},{7,6},{8,9},{9,8},{10,11... | collective-permute-start | bytes 786440 | tf_op jit(solution)/shard_map/ppermute | solution.py:399
